TPU v7x, 256 devices: a whole 4x4x8 slice. The times are simulated.
256 devices in a mesh: dp: 64 (over x, z, core), tensor: 4 (over y).
Axes of the slice: x: 4, y: 4, z: 8, core: 2. Of those that a mesh axis runs over, the one named last changes fastest.
Arguments:
- activations: bfloat16 [768, 8192], P('dp', 'tensor'), may hold values from -400 to 400, as said below
- weight: bfloat16 [8192, 28672], P('dp', 'tensor'), may hold values from -0.0625 to 0.0625
Outputs:
- channel_mean: float32 [8192], P('dp')
- column_errors: float32 [4, 28672], P(None, ('tensor', 'dp'))
- errors: float32 [4], replicated
Inputs may be any that keep to these rules, and one draw needn't show every extreme that they name: activations and weight are finite real values within the ranges stated above.
All inputs are finite; a program needn't handle non-finite values.
Results may differ from a plain program's by a relative error of at most 0.0012.
The roundings to bfloat16 on the way count: a program that leaves them out, or rounds other values in their place, can miss the bound.
Values may be sent and summed in bfloat16 or wider, within the bound.
No kernel may reach another device: no remote copies, remote signals or barrier semaphores. Data moves between devices by JAX's collectives and lax.ppermute only.
A program may use at most 128 MiB of HBM per device.

v0:
```python
import functools
import math

import jax
import jax.numpy as jnp
from jax import lax
from jax.sharding import Mesh
from jax.sharding import PartitionSpec as P

D = 8192
F = 28672
GROUP = 128
GRID = 4
DP = ("dp_0", "dp_1", "dp_2")
DP_TENSOR = ("dp_0", "dp_1", "dp_2", "tensor")
TENSOR_DP = ("tensor", "dp_0", "dp_1", "dp_2")


def laid_out(parts, dim):
    parts = jnp.moveaxis(parts, 0, dim)
    dims = parts.shape
    return parts.reshape(*dims[:dim], dims[dim] * dims[dim + 1], *dims[dim + 2 :])


def from_everyone(shard, axis):
    devices = lax.axis_size(axis)
    return lax.all_to_all(
        jnp.broadcast_to(shard[None], (devices, *shard.shape)), axis, 0, 0, tiled=True
    )


def gather_directly(shard, axis, dim):
    return laid_out(from_everyone(shard, axis), dim)


def by_axis(shard, axes):
    return functools.reduce(lax.psum, axes, shard)


def soft_round(values):
    return values - jnp.sin(2.0 * math.pi * values) / (2.0 * math.pi)


def scale_table(channel_mean):
    ratios = jnp.arange(GRID, dtype=jnp.float32) / GRID
    raw = jnp.exp(ratios[:, None] * jnp.log(channel_mean)[None, :])
    top = jnp.max(raw, axis=1, keepdims=True)
    bottom = jnp.min(raw, axis=1, keepdims=True)
    return raw / jnp.sqrt(top * bottom)


def on_device(activations, weight):
    widened = gather_directly(activations, "tensor", 1)
    gathered = lax.all_gather(widened, DP, axis=0, tiled=True)
    columns = lax.all_to_all(weight, DP, split_axis=1, concat_axis=0, tiled=True)
    width = columns.shape[1]
    token_count = gathered.shape[0]
    channel_mean = jnp.sum(jnp.abs(gathered), axis=0, dtype=jnp.float32) / token_count + 1e-06
    scales = scale_table(channel_mean)
    base_out = jnp.dot(gathered, columns, preferred_element_type=jnp.float32)
    weight_float = columns.astype(jnp.float32)

    def local_error(factor):
        scaled = weight_float * factor[:, None]
        grouped = scaled.reshape(D // GROUP, GROUP, width)
        quant_step = (jnp.max(jnp.abs(grouped), axis=1, keepdims=True) + 1e-06) / 7.0
        levels = soft_round(grouped / quant_step)
        dequant = ((levels * quant_step).reshape(D, width) / factor[:, None]).astype(jnp.bfloat16)
        quant_out = jnp.dot(gathered, dequant, preferred_element_type=jnp.float32)
        residue = quant_out - base_out
        return jnp.sum(residue * residue, axis=0)

    column_sums = lax.map(local_error, scales)
    totals = by_axis(jnp.sum(column_sums, axis=1), DP_TENSOR)
    errors = totals / (token_count * F)
    column_errors = column_sums / token_count
    rows = D // lax.axis_size(DP)
    own_mean = lax.dynamic_slice_in_dim(channel_mean, lax.axis_index(DP) * rows, rows)
    return (own_mean, column_errors, errors)


def solution(mesh):
    torus = Mesh(
        mesh.devices.reshape(4, 8, 2, mesh.shape["tensor"]), ("dp_0", "dp_1", "dp_2", "tensor")
    )
    placed = (P(DP, "tensor"), P(DP, "tensor"))
    return jax.shard_map(
        on_device,
        mesh=torus,
        in_specs=placed,
        out_specs=(P(DP), P(None, TENSOR_DP), P()),
        check_vma=False,
    )
```

profile of v0, /device:TPU:2, one launch (start us, length us, event | category | flops | bytes accessed | tf_op | source)
XLA Modules:
  0.0 334.3 jit_solution(7435003003157472509)
XLA Ops:
  7.2 0.0 all-gather.3.cloned.1.call-start
  7.2 0.9 broadcast_in_dim.7
  8.1 10.9 %all_to_all.24 = bf16[4,12,2048]{2,1,0:T(8,128)(2,1)S(1)} all-to-all(bf16[4,12,2048]{2,1,0:T(8,128)(2,1)S(1)} %broadcast_in_dim.7), channel_id=1, replica_groups=mesh['dp_0'=4,'dp_1'=8,'dp_2'=2,'tensor'=4] {'tensor'}, dimensions={0} | all-to-all | bytes 393216 | tf_op jit(solution)/shard_map/all_to_all | solution.py:27
  19.0 0.2 copy.13
  19.2 0.8 reshape.54
  20.0 0.0 all-gather.3.cloned.1.call-update
  20.0 3.9 %copy.14 = bf16[128,7168]{0,1:T(8,128)(2,1)} copy(bf16[128,7168]{1,0:T(8,128)(2,1)} %param.5) | data formatting | bytes 3670016 | tf_op args[1]
  23.9 12.0 %all-to-all-start.1 = ((bf16[128,64,112]{0,2,1:T(8,128)(2,1)}), bf16[128,64,112]{0,2,1:T(8,128)(2,1)S(1)}, u32[]{:S(2)}, u32[]{:S(2)}) async-start(bf16[128,64,112]{0,2,1:T(8,128)(2,1)} %bitcast.7), calls=%async_computation.1 | async-start | bytes 3670016 | tf_op jit(solution)/shard_map/all_to_all | solution.py:55
  36.0 52.4 %all-to-all-done.1 = bf16[128,64,112]{0,2,1:T(8,128)(2,1)S(1)} async-done(((bf16[128,64,112]{0,2,1:T(8,128)(2,1)}), bf16[128,64,112]{0,2,1:T(8,128)(2,1)S(1)}, u32[]{:S(2)}, u32[]{:S(2)}) %all-to-all-start.1) | async-done | bytes 1835040 | tf_op jit(solution)/shard_map/all_to_all | solution.py:55
  88.4 2.1 bitcast_convert_fusion
  90.5 5.4 %copy.16 = f32[8192,112]{1,0:T(8,128)} copy(f32[8192,112]{0,1:T(8,128)} %bitcast_convert_fusion) | data formatting | bytes 7340032 | tf_op jit(solution)/shard_map/while | solution.py:73
  96.0 36.0 %all-gather.3.cloned.1.call-done = bf16[64,12,8192]{2,1,0:T(8,128)(2,1)} async-done(((bf16[1,12,8192]{2,1,0:T(8,128)(2,1)}), bf16[64,12,8192]{2,1,0:T(8,128)(2,1)}) %all-gather.3.cloned.1.call-update) | async-done | bytes 12582928 | tf_op jit(solution)/shard_map/all_gather | solution.py:54
  131.9 16.8 %reshape.55 = bf16[768,8192]{1,0:T(8,128)(2,1)} reshape(bf16[64,12,8192]{2,1,0:T(8,128)(2,1)} %all-gather.3.cloned.1.call-done) | data formatting | bytes 25165824
  148.8 7.6 %convert_reduce_fusion = f32[8192]{0:T(1024)S(1)} fusion(bf16[768,8192]{1,0:T(8,128)(2,1)} %reshape.55), kind=kLoop, calls=%fused_computation.11 | loop fusion | flops 18866176 | bytes 12615680 | tf_op jit(solution)/shard_map/reduce_sum | solution.py:58
  156.5 0.3 fusion.9
  156.7 0.1 fusion.8
  156.9 8.7 %fusion.5 = f32[768,112]{0,1:T(8,128)S(1)} fusion(bf16[768,8192]{1,0:T(8,128)(2,1)} %reshape.55, bf16[128,64,112]{0,2,1:T(8,128)(2,1)S(1)} %all-to-all-done.1), kind=kOutput, calls=%fused_computation.12 | convolution fusion | flops 1409286144 | bytes 14761984 | tf_op jit(solution)/shard_map/dot_general | solution.py:60
  165.6 122.5 %while.10 = (s32[]{:T(128)}, f32[4,112]{1,0:T(4,128)S(1)}, f32[4,8192]{1,0:T(4,128)S(1)}, f32[8192,112]{1,0:T(8,128)}, bf16[768,8192]{1,0:T(8,128)(2,1)}, /*index=5*/f32[768,112]{0,1:T(8,128)S(1)}, s32[]{:T(128)}, s32[]{:T(128)}) while((s32[]{:T(128)}, f32[4,112]{1,0:T(4,128)S(1)}, f32[4,8192]{1,0:T(4,128)S(1)}, f32[8192,112]{1,0:T(8,128)}, ...), condition=%wide.region_6.7_spmd, body=%wide.region_3.6_spmd.sunk | while | flops 1419643776 | bytes 38864320 | solution.py:73
  165.8 0.0 copy-start
  165.9 3.2 abs_reduce_fusion.2
  169.1 0.2 copy-done
  169.3 18.3 %fusion.24 = bf16[8192,112]{1,0:T(8,128)(2,1)S(1)} fusion(f32[8192,112]{1,0:T(8,128)S(1)} %copy-done, f32[64,112]{1,0:T(8,128)S(1)} %add_multiply_fusion.2, f32[8192]{0:T(1024)S(1)} %bitcast.55), kind=kLoop, calls=%fused_computation.3.clone.1 | loop fusion | flops 7340032 | bytes 5566464 | tf_op jit(solution)/shard_map/while/body/eval_jaxpr/convert_element_type | solution.py:68
  187.5 8.8 %fusion.25 = f32[112]{0:T(128)S(1)} fusion(f32[768,112]{0,1:T(8,128)S(1)} %get-tuple-element.130, bf16[8192,112]{1,0:T(8,128)(2,1)S(1)} %fusion.24, bf16[768,8192]{1,0:T(8,128)(2,1)} %get-tuple-element.129), kind=kOutput, calls=%fused_computation.8.clone.1 | convolution fusion | flops 1409544064 | bytes 14762432 | tf_op jit(solution)/shard_map/while/body/eval_jaxpr/dot_general | solution.py:69
  196.4 0.0 copy-start
  196.5 3.2 abs_reduce_fusion.2
  199.7 0.2 copy-done
  199.8 18.3 %fusion.24 = bf16[8192,112]{1,0:T(8,128)(2,1)S(1)} fusion(f32[8192,112]{1,0:T(8,128)S(1)} %copy-done, f32[64,112]{1,0:T(8,128)S(1)} %add_multiply_fusion.2, f32[8192]{0:T(1024)S(1)} %bitcast.55), kind=kLoop, calls=%fused_computation.3.clone.1 | loop fusion | flops 7340032 | bytes 5566464 | tf_op jit(solution)/shard_map/while/body/eval_jaxpr/convert_element_type | solution.py:68
  218.1 8.8 %fusion.25 = f32[112]{0:T(128)S(1)} fusion(f32[768,112]{0,1:T(8,128)S(1)} %get-tuple-element.130, bf16[8192,112]{1,0:T(8,128)(2,1)S(1)} %fusion.24, bf16[768,8192]{1,0:T(8,128)(2,1)} %get-tuple-element.129), kind=kOutput, calls=%fused_computation.8.clone.1 | convolution fusion | flops 1409544064 | bytes 14762432 | tf_op jit(solution)/shard_map/while/body/eval_jaxpr/dot_general | solution.py:69
  227.0 0.0 copy-start
  227.0 3.2 abs_reduce_fusion.2
  230.2 0.2 copy-done
  230.4 18.3 %fusion.24 = bf16[8192,112]{1,0:T(8,128)(2,1)S(1)} fusion(f32[8192,112]{1,0:T(8,128)S(1)} %copy-done, f32[64,112]{1,0:T(8,128)S(1)} %add_multiply_fusion.2, f32[8192]{0:T(1024)S(1)} %bitcast.55), kind=kLoop, calls=%fused_computation.3.clone.1 | loop fusion | flops 7340032 | bytes 5566464 | tf_op jit(solution)/shard_map/while/body/eval_jaxpr/convert_element_type | solution.py:68
  248.7 8.8 %fusion.25 = f32[112]{0:T(128)S(1)} fusion(f32[768,112]{0,1:T(8,128)S(1)} %get-tuple-element.130, bf16[8192,112]{1,0:T(8,128)(2,1)S(1)} %fusion.24, bf16[768,8192]{1,0:T(8,128)(2,1)} %get-tuple-element.129), kind=kOutput, calls=%fused_computation.8.clone.1 | convolution fusion | flops 1409544064 | bytes 14762432 | tf_op jit(solution)/shard_map/while/body/eval_jaxpr/dot_general | solution.py:69
  257.6 0.0 copy-start
  257.6 3.2 abs_reduce_fusion.2
  260.8 0.2 copy-done
  261.0 18.3 %fusion.24 = bf16[8192,112]{1,0:T(8,128)(2,1)S(1)} fusion(f32[8192,112]{1,0:T(8,128)S(1)} %copy-done, f32[64,112]{1,0:T(8,128)S(1)} %add_multiply_fusion.2, f32[8192]{0:T(1024)S(1)} %bitcast.55), kind=kLoop, calls=%fused_computation.3.clone.1 | loop fusion | flops 7340032 | bytes 5566464 | tf_op jit(solution)/shard_map/while/body/eval_jaxpr/convert_element_type | solution.py:68
  279.3 8.8 %fusion.25 = f32[112]{0:T(128)S(1)} fusion(f32[768,112]{0,1:T(8,128)S(1)} %get-tuple-element.130, bf16[8192,112]{1,0:T(8,128)(2,1)S(1)} %fusion.24, bf16[768,8192]{1,0:T(8,128)(2,1)} %get-tuple-element.129), kind=kOutput, calls=%fused_computation.8.clone.1 | convolution fusion | flops 1409544064 | bytes 14762432 | tf_op jit(solution)/shard_map/while/body/eval_jaxpr/dot_general | solution.py:69
  288.1 0.7 fusion.12
  288.8 9.1 %psum.28 = f32[4]{0:T(128)S(1)} all-reduce(f32[4]{0:T(128)S(1)} %get-tuple-element.70), channel_id=1, replica_groups=mesh['dp_0'=4,'dp_1'=8,'dp_2'=2,'tensor'=4] {'dp_0'}, use_global_device_ids=true, to_apply=%region_8.9 | all-reduce | flops 4 | bytes 32 | tf_op jit(solution)/shard_map/psum | solution.py:37
  298.0 15.8 %psum.29 = f32[4]{0:T(128)S(1)} all-reduce(f32[4]{0:T(128)S(1)} %psum.28), channel_id=1, replica_groups=mesh['dp_0'=4,'dp_1'=8,'dp_2'=2,'tensor'=4] {'dp_1'}, use_global_device_ids=true, to_apply=%region_9.10 | all-reduce | flops 4 | bytes 32 | tf_op jit(solution)/shard_map/psum | solution.py:37
  313.7 2.5 psum.30
  316.2 10.2 %psum.31 = f32[4]{0:T(128)S(1)} all-reduce(f32[4]{0:T(128)S(1)} %psum.30), channel_id=1, replica_groups=mesh['dp_0'=4,'dp_1'=8,'dp_2'=2,'tensor'=4] {'tensor'}, use_global_device_ids=true, to_apply=%region_11.12 | all-reduce | flops 4 | bytes 32 | tf_op jit(solution)/shard_map/psum | solution.py:37
  326.3 0.5 broadcast_multiply_fusion.1
  326.9 0.6 dynamic_slice.7
  (16 shorter events, 0.4 us)
Async XLA Ops:
  7.2 124.8 %all-gather.3.cloned.1.call-start = ((), (), s32[]{:S(2)}) async-start(), calls=%async_computation.2 | async-start | bytes 17039360 | tf_op jit(solution)/shard_map/all_gather | solution.py:54
  23.9 64.5 %all-to-all-start.1 = ((bf16[128,64,112]{0,2,1:T(8,128)(2,1)}), bf16[128,64,112]{0,2,1:T(8,128)(2,1)S(1)}, u32[]{:S(2)}, u32[]{:S(2)}) async-start(bf16[128,64,112]{0,2,1:T(8,128)(2,1)} %bitcast.7), calls=%async_computation.1 | async-start | bytes 3670016 | tf_op jit(solution)/shard_map/all_to_all | solution.py:55
  165.8 3.5 %copy-start = (f32[8192,112]{1,0:T(8,128)S(1)}, f32[8192,112]{1,0:T(8,128)}, u32[]{:S(2)}) copy-start(f32[8192,112]{1,0:T(8,128)} %get-tuple-element.128) | copy-start | bytes 11010052 | tf_op jit(solution)/shard_map/while
  196.4 3.5 %copy-start = (f32[8192,112]{1,0:T(8,128)S(1)}, f32[8192,112]{1,0:T(8,128)}, u32[]{:S(2)}) copy-start(f32[8192,112]{1,0:T(8,128)} %get-tuple-element.128) | copy-start | bytes 11010052 | tf_op jit(solution)/shard_map/while
  227.0 3.5 %copy-start = (f32[8192,112]{1,0:T(8,128)S(1)}, f32[8192,112]{1,0:T(8,128)}, u32[]{:S(2)}) copy-start(f32[8192,112]{1,0:T(8,128)} %get-tuple-element.128) | copy-start | bytes 11010052 | tf_op jit(solution)/shard_map/while
  257.6 3.5 %copy-start = (f32[8192,112]{1,0:T(8,128)S(1)}, f32[8192,112]{1,0:T(8,128)}, u32[]{:S(2)}) copy-start(f32[8192,112]{1,0:T(8,128)} %get-tuple-element.128) | copy-start | bytes 11010052 | tf_op jit(solution)/shard_map/while
Sparse Core Ops, SparseCore 0:
  20.1 111.7 all-gather.2
where the time goes:
time: 335 us; the launch traced here: 334 us
  other arithmetic  97.2 us (29%)
  waiting for transfers between devices  88.4 us (26%)
  blocking collectives  48.5 us (14%)
  matrix products  44 us (13%)
  local copies, waits for them, and re-layouts  29.7 us (9%)
  between operations  14.1 us (4%)
  starting transfers between devices  12.1 us (4%)
    convert_element_type x4, other arithmetic, local_error(): ((levels * quant_step).reshape(D, width) / factor[:, None]).astype(jnp.bf...  73 us
    all_to_all x1, waiting for transfers between devices, on_device(): lax.all_to_all(weight, DP, split_axis=1, concat_axis=0, tiled=True)  52.4 us
    psum x4, blocking collectives, by_axis(): return functools.reduce(lax.psum, axes, shard)  37.5 us
    all_gather x1, waiting for transfers between devices, on_device(): gathered = lax.all_gather(widened, DP, axis=0, tiled=True)  36 us
    dot_general x4, matrix products, local_error(): quant_out = jnp.dot(gathered, dequant, preferred_element_type=jnp.float32)  35.2 us
    unnamed x3, local copies, waits for them, and re-layouts  21.6 us
    reduce_max x4, other arithmetic, local_error(): jnp.max(jnp.abs(grouped), axis=1, keepdims=True) + 1e-06  12.7 us
    all_to_all x1, starting transfers between devices, on_device(): lax.all_to_all(weight, DP, split_axis=1, concat_axis=0, tiled=True)  12 us
  transfers between devices with their start and end apart: 2, of which 2 were waited for; matrix products, arithmetic and copies ran while one was open for 3% of the time, Pallas kernels for 0%

commit v1 on v0

v1 whole, which is shorter than its diff:
```python
import jax
import jax.numpy as jnp
from jax import lax
from jax.experimental import pallas as pl
from jax.experimental.pallas import tpu as pltpu
from jax.sharding import Mesh
from jax.sharding import PartitionSpec as P

D = 8192
F = 28672
GROUP = 128
GRID = 4
TOKENS = 768
DP = ("dp_0", "dp_1", "dp_2")
ALL = ("dp_0", "dp_1", "dp_2", "tensor")
TENSOR_DP = ("tensor", "dp_0", "dp_1", "dp_2")
ZC = ("dp_1", "dp_2")
YC = ("tensor", "dp_2")
NX, NZ, NC, NY = 4, 8, 2, 4
UNITS = 7
ROWS = 16
UNIT = NX * ROWS
BLOCK = D // NX
GROUPS = BLOCK // GROUP
CHUNKS = (7,)
MIB = 1 << 20

SINE = (
    0.9999996039230294,
    -6.579691569847717,
    12.98643599053418,
    -12.188101430391939,
    6.558041838366218,
    -1.9530314806292366,
)


def vmem(limit):
    return pltpu.CompilerParams(vmem_limit_bytes=limit * MIB)


def starts():
    first, out = 0, []
    for units in CHUNKS:
        out.append(first)
        first += units
    return out


def split_columns(weight_ref, *out_refs):
    for block in range(weight_ref.shape[1] // 128):
        turned = weight_ref[:, block * 128 : (block + 1) * 128].T
        for piece in range(128 // ROWS):
            column = block * 128 + piece * ROWS
            x, rest = divmod(column, F // NY // NX)
            owner, rest = divmod(rest, UNITS * ROWS)
            unit = rest // ROWS
            for out, first, units in zip(out_refs, starts(), CHUNKS):
                if first <= unit < first + units:
                    at = ((unit - first) * NX + x) * ROWS
                    out[owner, at : at + ROWS, :] = turned[piece * ROWS : (piece + 1) * ROWS, :]


def join_tokens(parts_ref, out_ref, sums_ref):
    total = jnp.zeros((1, BLOCK), jnp.float32)
    for part in range(NZ):
        rows = parts_ref[part]
        out_ref[part * 12 : (part + 1) * 12, :] = rows
        total += jnp.sum(jnp.abs(rows.astype(jnp.float32)), axis=0, keepdims=True)
    sums_ref[...] = total


def scale_kernel(sums_ref, mean_ref, scale_ref, inverse_ref):
    mean = jnp.sum(sums_ref[...], axis=1) / TOKENS + 1e-06
    mean_ref[...] = mean
    log = jnp.log(mean)
    for k in range(GRID):
        raw = jnp.exp((k / GRID) * log)
        root = jnp.sqrt(jnp.max(raw) * jnp.min(raw))
        scale = raw / root
        scale_ref[k] = scale
        inverse_ref[k] = 1.0 / scale


def quantize(columns_ref, rows, scale_ref, inverse_ref, delta_ref):
    for group in range(GROUPS):
        packed = columns_ref[group, rows, :]
        wide = packed.astype(jnp.float32)
        for k in range(GRID):
            scaled = wide if k == 0 else wide * scale_ref[k, group : group + 1, :]
            top = jnp.max(jnp.abs(scaled), axis=1, keepdims=True) + 1e-06
            v = scaled * (7.0 / top)
            r = v - jnp.round(v)
            square = r * r
            poly = jnp.full_like(square, SINE[-1])
            for coefficient in SINE[-2::-1]:
                poly = poly * square + coefficient
            shift = (r * poly) * (top * (1.0 / 7.0))
            if k:
                shift = shift * inverse_ref[k, group : group + 1, :]
            dequant = (wide - shift).astype(jnp.bfloat16)
            delta_ref[k * UNIT : (k + 1) * UNIT, group * GROUP : (group + 1) * GROUP] = dequant - packed


def chunk_kernel(units):
    def body(columns_ref, own_ref, other_ref, scale_ref, inverse_ref, out_ref, tokens, delta_0, delta_1):
        half = TOKENS // 2
        tokens[:half, :] = own_ref[...]
        tokens[half:, :] = other_ref[...]
        deltas = (delta_0, delta_1)
        for unit in range(units):
            delta = deltas[unit % 2]
            quantize(columns_ref, pl.ds(unit * UNIT, UNIT), scale_ref, inverse_ref, delta)
            out = lax.dot_general(
                delta[...], tokens[...], (((1,), (1,)), ((), ())), preferred_element_type=jnp.float32
            ).astype(jnp.bfloat16)
            for k in range(GRID):
                for x in range(NX):
                    at = k * UNIT + x * ROWS
                    out_ref[x, unit, k] = out[at : at + ROWS, :]

    return body


def error_kernel(*refs):
    *parts, errors_ref, total_ref = refs
    rows = []
    for k in range(GRID):
        for part in parts:
            for unit in range(part.shape[1]):
                block = part[0, unit, k].astype(jnp.float32)
                for x in range(1, NX):
                    block += part[x, unit, k].astype(jnp.float32)
                block = block * block
                lanes = block[:, :128]
                for at in range(128, TOKENS, 128):
                    lanes += block[:, at : at + 128]
                rows.append(lanes)
    sums = jnp.sum(jnp.concatenate(rows, axis=0).T, axis=0, keepdims=True)
    width = UNITS * ROWS
    for k in range(GRID):
        row = sums[:, k * width : (k + 1) * width]
        errors_ref[k : k + 1, :] = row / TOKENS
        total_ref[:, k : k + 1] = jnp.sum(row, axis=1, keepdims=True)


def spread(value, axes, size):
    wide = jnp.broadcast_to(value[None], (size, *value.shape))
    return lax.all_to_all(wide, axes, 0, 0, tiled=True)


def on_device(activations, weight):
    f32, bf16 = jnp.float32, jnp.bfloat16
    turn = [(x * NY + y, y * NY + x) for x in range(NX) for y in range(NY)]
    turned = lax.ppermute(activations, ("dp_0", "tensor"), turn)
    columns = pl.pallas_call(
        split_columns,
        out_shape=[jax.ShapeDtypeStruct((NZ * NC, u * UNIT, GROUP), bf16) for u in CHUNKS],
        compiler_params=vmem(16),
        name="split_columns",
    )(weight)
    parts = spread(turned, "dp_1", NZ)
    received = [lax.all_to_all(part, ZC, 0, 0, tiled=True) for part in columns]
    joined, sums = pl.pallas_call(
        join_tokens,
        out_shape=[jax.ShapeDtypeStruct((96, BLOCK), bf16), jax.ShapeDtypeStruct((1, BLOCK), f32)],
        compiler_params=vmem(16),
        name="join_tokens",
    )(parts)
    sums = spread(sums, ("dp_0", "tensor", "dp_2"), NX * NY * NC)
    own = spread(joined, "tensor", NY).reshape(TOKENS // 2, BLOCK)
    other = lax.ppermute(own, "dp_2", [(0, 1), (1, 0)])
    mean, scale, inverse = pl.pallas_call(
        scale_kernel,
        out_shape=[
            jax.ShapeDtypeStruct((NX, BLOCK), f32),
            jax.ShapeDtypeStruct((GRID, NX, BLOCK), f32),
            jax.ShapeDtypeStruct((GRID, NX, BLOCK), f32),
        ],
        compiler_params=vmem(16),
        name="scales",
    )(sums.reshape(NX, NY * NC, BLOCK))
    at = lax.axis_index("dp_0")
    mean = lax.dynamic_index_in_dim(mean, at, 0, keepdims=False)
    scale = lax.dynamic_index_in_dim(scale, at, 1, keepdims=False).reshape(GRID, GROUPS, GROUP)
    inverse = lax.dynamic_index_in_dim(inverse, at, 1, keepdims=False).reshape(GRID, GROUPS, GROUP)
    own_mean = lax.dynamic_slice_in_dim(mean, lax.axis_index(ZC) * GROUP, GROUP)

    shares = []
    for units, part in zip(CHUNKS, received):
        partial = pl.pallas_call(
            chunk_kernel(units),
            out_shape=jax.ShapeDtypeStruct((NX, units, GRID, ROWS, TOKENS), bf16),
            scratch_shapes=[
                pltpu.VMEM((TOKENS, BLOCK), bf16),
                pltpu.VMEM((GRID * UNIT, BLOCK), bf16),
                pltpu.VMEM((GRID * UNIT, BLOCK), bf16),
            ],
            compiler_params=vmem(48),
            name="candidates",
        )(part, own, other, scale, inverse)
        shares.append(lax.all_to_all(partial, "dp_0", 0, 0, tiled=True))
    column_errors, totals = pl.pallas_call(
        error_kernel,
        out_shape=[jax.ShapeDtypeStruct((GRID, UNITS * ROWS), f32), jax.ShapeDtypeStruct((1, GRID), f32)],
        compiler_params=vmem(16),
        name="column_errors",
    )(*shares)
    totals = spread(totals, ALL, NX * NY * NZ * NC)
    errors = jnp.sum(totals.reshape(-1, GRID), axis=0) / (TOKENS * F)
    return (own_mean, column_errors, errors)


def solution(mesh):
    torus = Mesh(
        mesh.devices.reshape(NX, NZ, NC, mesh.shape["tensor"]), ("dp_0", "dp_1", "dp_2", "tensor")
    )
    placed = (P(DP, "tensor"), P(DP, "tensor"))
    return jax.shard_map(
        on_device,
        mesh=torus,
        in_specs=placed,
        out_specs=(P(DP), P(None, TENSOR_DP), P()),
        check_vma=False,
    )
```

time: 335 us -> 206 us (0.61)
  other arithmetic: 97.2 us -> 0.8 us
  matrix products: 44 us -> 0 us
  local copies, waits for them, and re-layouts: 29.7 us -> 3.93 us
  Pallas kernels: 0 us -> 24.1 us
  waiting for transfers between devices: 88.4 us -> 110 us
  between operations: 14.1 us -> 0.71 us
  starting transfers between devices: 12.1 us -> 23.6 us
  blocking collectives: 48.5 us -> 41.1 us
    convert_element_type x5 -> x0, other arithmetic: 75.2 us -> none  [the longest x4 73 us: local_error(): ((levels * quant_step).reshape(D, width) / factor[:, None]).astype(jnp.bf...]
    all_to_all x1 -> x4, waiting for transfers between devices: 52.4 us -> 106 us  [the longest x1 41.4 us: on_device(): received = [lax.all_to_all(part, ZC, 0, 0, tiled=True) for part in columns]]
    dot_general x5 -> x0, matrix products: 44 us -> none  [the longest x4 35.2 us: local_error(): quant_out = jnp.dot(gathered, dequant, preferred_element_type=jnp.float32)]
    psum x4 -> x0, blocking collectives: 37.5 us -> none  [by_axis(): return functools.reduce(lax.psum, axes, shard)]
    all_gather x1 -> x0, waiting for transfers between devices: 36 us -> none  [on_device(): gathered = lax.all_gather(widened, DP, axis=0, tiled=True)]
    all_to_all x1 -> x2, blocking collectives: 10.9 us -> 41.1 us  [spread(): return lax.all_to_all(wide, axes, 0, 0, tiled=True)]
    pallas_call x0 -> x5, Pallas kernels: none -> 24.1 us  [the longest x1 20.3 us: on_device(): pl.pallas_call(chunk_kernel(units), out_shape=jax.ShapeDtypeStruct((NX, u...]
    unnamed x3, local copies, waits for them, and re-layouts: 21.6 us -> 1.04 us
  transfers between devices with their start and end apart: 2 -> 6, of which waited for: 2 -> 5; matrix products, arithmetic and copies ran while one was open for 3% -> 1% of each run, Pallas kernels for 0% -> 1%
where the time goes in v1:
time: 206 us; the launch traced here: 204 us
  waiting for transfers between devices  110 us (53%)
  blocking collectives  41.1 us (20%)
  Pallas kernels  24.1 us (12%)
  starting transfers between devices  23.6 us (11%)
  local copies, waits for them, and re-layouts  3.93 us (2%)
    all_to_all x1, waiting for transfers between devices, on_device(): received = [lax.all_to_all(part, ZC, 0, 0, tiled=True) for part in columns]  41.4 us
    all_to_all x2, blocking collectives, spread(): return lax.all_to_all(wide, axes, 0, 0, tiled=True)  41.1 us
    all_to_all x1, waiting for transfers between devices, on_device(): shares.append(lax.all_to_all(partial, 'dp_0', 0, 0, tiled=True))  33 us
    all_to_all x2, waiting for transfers between devices, spread(): return lax.all_to_all(wide, axes, 0, 0, tiled=True)  31.3 us
    pallas_call x1, Pallas kernels, on_device(): pl.pallas_call(chunk_kernel(units), out_shape=jax.ShapeDtypeStruct((NX, u...  20.3 us
    all_to_all x2, starting transfers between devices, spread(): return lax.all_to_all(wide, axes, 0, 0, tiled=True)  11 us
    all_to_all x1, starting transfers between devices, on_device(): shares.append(lax.all_to_all(partial, 'dp_0', 0, 0, tiled=True))  5.13 us
  transfers between devices with their start and end apart: 6, of which 5 were waited for; matrix products, arithmetic and copies ran while one was open for 1% of the time, Pallas kernels for 1%

profile of v1, /device:TPU:2, one launch (start us, length us, event | category | flops | bytes accessed | tf_op | source)
XLA Modules:
  0.0 203.8 jit_solution(9339103734839442758)
XLA Ops:
  0.6 3.5 %collective-permute-start = (bf16[12,2048]{1,0:T(8,128)(2,1)}, bf16[12,2048]{1,0:T(8,128)(2,1)S(1)}, u32[]{:S(2)}, u32[]{:S(2)}) collective-permute-start(bf16[12,2048]{1,0:T(8,128)(2,1)} %param.2), channel_id=1, source_target_pairs={{0,0},{1,64},{2,128},{3,192},{64,1},{65,65},{66,129},{67,193},{128... | collective-permute-start | bytes 147464 | tf_op jit(solution)/shard_map/ppermute | solution.py:155
  4.1 3.8 %collective-permute-done = bf16[12,2048]{1,0:T(8,128)(2,1)S(1)} collective-permute-done((bf16[12,2048]{1,0:T(8,128)(2,1)}, bf16[12,2048]{1,0:T(8,128)(2,1)S(1)}, u32[]{:S(2)}, u32[]{:S(2)}) %collective-permute-start) | collective-permute-done | bytes 49184 | tf_op jit(solution)/shard_map/ppermute | solution.py:155
  7.9 24.6 %all_to_all.30.parts_ref = bf16[8,12,2048]{2,1,0:T(8,128)(2,1)S(1)} all-to-all(bf16[8,12,2048]{2,1,0:T(8,128)(2,1)S(1)} %broadcast_in_dim.12), channel_id=1, replica_groups=mesh['dp_0'=4,'dp_1'=8,'dp_2'=2,'tensor'=4] {'dp_1'}, dimensions={0} | all-to-all | bytes 786432 | tf_op jit(solution)/shard_map/all_to_all | solution.py:149
  32.6 0.3 join_tokens.1
  32.8 0.1 broadcast_in_dim.14
  33.0 16.5 %all_to_all.31 = f32[32,1,2048]{2,1,0:T(1,128)} all-to-all(f32[32,1,2048]{2,1,0:T(1,128)S(1)} %broadcast_in_dim.14), channel_id=1, replica_groups=mesh['dp_0'=4,'dp_1'=8,'dp_2'=2,'tensor'=4] {'dp_0','tensor','dp_2'}, dimensions={0} | all-to-all | bytes 524288 | tf_op jit(solution)/shard_map/all_to_all | solution.py:149
  49.5 1.3 broadcast_in_dim.15
  50.8 0.0 copy-start
  50.8 3.7 %all-to-all-start.3 = ((bf16[4,96,2048]{2,1,0:T(8,128)(2,1)}), bf16[4,96,2048]{2,1,0:T(8,128)(2,1)S(1)}, u32[]{:S(2)}, u32[]{:S(2)}) async-start(bf16[4,96,2048]{2,1,0:T(8,128)(2,1)} %broadcast_in_dim.15), calls=%async_computation.3 | async-start | bytes 3145728 | tf_op jit(solution)/shard_map/all_to_all | solution.py:149
  54.5 0.0 copy-done
  54.5 1.8 split_columns.1
  56.3 19.6 %all-to-all-done.3 = bf16[4,96,2048]{2,1,0:T(8,128)(2,1)S(1)} async-done(((bf16[4,96,2048]{2,1,0:T(8,128)(2,1)}), bf16[4,96,2048]{2,1,0:T(8,128)(2,1)S(1)}, u32[]{:S(2)}, u32[]{:S(2)}) %all-to-all-start.3) | async-done | bytes 1572896 | tf_op jit(solution)/shard_map/all_to_all | solution.py:149
  75.9 3.7 %all-to-all-start.2 = ((bf16[16,448,128]{2,1,0:T(8,128)(2,1)}), bf16[16,448,128]{2,1,0:T(8,128)(2,1)S(1)}, u32[]{:S(2)}, u32[]{:S(2)}) async-start(bf16[16,448,128]{2,1,0:T(8,128)(2,1)} %split_columns.1), calls=%async_computation.2 | async-start | bytes 3670016 | tf_op jit(solution)/shard_map/all_to_all | solution.py:163
  79.6 0.3 collective-permute-start.1
  79.9 1.0 copy.9
  81.0 0.6 scales.1
  81.6 0.1 constant_dynamic-slice_fusion
  81.7 41.4 %all-to-all-done.2.columns_ref = bf16[16,448,128]{2,1,0:T(8,128)(2,1)S(1)} async-done(((bf16[16,448,128]{2,1,0:T(8,128)(2,1)}), bf16[16,448,128]{2,1,0:T(8,128)(2,1)S(1)}, u32[]{:S(2)}, u32[]{:S(2)}) %all-to-all-start.2) | async-done | bytes 1835040 | tf_op jit(solution)/shard_map/all_to_all | solution.py:163
  123.1 0.0 collective-permute-done.1.other_ref
  123.1 20.3 %candidates.1 = bf16[4,7,4,16,768]{4,3,2,1,0:T(8,128)(2,1)} custom-call(bf16[16,448,128]{2,1,0:T(8,128)(2,1)S(1)} %all-to-all-done.2.columns_ref, bf16[384,2048]{1,0:T(8,128)(2,1)S(1)} %bitcast.11, bf16[384,2048]{1,0:T(8,128)(2,1)} %collective-permute-done.1.other_ref, f32[4,16,128]{2,1,0:T(8,128)S(1)} %bitcast.14, f32[4,16,128]{2,1,0:T(8,128)S(1)} %bitcast.13), custom_call_target="tpu_custom_call" | custom-call | tf_op jit(solution)/shard_map/candidates/pallas_call | solution.py:191
  143.4 5.1 %all-to-all-start.4 = ((bf16[4,7,4,16,768]{4,3,2,1,0:T(8,128)(2,1)}), bf16[4,7,4,16,768]{4,3,2,1,0:T(8,128)(2,1)S(1)}, u32[]{:S(2)}, u32[]{:S(2)}) async-start(bf16[4,7,4,16,768]{4,3,2,1,0:T(8,128)(2,1)} %candidates.1), calls=%async_computation.4 | async-start | bytes 5505024 | tf_op jit(solution)/shard_map/all_to_all | solution.py:202
  148.5 33.0 %all-to-all-done.4.refs_0_ = bf16[4,7,4,16,768]{4,3,2,1,0:T(8,128)(2,1)S(1)} async-done(((bf16[4,7,4,16,768]{4,3,2,1,0:T(8,128)(2,1)}), bf16[4,7,4,16,768]{4,3,2,1,0:T(8,128)(2,1)S(1)}, u32[]{:S(2)}, u32[]{:S(2)}) %all-to-all-start.4) | async-done | bytes 2752544 | tf_op jit(solution)/shard_map/all_to_all | solution.py:202
  181.5 1.2 column_errors.1
  182.7 0.7 broadcast_in_dim.33
  183.4 7.3 %all-to-all-start.5 = ((f32[256,1,4]{2,1,0:T(1,128)}), f32[256,1,4]{2,1,0:T(1,128)S(1)}, u32[]{:S(2)}, u32[]{:S(2)}) async-start(f32[256,1,4]{2,1,0:T(1,128)} %broadcast_in_dim.33), calls=%async_computation.5 | async-start | bytes 262144 | tf_op jit(solution)/shard_map/all_to_all | solution.py:149
  190.7 0.6 dynamic-slice_bitcast_fusion
  191.3 11.7 %all-to-all-done.5 = f32[256,1,4]{2,1,0:T(1,128)S(1)} async-done(((f32[256,1,4]{2,1,0:T(1,128)}), f32[256,1,4]{2,1,0:T(1,128)S(1)}, u32[]{:S(2)}, u32[]{:S(2)}) %all-to-all-start.5) | async-done | bytes 4128 | tf_op jit(solution)/shard_map/all_to_all | solution.py:149
  203.0 0.3 reduce_sum.9
  203.3 0.5 broadcast_multiply_fusion
  (1 shorter events, 0.0 us)
Async XLA Ops:
  0.6 7.3 %collective-permute-start = (bf16[12,2048]{1,0:T(8,128)(2,1)}, bf16[12,2048]{1,0:T(8,128)(2,1)S(1)}, u32[]{:S(2)}, u32[]{:S(2)}) collective-permute-start(bf16[12,2048]{1,0:T(8,128)(2,1)} %param.2), channel_id=1, source_target_pairs={{0,0},{1,64},{2,128},{3,192},{64,1},{65,65},{66,129},{67,193},{128... | collective-permute-start | bytes 147464 | tf_op jit(solution)/shard_map/ppermute | solution.py:155
  50.8 3.7 %copy-start = (bf16[128,7168]{1,0:T(8,128)(2,1)S(1)}, bf16[128,7168]{1,0:T(8,128)(2,1)}, u32[]{:S(2)}) copy-start(bf16[128,7168]{1,0:T(8,128)(2,1)} %weight_ref.1) | copy-start | bytes 5505028
  50.8 25.1 %all-to-all-start.3 = ((bf16[4,96,2048]{2,1,0:T(8,128)(2,1)}), bf16[4,96,2048]{2,1,0:T(8,128)(2,1)S(1)}, u32[]{:S(2)}, u32[]{:S(2)}) async-start(bf16[4,96,2048]{2,1,0:T(8,128)(2,1)} %broadcast_in_dim.15), calls=%async_computation.3 | async-start | bytes 3145728 | tf_op jit(solution)/shard_map/all_to_all | solution.py:149
  75.9 47.2 %all-to-all-start.2 = ((bf16[16,448,128]{2,1,0:T(8,128)(2,1)}), bf16[16,448,128]{2,1,0:T(8,128)(2,1)S(1)}, u32[]{:S(2)}, u32[]{:S(2)}) async-start(bf16[16,448,128]{2,1,0:T(8,128)(2,1)} %split_columns.1), calls=%async_computation.2 | async-start | bytes 3670016 | tf_op jit(solution)/shard_map/all_to_all | solution.py:163
  79.6 43.5 %collective-permute-start.1 = (bf16[384,2048]{1,0:T(8,128)(2,1)S(1)}, bf16[384,2048]{1,0:T(8,128)(2,1)}, u32[]{:S(2)}, u32[]{:S(2)}) collective-permute-start(bf16[384,2048]{1,0:T(8,128)(2,1)S(1)} %bitcast.10), channel_id=1, source_target_pairs={{0,4},{4,0},{1,5},{5,1},{2,6},{6,2},{3,7},{7,3},{8,12},{12,8},{9,1... | collective-permute-start | bytes 4718600 | tf_op jit(solution)/shard_map/ppermute | solution.py:172
  143.4 38.1 %all-to-all-start.4 = ((bf16[4,7,4,16,768]{4,3,2,1,0:T(8,128)(2,1)}), bf16[4,7,4,16,768]{4,3,2,1,0:T(8,128)(2,1)S(1)}, u32[]{:S(2)}, u32[]{:S(2)}) async-start(bf16[4,7,4,16,768]{4,3,2,1,0:T(8,128)(2,1)} %candidates.1), calls=%async_computation.4 | async-start | bytes 5505024 | tf_op jit(solution)/shard_map/all_to_all | solution.py:202
  183.4 19.6 %all-to-all-start.5 = ((f32[256,1,4]{2,1,0:T(1,128)}), f32[256,1,4]{2,1,0:T(1,128)S(1)}, u32[]{:S(2)}, u32[]{:S(2)}) async-start(f32[256,1,4]{2,1,0:T(1,128)} %broadcast_in_dim.33), calls=%async_computation.5 | async-start | bytes 262144 | tf_op jit(solution)/shard_map/all_to_all | solution.py:149

commit v2 on v1

v2 whole, which is shorter than its diff:
```python
import jax
import jax.numpy as jnp
from jax import lax
from jax.experimental import pallas as pl
from jax.experimental.pallas import tpu as pltpu
from jax.sharding import Mesh
from jax.sharding import PartitionSpec as P

D = 8192
F = 28672
GROUP = 128
GRID = 4
TOKENS = 768
DP = ("dp_0", "dp_1", "dp_2")
TENSOR_DP = ("tensor", "dp_0", "dp_1", "dp_2")
ZC = ("dp_1", "dp_2")
NX, NZ, NC, NY = 4, 8, 2, 4
UNITS = 7
ROWS = 16
UNIT = NX * ROWS
BLOCK = D // NX
GROUPS = BLOCK // GROUP
SENDS = (3, 4)
PIECES = ((0, 0, 3), (1, 0, 2), (1, 2, 2))
MIB = 1 << 20

SINE = (
    0.9999996039230294,
    -6.579691569847717,
    12.98643599053418,
    -12.188101430391939,
    6.558041838366218,
    -1.9530314806292366,
)


def starts():
    first, out = 0, []
    for units in SENDS:
        out.append(first)
        first += units
    return out


def split_columns(x_ref, weight_ref, *out_refs):
    for block in range(weight_ref.shape[1] // 128):
        turned = weight_ref[:, block * 128 : (block + 1) * 128].T
        for piece in range(128 // ROWS):
            column = block * 128 + piece * ROWS
            x, rest = divmod(column, F // NY // NX)
            owner, rest = divmod(rest, UNITS * ROWS)
            unit = rest // ROWS
            hops = (x + NX - x_ref[0]) % NX
            for out, first, units in zip(out_refs, starts(), SENDS):
                if first <= unit < first + units:
                    at = pl.multiple_of(((unit - first) * NX + hops) * ROWS, ROWS)
                    out[owner, pl.ds(at, ROWS), :] = turned[piece * ROWS : (piece + 1) * ROWS, :]


def join_tokens(parts_ref, out_ref, sums_ref):
    total = jnp.zeros((1, BLOCK), jnp.float32)
    for part in range(NZ):
        rows = parts_ref[part]
        out_ref[part * 12 : (part + 1) * 12, :] = rows
        total += jnp.sum(jnp.abs(rows.astype(jnp.float32)), axis=0, keepdims=True)
    sums_ref[...] = total


def mean_kernel(core_0, core_1, mean_ref):
    mean_ref[...] = (core_0[...] + core_1[...]) / TOKENS + 1e-06


def scale_kernel(mean_0, mean_1, mean_2, mean_3, scale_ref, inverse_ref):
    logs = [jnp.log(mean[...]) for mean in (mean_0, mean_1, mean_2, mean_3)]
    for k in range(GRID):
        raws = [jnp.exp((k / GRID) * log) for log in logs]
        top = jnp.max(jnp.maximum(jnp.maximum(raws[0], raws[1]), jnp.maximum(raws[2], raws[3])))
        bottom = jnp.min(jnp.minimum(jnp.minimum(raws[0], raws[1]), jnp.minimum(raws[2], raws[3])))
        scale = raws[0] / jnp.sqrt(top * bottom)
        scale_ref[k] = scale
        inverse_ref[k] = 1.0 / scale


def quantize(columns_ref, rows, scale_ref, inverse_ref, delta_ref):
    for group in range(GROUPS):
        packed = columns_ref[group, rows, :]
        wide = packed.astype(jnp.float32)
        for k in range(GRID):
            scaled = wide if k == 0 else wide * scale_ref[k, group : group + 1, :]
            top = jnp.max(jnp.abs(scaled), axis=1, keepdims=True) + 1e-06
            v = scaled * (7.0 / top)
            r = v - jnp.round(v)
            square = r * r
            poly = jnp.full_like(square, SINE[-1])
            for coefficient in SINE[-2::-1]:
                poly = poly * square + coefficient
            shift = (r * poly) * (top * (1.0 / 7.0))
            if k:
                shift = shift * inverse_ref[k, group : group + 1, :]
            dequant = (wide - shift).astype(jnp.bfloat16)
            delta_ref[k * UNIT : (k + 1) * UNIT, group * GROUP : (group + 1) * GROUP] = dequant - packed


def piece_kernel(first, units, gathers):
    def body(columns_ref, scale_ref, inverse_ref, *refs):
        if gathers:
            parts, out_refs, tokens, deltas = refs[:8], refs[8:12], refs[12], refs[13:]
            for at, part in enumerate(parts):
                tokens[at * 96 : (at + 1) * 96, :] = part[...]
        else:
            tokens, out_refs, deltas = refs[0], refs[1:5], refs[5:]
        for unit in range(units):
            delta = deltas[unit % 2]
            quantize(columns_ref, pl.ds((first + unit) * UNIT, UNIT), scale_ref, inverse_ref, delta)
            out = lax.dot_general(
                delta[...], tokens[...], (((1,), (1,)), ((), ())), preferred_element_type=jnp.float32
            ).astype(jnp.bfloat16)
            for k in range(GRID):
                for hops in range(NX):
                    at = k * UNIT + hops * ROWS
                    out_refs[hops][unit, k] = out[at : at + ROWS, :]

    return body


def error_kernel(*refs):
    *parts, sums_ref, total_ref = refs
    rows = []
    for k in range(GRID):
        for piece in range(len(PIECES)):
            shares = parts[piece * NX : (piece + 1) * NX]
            for unit in range(shares[0].shape[0]):
                block = shares[0][unit, k].astype(jnp.float32)
                for share in shares[1:]:
                    block += share[unit, k].astype(jnp.float32)
                block = block * block
                lanes = block[:, :128]
                for at in range(128, TOKENS, 128):
                    lanes += block[:, at : at + 128]
                rows.append(lanes)
    sums = jnp.sum(jnp.concatenate(rows, axis=0).T, axis=0, keepdims=True)
    width = UNITS * ROWS
    for k in range(GRID):
        row = sums[:, k * width : (k + 1) * width]
        sums_ref[k : k + 1, :] = row
        total_ref[:, k : k + 1] = jnp.sum(row, axis=1, keepdims=True)


def kernel(body, out_shape, limit=8, flops=0, **more):
    params = pltpu.CompilerParams(vmem_limit_bytes=limit * MIB)
    if flops:
        more["cost_estimate"] = pl.CostEstimate(flops=flops, transcendentals=0, bytes_accessed=0)
    return pl.pallas_call(body, out_shape=out_shape, compiler_params=params, **more)


def spread(value, axes, size):
    wide = jnp.broadcast_to(value[None], (size, *value.shape))
    return lax.all_to_all(wide, axes, 0, 0, tiled=True)


def shifted(value, axis, hops):
    size = lax.axis_size(axis)
    return lax.ppermute(value, axis, [(i, (i + hops) % size) for i in range(size)])


def after(value, *others):
    return lax.optimization_barrier((value, *others))[0]


def search(activations, weight):
    array = jax.ShapeDtypeStruct
    f32, bf16 = jnp.float32, jnp.bfloat16
    turn = [(x * NY + y, y * NY + x) for x in range(NX) for y in range(NY)]
    turned = lax.ppermute(activations, ("dp_0", "tensor"), turn)
    parts = spread(turned, "dp_1", NZ)
    columns = kernel(
        split_columns,
        [array((NZ * NC, u * UNIT, GROUP), bf16) for u in SENDS],
        in_specs=[pl.BlockSpec(memory_space=pltpu.SMEM), pl.BlockSpec(memory_space=pltpu.VMEM)],
    )(lax.axis_index("dp_0").reshape(1), after(weight, turned))
    parts = after(parts, *columns)
    joined, sums = kernel(join_tokens, [array((96, BLOCK), bf16), array((1, BLOCK), f32)])(parts)

    sums = sums.reshape(GROUPS, GROUP)
    around = [shifted(sums, "tensor", hops) for hops in (2, 1, 3)]
    sums = (sums + around[0]) + (around[1] + around[2])
    mean = kernel(mean_kernel, array((GROUPS, GROUP), f32))(sums, shifted(sums, "dp_2", 1))
    around = [shifted(mean, "dp_0", hops) for hops in (2, 1, 3)]
    scale, inverse = kernel(scale_kernel, [array((GRID, GROUPS, GROUP), f32)] * 2)(mean, *around)

    received = []
    for part, gate in zip(columns, ([joined], [scale])):
        part = after(part, *gate, *received)
        received.append(lax.all_to_all(part, ZC, 0, 0, tiled=True))

    tokens = [joined] + [shifted(joined, "tensor", hops) for hops in (2, 1, 3)]
    tokens += [shifted(part, "dp_2", 1) for part in tokens]

    shares = []
    for at, (source, first, units) in enumerate(PIECES):
        gathers = at == 0
        out_shape = [array((units, GRID, ROWS, TOKENS), bf16)] * NX
        if gathers:
            out_shape.append(array((TOKENS, BLOCK), bf16))
        columns = received[source] if gathers else after(received[source], shares[-NX])
        partial = kernel(
            piece_kernel(first, units, gathers),
            out_shape,
            limit=14,
            flops=3 * units * GRID * UNIT * TOKENS * BLOCK,
            scratch_shapes=[pltpu.VMEM((GRID * UNIT, BLOCK), bf16)] * min(units, 2),
        )(columns, scale, inverse, *tokens)
        if gathers:
            tokens = partial[NX:]
        shares += [partial[0]] + [shifted(partial[hops], "dp_0", hops) for hops in (2, 1, 3)]
    sums, totals = kernel(error_kernel, [array((GRID, UNITS * ROWS), f32), array((1, GRID), f32)])(*shares)
    totals = jnp.sum(spread(totals, ("dp_0", "tensor"), NX * NY), axis=0)
    own_mean = lax.dynamic_slice_in_dim(after(mean, sums).reshape(-1), lax.axis_index(ZC) * GROUP, GROUP)
    errors = jnp.sum(spread(totals, ZC, NZ * NC), axis=0).reshape(GRID) / (TOKENS * F)
    column_errors = after(sums, totals) / TOKENS
    return (own_mean, column_errors, errors)


def solution(mesh):
    torus = Mesh(
        mesh.devices.reshape(NX, NZ, NC, mesh.shape["tensor"]), ("dp_0", "dp_1", "dp_2", "tensor")
    )
    placed = (P(DP, "tensor"), P(DP, "tensor"))
    return jax.shard_map(
        search,
        mesh=torus,
        in_specs=placed,
        out_specs=(P(DP), P(None, TENSOR_DP), P()),
        check_vma=False,
    )
```

time: 206 us -> 169 us (0.82)
  starting transfers between devices: 23.6 us -> 66.1 us
  waiting for transfers between devices: 110 us -> 68.8 us
  blocking collectives: 41.1 us -> 0 us
  local copies, waits for them, and re-layouts: 3.93 us -> 7.67 us
    all_to_all x2, waiting for transfers between devices: 74.4 us -> 0.56 us  [search(): received.append(lax.all_to_all(part, ZC, 0, 0, tiled=True))]
    all_to_all x2 -> x0, blocking collectives: 41.1 us -> none  [spread(): return lax.all_to_all(wide, axes, 0, 0, tiled=True)]
    ppermute x2 -> x24, waiting for transfers between devices: 3.81 us -> 42.7 us  [the longest x23 38.9 us: shifted(): lax.ppermute(value, axis, [(i, (i + hops) % size) for i in range(size)])]
    ppermute x2 -> x24, starting transfers between devices: 3.75 us -> 35.9 us  [the longest x23 32.5 us: shifted(): lax.ppermute(value, axis, [(i, (i + hops) % size) for i in range(size)])]
    all_to_all x2 -> x3, starting transfers between devices: 11 us -> 20 us  [spread(): return lax.all_to_all(wide, axes, 0, 0, tiled=True)]
    all_to_all x2 -> x3, waiting for transfers between devices: 31.3 us -> 25.6 us  [spread(): return lax.all_to_all(wide, axes, 0, 0, tiled=True)]
    unnamed x3 -> x6, local copies, waits for them, and re-layouts: 1.04 us -> 5.02 us
    pallas_call x5 -> x8, Pallas kernels: 24.1 us -> 22.5 us  [the longest x3 19.6 us: search(): kernel(piece_kernel(first, units, gathers), out_shape, limit=14, flops=3...]
  transfers between devices with their start and end apart: 6 -> 29, of which waited for: 5 -> 19; matrix products, arithmetic and copies ran while one was open for 1% -> 1% of each run, Pallas kernels for 1% -> 13%
where the time goes in v2:
time: 169 us; the launch traced here: 167 us
  waiting for transfers between devices  68.8 us (41%)
  starting transfers between devices  66.1 us (39%)
  Pallas kernels  22.5 us (13%)
  local copies, waits for them, and re-layouts  7.67 us (5%)
    ppermute x23, waiting for transfers between devices, shifted(): lax.ppermute(value, axis, [(i, (i + hops) % size) for i in range(size)])  38.9 us
    ppermute x23, starting transfers between devices, shifted(): lax.ppermute(value, axis, [(i, (i + hops) % size) for i in range(size)])  32.5 us
    all_to_all x3, waiting for transfers between devices, spread(): return lax.all_to_all(wide, axes, 0, 0, tiled=True)  25.6 us
    all_to_all x3, starting transfers between devices, spread(): return lax.all_to_all(wide, axes, 0, 0, tiled=True)  20 us
    pallas_call x3, Pallas kernels, search(): kernel(piece_kernel(first, units, gathers), out_shape, limit=14, flops=3...  19.6 us
    all_to_all x2, starting transfers between devices, search(): received.append(lax.all_to_all(part, ZC, 0, 0, tiled=True))  10.2 us
    unnamed x6, local copies, waits for them, and re-layouts  5.02 us
    ppermute x1, waiting for transfers between devices, search(): turned = lax.ppermute(activations, ('dp_0', 'tensor'), turn)  3.8 us
  transfers between devices with their start and end apart: 29, of which 19 were waited for; matrix products, arithmetic and copies ran while one was open for 1% of the time, Pallas kernels for 13%

profile of v2, /device:TPU:2, one launch (start us, length us, event | category | flops | bytes accessed | tf_op | source)
XLA Modules:
  0.0 167.0 jit_solution(17228745405869093296)
XLA Ops:
  0.6 3.5 %collective-permute-start = (bf16[12,2048]{1,0:T(8,128)(2,1)}, bf16[12,2048]{1,0:T(8,128)(2,1)S(1)}, u32[]{:S(2)}, u32[]{:S(2)}) collective-permute-start(bf16[12,2048]{1,0:T(8,128)(2,1)} %param.2), channel_id=1, source_target_pairs={{0,0},{1,64},{2,128},{3,192},{64,1},{65,65},{66,129},{67,193},{128... | collective-permute-start | bytes 147464 | tf_op jit(solution)/shard_map/ppermute | solution.py:174
  4.1 3.8 %collective-permute-done = bf16[12,2048]{1,0:T(8,128)(2,1)S(1)} collective-permute-done((bf16[12,2048]{1,0:T(8,128)(2,1)}, bf16[12,2048]{1,0:T(8,128)(2,1)S(1)}, u32[]{:S(2)}, u32[]{:S(2)}) %collective-permute-start) | collective-permute-done | bytes 49184 | tf_op jit(solution)/shard_map/ppermute | solution.py:174
  7.9 0.8 broadcast_in_dim.8
  8.7 8.5 %all-to-all-start = ((bf16[8,12,2048]{2,1,0:T(8,128)(2,1)}), bf16[8,12,2048]{2,1,0:T(8,128)(2,1)S(1)}, u32[]{:S(2)}, u32[]{:S(2)}) async-start(bf16[8,12,2048]{2,1,0:T(8,128)(2,1)} %broadcast_in_dim.8), calls=%async_computation | async-start | bytes 1048576 | tf_op jit(solution)/shard_map/all_to_all | solution.py:158
  17.2 1.5 copy-done
  18.7 1.8 %shard_map.49 = (bf16[16,192,128]{2,1,0:T(8,128)(2,1)}, bf16[16,256,128]{2,1,0:T(8,128)(2,1)}) custom-call(s32[1]{0:T(128)} %bitcast.x_ref, bf16[128,7168]{1,0:T(8,128)(2,1)S(1)} %copy-done), custom_call_target="tpu_custom_call" | custom-call | tf_op jit(solution)/shard_map/pallas_call | solution.py:176
  20.5 13.1 %all-to-all-done.parts_ref = bf16[8,12,2048]{2,1,0:T(8,128)(2,1)S(1)} async-done(((bf16[8,12,2048]{2,1,0:T(8,128)(2,1)}), bf16[8,12,2048]{2,1,0:T(8,128)(2,1)S(1)}, u32[]{:S(2)}, u32[]{:S(2)}) %all-to-all-start) | async-done | bytes 393248 | tf_op jit(solution)/shard_map/all_to_all | solution.py:158
  33.8 3.6 %all-to-all-start.1 = ((bf16[16,192,128]{2,1,0:T(8,128)(2,1)}), bf16[16,192,128]{2,1,0:T(8,128)(2,1)S(1)}, u32[]{:S(2)}, u32[]{:S(2)}) async-start(bf16[16,192,128]{2,1,0:T(8,128)(2,1)} %get-tuple-element.37), calls=%async_computation.1 | async-start | bytes 1572864 | tf_op jit(solution)/shard_map/all_to_all | solution.py:194
  37.4 6.1 %collective-permute-start.3 = (f32[16,128]{1,0:T(8,128)S(1)}, f32[16,128]{1,0:T(8,128)S(1)}, u32[]{:S(2)}, u32[]{:S(2)}) collective-permute-start(f32[16,128]{1,0:T(8,128)S(1)} %bitcast.5), channel_id=1, source_target_pairs={{0,3},{1,0},{2,1},{3,2},{4,7},{5,4},{6,5},{7,6},{8,11},{9,8},{10,9... | collective-permute-start | bytes 24584 | tf_op jit(solution)/shard_map/ppermute | solution.py:163
  43.5 1.6 collective-permute-start.1
  45.1 3.3 %collective-permute-done.2 = f32[16,128]{1,0:T(8,128)S(1)} collective-permute-done((f32[16,128]{1,0:T(8,128)S(1)}, f32[16,128]{1,0:T(8,128)S(1)}, u32[]{:S(2)}, u32[]{:S(2)}) %collective-permute-start.2) | collective-permute-done | bytes 8224 | tf_op jit(solution)/shard_map/ppermute | solution.py:163
  48.7 1.2 collective-permute-done.4.core_1
  49.9 1.1 collective-permute-start.7
  51.0 1.0 collective-permute-start.6
  51.9 2.1 %collective-permute-start.5 = (f32[16,128]{1,0:T(8,128)S(1)}, f32[16,128]{1,0:T(8,128)S(1)}, u32[]{:S(2)}, u32[]{:S(2)}) collective-permute-start(f32[16,128]{1,0:T(8,128)S(1)} %shard_map.51.mean_0), channel_id=1, source_target_pairs={{0,128},{64,192},{128,0},{192,64},{1,129},{65,193},{129,1},{193,65... | collective-permute-start | bytes 24584 | tf_op jit(solution)/shard_map/ppermute | solution.py:163
  54.0 0.6 collective-permute-done.6.mean_2
  54.6 2.5 %collective-permute-done.5.mean_1 = f32[16,128]{1,0:T(8,128)S(1)} collective-permute-done((f32[16,128]{1,0:T(8,128)S(1)}, f32[16,128]{1,0:T(8,128)S(1)}, u32[]{:S(2)}, u32[]{:S(2)}) %collective-permute-start.5) | collective-permute-done | bytes 8224 | tf_op jit(solution)/shard_map/ppermute | solution.py:163
  58.0 6.5 %all-to-all-start.2 = ((bf16[16,256,128]{2,1,0:T(8,128)(2,1)}), bf16[16,256,128]{2,1,0:T(8,128)(2,1)S(1)}, u32[]{:S(2)}, u32[]{:S(2)}) async-start(bf16[16,256,128]{2,1,0:T(8,128)(2,1)} %get-tuple-element.44), calls=%async_computation.2 | async-start | bytes 2097152 | tf_op jit(solution)/shard_map/all_to_all | solution.py:194
  64.5 4.8 %collective-permute-start.10 = (bf16[96,2048]{1,0:T(8,128)(2,1)S(1)}, bf16[96,2048]{1,0:T(8,128)(2,1)S(1)}, u32[]{:S(2)}, u32[]{:S(2)}) collective-permute-start(bf16[96,2048]{1,0:T(8,128)(2,1)S(1)} %get-tuple-element.36.refs_0_), channel_id=1, source_target_pairs={{0,3},{1,0},{2,1},{3,2},{4,7},{5,4},{6,5},{7,6},{8,11},{9,8},{10,9... | collective-permute-start | bytes 1179656 | tf_op jit(solution)/shard_map/ppermute | solution.py:163
  69.3 1.6 collective-permute-start.8
  71.2 16.0 %collective-permute-done.10.refs_3_ = bf16[96,2048]{1,0:T(8,128)(2,1)S(1)} collective-permute-done((bf16[96,2048]{1,0:T(8,128)(2,1)S(1)}, bf16[96,2048]{1,0:T(8,128)(2,1)S(1)}, u32[]{:S(2)}, u32[]{:S(2)}) %collective-permute-start.10) | collective-permute-done | bytes 393248 | tf_op jit(solution)/shard_map/ppermute | solution.py:163
  87.2 3.4 %collective-permute-done.9.refs_2_ = bf16[96,2048]{1,0:T(8,128)(2,1)S(1)} collective-permute-done((bf16[96,2048]{1,0:T(8,128)(2,1)S(1)}, bf16[96,2048]{1,0:T(8,128)(2,1)S(1)}, u32[]{:S(2)}, u32[]{:S(2)}) %collective-permute-start.9) | collective-permute-done | bytes 393248 | tf_op jit(solution)/shard_map/ppermute | solution.py:163
  91.1 1.2 collective-permute-done.13.refs_6_
  92.8 8.1 %shard_map.53 = (bf16[3,4,16,768]{3,2,1,0:T(8,128)(2,1)S(1)}, bf16[3,4,16,768]{3,2,1,0:T(8,128)(2,1)S(1)}, bf16[3,4,16,768]{3,2,1,0:T(8,128)(2,1)}, bf16[3,4,16,...) custom-call(bf16[16,192,128]{2,1,0:T(8,128)(2,1)S(1)} %all-to-all-done.1.columns_ref, ...), custom_call_target="tpu_custom_call" | custom-call | flops 3623878656 | tf_op jit(solution)/shard_map/pallas_call | solution.py:206
  100.9 1.6 copy-done.1
  102.5 2.5 %collective-permute-start.16 = (bf16[3,4,16,768]{3,2,1,0:T(8,128)(2,1)S(1)}, bf16[3,4,16,768]{3,2,1,0:T(8,128)(2,1)S(1)}, u32[]{:S(2)}, u32[]{:S(2)}) collective-permute-start(bf16[3,4,16,768]{3,2,1,0:T(8,128)(2,1)S(1)} %get-tuple-element.42), channel_id=1, source_target_pairs={{0,64},{64,128},{128,192},{192,0},{1,65},{65,129},{129,193},{193,1... | collective-permute-start | bytes 884744 | tf_op jit(solution)/shard_map/ppermute | solution.py:163
  105.1 1.9 %copy-done.2 = bf16[768,2048]{1,0:T(8,128)(2,1)S(1)} copy-done((bf16[768,2048]{1,0:T(8,128)(2,1)S(1)}, bf16[768,2048]{1,0:T(8,128)(2,1)}, u32[]{:S(2)}) %copy-start.2) | copy-done | bytes 3145752
  106.9 5.8 %shard_map.54 = (bf16[2,4,16,768]{3,2,1,0:T(8,128)(2,1)S(1)}, bf16[2,4,16,768]{3,2,1,0:T(8,128)(2,1)}, bf16[2,4,16,768]{3,2,1,0:T(8,128)(2,1)}, bf16[2,4,16,768]{3,2,1,0:T(8,128)(2,1)}) custom-call(bf16[16,256,128]{2,1,0:T(8,128)(2,1)S(1)} %all-to-all-done.2.columns_ref, f32[4,16,128]{2,1,0:T(8,128)S(1)} %get-tuple-element.38.scale_ref, ...), custom_call_target="tpu_custom_call" | custom-call | flops 2415919104 | tf_op jit(solution)/shard_map/pallas_call | solution.py:206
  112.7 5.8 %shard_map.55 = (bf16[2,4,16,768]{3,2,1,0:T(8,128)(2,1)S(1)}, bf16[2,4,16,768]{3,2,1,0:T(8,128)(2,1)}, bf16[2,4,16,768]{3,2,1,0:T(8,128)(2,1)S(1)}, bf16[2,4,16,768]{3,2,1,0:T(8,128)(2,1)}) custom-call(bf16[16,256,128]{2,1,0:T(8,128)(2,1)S(1)} %all-to-all-done.2.columns_ref, f32[4,16,128]{2,1,0:T(8,128)S(1)} %get-tuple-element.38.scale_ref, ...), custom_call_target="tpu_custom_call" | custom-call | flops 2415919104 | tf_op jit(solution)/shard_map/pallas_call | solution.py:206
  118.5 3.0 %collective-permute-start.21 = (bf16[2,4,16,768]{3,2,1,0:T(8,128)(2,1)S(1)}, bf16[2,4,16,768]{3,2,1,0:T(8,128)(2,1)S(1)}, u32[]{:S(2)}, u32[]{:S(2)}) collective-permute-start(bf16[2,4,16,768]{3,2,1,0:T(8,128)(2,1)S(1)} %get-tuple-element.53), channel_id=1, source_target_pairs={{0,128},{64,192},{128,0},{192,64},{1,129},{65,193},{129,1},{193,65... | collective-permute-start | bytes 589832 | tf_op jit(solution)/shard_map/ppermute | solution.py:163
  121.5 0.6 collective-permute-start.22
  122.1 1.4 collective-permute-start.23
  123.5 1.2 collective-permute-start.18
  124.7 2.5 %collective-permute-start.19 = (bf16[2,4,16,768]{3,2,1,0:T(8,128)(2,1)}, bf16[2,4,16,768]{3,2,1,0:T(8,128)(2,1)S(1)}, u32[]{:S(2)}, u32[]{:S(2)}) collective-permute-start(bf16[2,4,16,768]{3,2,1,0:T(8,128)(2,1)} %get-tuple-element.49), channel_id=1, source_target_pairs={{0,64},{64,128},{128,192},{192,0},{1,65},{65,129},{129,193},{193,1... | collective-permute-start | bytes 589832 | tf_op jit(solution)/shard_map/ppermute | solution.py:163
  127.8 2.2 %collective-permute-start.20 = (bf16[2,4,16,768]{3,2,1,0:T(8,128)(2,1)}, bf16[2,4,16,768]{3,2,1,0:T(8,128)(2,1)S(1)}, u32[]{:S(2)}, u32[]{:S(2)}) collective-permute-start(bf16[2,4,16,768]{3,2,1,0:T(8,128)(2,1)} %get-tuple-element.50), channel_id=1, source_target_pairs={{0,192},{64,0},{128,64},{192,128},{1,193},{65,1},{129,65},{193,129... | collective-permute-start | bytes 589832 | tf_op jit(solution)/shard_map/ppermute | solution.py:163
  129.9 2.6 %collective-permute-done.22.refs_10_ = bf16[2,4,16,768]{3,2,1,0:T(8,128)(2,1)S(1)} collective-permute-done((bf16[2,4,16,768]{3,2,1,0:T(8,128)(2,1)}, bf16[2,4,16,768]{3,2,1,0:T(8,128)(2,1)S(1)}, u32[]{:S(2)}, u32[]{:S(2)}) %collective-permute-start.22) | collective-permute-done | bytes 196640 | tf_op jit(solution)/shard_map/ppermute | solution.py:163
  132.6 1.7 %collective-permute-done.23.refs_11_ = bf16[2,4,16,768]{3,2,1,0:T(8,128)(2,1)S(1)} collective-permute-done((bf16[2,4,16,768]{3,2,1,0:T(8,128)(2,1)}, bf16[2,4,16,768]{3,2,1,0:T(8,128)(2,1)S(1)}, u32[]{:S(2)}, u32[]{:S(2)}) %collective-permute-start.23) | collective-permute-done | bytes 196640 | tf_op jit(solution)/shard_map/ppermute | solution.py:163
  134.3 2.0 %collective-permute-done.18.refs_5_ = bf16[2,4,16,768]{3,2,1,0:T(8,128)(2,1)S(1)} collective-permute-done((bf16[2,4,16,768]{3,2,1,0:T(8,128)(2,1)}, bf16[2,4,16,768]{3,2,1,0:T(8,128)(2,1)S(1)}, u32[]{:S(2)}, u32[]{:S(2)}) %collective-permute-start.18) | collective-permute-done | bytes 196640 | tf_op jit(solution)/shard_map/ppermute | solution.py:163
  136.2 3.1 %collective-permute-done.19.refs_6_ = bf16[2,4,16,768]{3,2,1,0:T(8,128)(2,1)S(1)} collective-permute-done((bf16[2,4,16,768]{3,2,1,0:T(8,128)(2,1)}, bf16[2,4,16,768]{3,2,1,0:T(8,128)(2,1)S(1)}, u32[]{:S(2)}, u32[]{:S(2)}) %collective-permute-start.19) | collective-permute-done | bytes 196640 | tf_op jit(solution)/shard_map/ppermute | solution.py:163
  139.3 0.6 shard_map.56
  139.9 0.6 broadcast_in_dim.10
  140.6 5.1 %all-to-all-start.3 = ((f32[16,1,4]{2,1,0:T(1,128)}), f32[16,1,4]{2,1,0:T(1,128)S(1)}, u32[]{:S(2)}, u32[]{:S(2)}) async-start(f32[16,1,4]{2,1,0:T(1,128)} %broadcast_in_dim.10), calls=%async_computation.3 | async-start | bytes 16384 | tf_op jit(solution)/shard_map/all_to_all | solution.py:158
  145.7 6.1 %all-to-all-done.3 = f32[16,1,4]{2,1,0:T(1,128)S(1)} async-done(((f32[16,1,4]{2,1,0:T(1,128)}), f32[16,1,4]{2,1,0:T(1,128)S(1)}, u32[]{:S(2)}, u32[]{:S(2)}) %all-to-all-start.3) | async-done | bytes 288 | tf_op jit(solution)/shard_map/all_to_all | solution.py:158
  151.8 0.6 broadcast_in_dim.11
  152.4 6.4 %all-to-all-start.4 = ((f32[16,1,4]{2,1,0:T(1,128)}), f32[16,1,4]{2,1,0:T(1,128)S(1)}, u32[]{:S(2)}, u32[]{:S(2)}) async-start(f32[16,1,4]{2,1,0:T(1,128)} %broadcast_in_dim.11), calls=%async_computation.4 | async-start | bytes 16384 | tf_op jit(solution)/shard_map/all_to_all | solution.py:158
  158.8 0.6 broadcast_multiply_fusion
  159.4 0.6 dynamic_slice.3
  160.0 6.4 %all-to-all-done.4 = f32[16,1,4]{2,1,0:T(1,128)S(1)} async-done(((f32[16,1,4]{2,1,0:T(1,128)}), f32[16,1,4]{2,1,0:T(1,128)S(1)}, u32[]{:S(2)}, u32[]{:S(2)}) %all-to-all-start.4) | async-done | bytes 288 | tf_op jit(solution)/shard_map/all_to_all | solution.py:158
  (33 shorter events, 4.0 us)
Async XLA Ops:
  0.6 7.3 %collective-permute-start = (bf16[12,2048]{1,0:T(8,128)(2,1)}, bf16[12,2048]{1,0:T(8,128)(2,1)S(1)}, u32[]{:S(2)}, u32[]{:S(2)}) collective-permute-start(bf16[12,2048]{1,0:T(8,128)(2,1)} %param.2), channel_id=1, source_target_pairs={{0,0},{1,64},{2,128},{3,192},{64,1},{65,65},{66,129},{67,193},{128... | collective-permute-start | bytes 147464 | tf_op jit(solution)/shard_map/ppermute | solution.py:174
  8.7 24.8 %all-to-all-start = ((bf16[8,12,2048]{2,1,0:T(8,128)(2,1)}), bf16[8,12,2048]{2,1,0:T(8,128)(2,1)S(1)}, u32[]{:S(2)}, u32[]{:S(2)}) async-start(bf16[8,12,2048]{2,1,0:T(8,128)(2,1)} %broadcast_in_dim.8), calls=%async_computation | async-start | bytes 1048576 | tf_op jit(solution)/shard_map/all_to_all | solution.py:158
  17.2 1.5 copy-start
  33.8 24.1 %all-to-all-start.1 = ((bf16[16,192,128]{2,1,0:T(8,128)(2,1)}), bf16[16,192,128]{2,1,0:T(8,128)(2,1)S(1)}, u32[]{:S(2)}, u32[]{:S(2)}) async-start(bf16[16,192,128]{2,1,0:T(8,128)(2,1)} %get-tuple-element.37), calls=%async_computation.1 | async-start | bytes 1572864 | tf_op jit(solution)/shard_map/all_to_all | solution.py:194
  37.4 7.7 %collective-permute-start.3 = (f32[16,128]{1,0:T(8,128)S(1)}, f32[16,128]{1,0:T(8,128)S(1)}, u32[]{:S(2)}, u32[]{:S(2)}) collective-permute-start(f32[16,128]{1,0:T(8,128)S(1)} %bitcast.5), channel_id=1, source_target_pairs={{0,3},{1,0},{2,1},{3,2},{4,7},{5,4},{6,5},{7,6},{8,11},{9,8},{10,9... | collective-permute-start | bytes 24584 | tf_op jit(solution)/shard_map/ppermute | solution.py:163
  43.5 4.9 %collective-permute-start.2 = (f32[16,128]{1,0:T(8,128)S(1)}, f32[16,128]{1,0:T(8,128)S(1)}, u32[]{:S(2)}, u32[]{:S(2)}) collective-permute-start(f32[16,128]{1,0:T(8,128)S(1)} %bitcast.6), channel_id=1, source_target_pairs={{0,1},{1,2},{2,3},{3,0},{4,5},{5,6},{6,7},{7,4},{8,9},{9,10},{10,1... | collective-permute-start | bytes 24584 | tf_op jit(solution)/shard_map/ppermute | solution.py:163
  43.5 5.2 %collective-permute-start.1 = (f32[16,128]{1,0:T(8,128)S(1)}, f32[16,128]{1,0:T(8,128)S(1)}, u32[]{:S(2)}, u32[]{:S(2)}) collective-permute-start(f32[16,128]{1,0:T(8,128)S(1)} %bitcast.7), channel_id=1, source_target_pairs={{0,2},{1,3},{2,0},{3,1},{4,6},{5,7},{6,4},{7,5},{8,10},{9,11},{10,... | collective-permute-start | bytes 24584 | tf_op jit(solution)/shard_map/ppermute | solution.py:163
  48.7 1.2 collective-permute-start.4
  49.9 4.1 %collective-permute-start.7 = (f32[16,128]{1,0:T(8,128)S(1)}, f32[16,128]{1,0:T(8,128)S(1)}, u32[]{:S(2)}, u32[]{:S(2)}) collective-permute-start(f32[16,128]{1,0:T(8,128)S(1)} %shard_map.51.mean_0), channel_id=1, source_target_pairs={{0,192},{64,0},{128,64},{192,128},{1,193},{65,1},{129,65},{193,129... | collective-permute-start | bytes 24584 | tf_op jit(solution)/shard_map/ppermute | solution.py:163
  51.0 3.7 %collective-permute-start.6 = (f32[16,128]{1,0:T(8,128)S(1)}, f32[16,128]{1,0:T(8,128)S(1)}, u32[]{:S(2)}, u32[]{:S(2)}) collective-permute-start(f32[16,128]{1,0:T(8,128)S(1)} %shard_map.51.mean_0), channel_id=1, source_target_pairs={{0,64},{64,128},{128,192},{192,0},{1,65},{65,129},{129,193},{193,1... | collective-permute-start | bytes 24584 | tf_op jit(solution)/shard_map/ppermute | solution.py:163
  51.9 5.2 %collective-permute-start.5 = (f32[16,128]{1,0:T(8,128)S(1)}, f32[16,128]{1,0:T(8,128)S(1)}, u32[]{:S(2)}, u32[]{:S(2)}) collective-permute-start(f32[16,128]{1,0:T(8,128)S(1)} %shard_map.51.mean_0), channel_id=1, source_target_pairs={{0,128},{64,192},{128,0},{192,64},{1,129},{65,193},{129,1},{193,65... | collective-permute-start | bytes 24584 | tf_op jit(solution)/shard_map/ppermute | solution.py:163
  58.0 47.1 %all-to-all-start.2 = ((bf16[16,256,128]{2,1,0:T(8,128)(2,1)}), bf16[16,256,128]{2,1,0:T(8,128)(2,1)S(1)}, u32[]{:S(2)}, u32[]{:S(2)}) async-start(bf16[16,256,128]{2,1,0:T(8,128)(2,1)} %get-tuple-element.44), calls=%async_computation.2 | async-start | bytes 2097152 | tf_op jit(solution)/shard_map/all_to_all | solution.py:194
  64.5 22.6 %collective-permute-start.10 = (bf16[96,2048]{1,0:T(8,128)(2,1)S(1)}, bf16[96,2048]{1,0:T(8,128)(2,1)S(1)}, u32[]{:S(2)}, u32[]{:S(2)}) collective-permute-start(bf16[96,2048]{1,0:T(8,128)(2,1)S(1)} %get-tuple-element.36.refs_0_), channel_id=1, source_target_pairs={{0,3},{1,0},{2,1},{3,2},{4,7},{5,4},{6,5},{7,6},{8,11},{9,8},{10,9... | collective-permute-start | bytes 1179656 | tf_op jit(solution)/shard_map/ppermute | solution.py:163
  69.3 21.3 %collective-permute-start.9 = (bf16[96,2048]{1,0:T(8,128)(2,1)S(1)}, bf16[96,2048]{1,0:T(8,128)(2,1)S(1)}, u32[]{:S(2)}, u32[]{:S(2)}) collective-permute-start(bf16[96,2048]{1,0:T(8,128)(2,1)S(1)} %get-tuple-element.36.refs_0_), channel_id=1, source_target_pairs={{0,1},{1,2},{2,3},{3,0},{4,5},{5,6},{6,7},{7,4},{8,9},{9,10},{10,1... | collective-permute-start | bytes 1179656 | tf_op jit(solution)/shard_map/ppermute | solution.py:163
  69.3 21.3 %collective-permute-start.8 = (bf16[96,2048]{1,0:T(8,128)(2,1)S(1)}, bf16[96,2048]{1,0:T(8,128)(2,1)S(1)}, u32[]{:S(2)}, u32[]{:S(2)}) collective-permute-start(bf16[96,2048]{1,0:T(8,128)(2,1)S(1)} %get-tuple-element.36.refs_0_), channel_id=1, source_target_pairs={{0,2},{1,3},{2,0},{3,1},{4,6},{5,7},{6,4},{7,5},{8,10},{9,11},{10,... | collective-permute-start | bytes 1179656 | tf_op jit(solution)/shard_map/ppermute | solution.py:163
  70.8 20.2 %collective-permute-start.11 = (bf16[96,2048]{1,0:T(8,128)(2,1)S(1)}, bf16[96,2048]{1,0:T(8,128)(2,1)S(1)}, u32[]{:S(2)}, u32[]{:S(2)}) collective-permute-start(bf16[96,2048]{1,0:T(8,128)(2,1)S(1)} %get-tuple-element.36.refs_0_), channel_id=1, source_target_pairs={{0,4},{4,0},{1,5},{5,1},{2,6},{6,2},{3,7},{7,3},{8,12},{12,8},{9,1... | collective-permute-start | bytes 1179656 | tf_op jit(solution)/shard_map/ppermute | solution.py:163
  87.1 3.9 %collective-permute-start.14 = (bf16[96,2048]{1,0:T(8,128)(2,1)S(1)}, bf16[96,2048]{1,0:T(8,128)(2,1)S(1)}, u32[]{:S(2)}, u32[]{:S(2)}) collective-permute-start(bf16[96,2048]{1,0:T(8,128)(2,1)S(1)} %collective-permute-done.10.refs_3_), channel_id=1, source_target_pairs={{0,4},{4,0},{1,5},{5,1},{2,6},{6,2},{3,7},{7,3},{8,12},{12,8},{9,1... | collective-permute-start | bytes 1179656 | tf_op jit(solution)/shard_map/ppermute | solution.py:163
  90.5 1.7 %collective-permute-start.13 = (bf16[96,2048]{1,0:T(8,128)(2,1)S(1)}, bf16[96,2048]{1,0:T(8,128)(2,1)S(1)}, u32[]{:S(2)}, u32[]{:S(2)}) collective-permute-start(bf16[96,2048]{1,0:T(8,128)(2,1)S(1)} %collective-permute-done.9.refs_2_), channel_id=1, source_target_pairs={{0,4},{4,0},{1,5},{5,1},{2,6},{6,2},{3,7},{7,3},{8,12},{12,8},{9,1... | collective-permute-start | bytes 1179656 | tf_op jit(solution)/shard_map/ppermute | solution.py:163
  90.5 2.3 %collective-permute-start.12 = (bf16[96,2048]{1,0:T(8,128)(2,1)S(1)}, bf16[96,2048]{1,0:T(8,128)(2,1)S(1)}, u32[]{:S(2)}, u32[]{:S(2)}) collective-permute-start(bf16[96,2048]{1,0:T(8,128)(2,1)S(1)} %collective-permute-done.8.refs_1_), channel_id=1, source_target_pairs={{0,4},{4,0},{1,5},{5,1},{2,6},{6,2},{3,7},{7,3},{8,12},{12,8},{9,1... | collective-permute-start | bytes 1179656 | tf_op jit(solution)/shard_map/ppermute | solution.py:163
  100.9 1.6 copy-start.1
  102.5 19.6 %collective-permute-start.15 = (bf16[3,4,16,768]{3,2,1,0:T(8,128)(2,1)}, bf16[3,4,16,768]{3,2,1,0:T(8,128)(2,1)S(1)}, u32[]{:S(2)}, u32[]{:S(2)}) collective-permute-start(bf16[3,4,16,768]{3,2,1,0:T(8,128)(2,1)} %get-tuple-element.41), channel_id=1, source_target_pairs={{0,128},{64,192},{128,0},{192,64},{1,129},{65,193},{129,1},{193,65... | collective-permute-start | bytes 884744 | tf_op jit(solution)/shard_map/ppermute | solution.py:163
  102.5 21.0 %collective-permute-start.16 = (bf16[3,4,16,768]{3,2,1,0:T(8,128)(2,1)S(1)}, bf16[3,4,16,768]{3,2,1,0:T(8,128)(2,1)S(1)}, u32[]{:S(2)}, u32[]{:S(2)}) collective-permute-start(bf16[3,4,16,768]{3,2,1,0:T(8,128)(2,1)S(1)} %get-tuple-element.42), channel_id=1, source_target_pairs={{0,64},{64,128},{128,192},{192,0},{1,65},{65,129},{129,193},{193,1... | collective-permute-start | bytes 884744 | tf_op jit(solution)/shard_map/ppermute | solution.py:163
  105.0 19.7 %collective-permute-start.17 = (bf16[3,4,16,768]{3,2,1,0:T(8,128)(2,1)S(1)}, bf16[3,4,16,768]{3,2,1,0:T(8,128)(2,1)S(1)}, u32[]{:S(2)}, u32[]{:S(2)}) collective-permute-start(bf16[3,4,16,768]{3,2,1,0:T(8,128)(2,1)S(1)} %get-tuple-element.43), channel_id=1, source_target_pairs={{0,192},{64,0},{128,64},{192,128},{1,193},{65,1},{129,65},{193,129... | collective-permute-start | bytes 884744 | tf_op jit(solution)/shard_map/ppermute | solution.py:163
  105.0 1.9 %copy-start.2 = (bf16[768,2048]{1,0:T(8,128)(2,1)S(1)}, bf16[768,2048]{1,0:T(8,128)(2,1)}, u32[]{:S(2)}) copy-start(bf16[768,2048]{1,0:T(8,128)(2,1)} %copy-done.1) | copy-start | bytes 9437188
  118.5 9.3 %collective-permute-start.21 = (bf16[2,4,16,768]{3,2,1,0:T(8,128)(2,1)S(1)}, bf16[2,4,16,768]{3,2,1,0:T(8,128)(2,1)S(1)}, u32[]{:S(2)}, u32[]{:S(2)}) collective-permute-start(bf16[2,4,16,768]{3,2,1,0:T(8,128)(2,1)S(1)} %get-tuple-element.53), channel_id=1, source_target_pairs={{0,128},{64,192},{128,0},{192,64},{1,129},{65,193},{129,1},{193,65... | collective-permute-start | bytes 589832 | tf_op jit(solution)/shard_map/ppermute | solution.py:163
  121.5 11.1 %collective-permute-start.22 = (bf16[2,4,16,768]{3,2,1,0:T(8,128)(2,1)}, bf16[2,4,16,768]{3,2,1,0:T(8,128)(2,1)S(1)}, u32[]{:S(2)}, u32[]{:S(2)}) collective-permute-start(bf16[2,4,16,768]{3,2,1,0:T(8,128)(2,1)} %get-tuple-element.54), channel_id=1, source_target_pairs={{0,64},{64,128},{128,192},{192,0},{1,65},{65,129},{129,193},{193,1... | collective-permute-start | bytes 589832 | tf_op jit(solution)/shard_map/ppermute | solution.py:163
  122.1 12.2 %collective-permute-start.23 = (bf16[2,4,16,768]{3,2,1,0:T(8,128)(2,1)}, bf16[2,4,16,768]{3,2,1,0:T(8,128)(2,1)S(1)}, u32[]{:S(2)}, u32[]{:S(2)}) collective-permute-start(bf16[2,4,16,768]{3,2,1,0:T(8,128)(2,1)} %get-tuple-element.55), channel_id=1, source_target_pairs={{0,192},{64,0},{128,64},{192,128},{1,193},{65,1},{129,65},{193,129... | collective-permute-start | bytes 589832 | tf_op jit(solution)/shard_map/ppermute | solution.py:163
  123.5 12.7 %collective-permute-start.18 = (bf16[2,4,16,768]{3,2,1,0:T(8,128)(2,1)}, bf16[2,4,16,768]{3,2,1,0:T(8,128)(2,1)S(1)}, u32[]{:S(2)}, u32[]{:S(2)}) collective-permute-start(bf16[2,4,16,768]{3,2,1,0:T(8,128)(2,1)} %get-tuple-element.48), channel_id=1, source_target_pairs={{0,128},{64,192},{128,0},{192,64},{1,129},{65,193},{129,1},{193,65... | collective-permute-start | bytes 589832 | tf_op jit(solution)/shard_map/ppermute | solution.py:163
  124.7 14.6 %collective-permute-start.19 = (bf16[2,4,16,768]{3,2,1,0:T(8,128)(2,1)}, bf16[2,4,16,768]{3,2,1,0:T(8,128)(2,1)S(1)}, u32[]{:S(2)}, u32[]{:S(2)}) collective-permute-start(bf16[2,4,16,768]{3,2,1,0:T(8,128)(2,1)} %get-tuple-element.49), channel_id=1, source_target_pairs={{0,64},{64,128},{128,192},{192,0},{1,65},{65,129},{129,193},{193,1... | collective-permute-start | bytes 589832 | tf_op jit(solution)/shard_map/ppermute | solution.py:163
  127.8 11.6 %collective-permute-start.20 = (bf16[2,4,16,768]{3,2,1,0:T(8,128)(2,1)}, bf16[2,4,16,768]{3,2,1,0:T(8,128)(2,1)S(1)}, u32[]{:S(2)}, u32[]{:S(2)}) collective-permute-start(bf16[2,4,16,768]{3,2,1,0:T(8,128)(2,1)} %get-tuple-element.50), channel_id=1, source_target_pairs={{0,192},{64,0},{128,64},{192,128},{1,193},{65,1},{129,65},{193,129... | collective-permute-start | bytes 589832 | tf_op jit(solution)/shard_map/ppermute | solution.py:163
  140.6 11.2 %all-to-all-start.3 = ((f32[16,1,4]{2,1,0:T(1,128)}), f32[16,1,4]{2,1,0:T(1,128)S(1)}, u32[]{:S(2)}, u32[]{:S(2)}) async-start(f32[16,1,4]{2,1,0:T(1,128)} %broadcast_in_dim.10), calls=%async_computation.3 | async-start | bytes 16384 | tf_op jit(solution)/shard_map/all_to_all | solution.py:158
  152.4 14.0 %all-to-all-start.4 = ((f32[16,1,4]{2,1,0:T(1,128)}), f32[16,1,4]{2,1,0:T(1,128)S(1)}, u32[]{:S(2)}, u32[]{:S(2)}) async-start(f32[16,1,4]{2,1,0:T(1,128)} %broadcast_in_dim.11), calls=%async_computation.4 | async-start | bytes 16384 | tf_op jit(solution)/shard_map/all_to_all | solution.py:158

commit v3 on v2

--- a/solution.py
+++ b/solution.py
@@ -20,8 +20,8 @@
 UNIT = NX * ROWS
 BLOCK = D // NX
 GROUPS = BLOCK // GROUP
-SENDS = (3, 4)
-PIECES = ((0, 0, 3), (1, 0, 2), (1, 2, 2))
+SENDS = (4, 3)
+PIECES = ((0, 0, 4), (1, 0, 3))
 MIB = 1 << 20
 
 SINE = (
@@ -57,13 +57,21 @@
                     out[owner, pl.ds(at, ROWS), :] = turned[piece * ROWS : (piece + 1) * ROWS, :]
 
 
-def join_tokens(parts_ref, out_ref, sums_ref):
-    total = jnp.zeros((1, BLOCK), jnp.float32)
-    for part in range(NZ):
-        rows = parts_ref[part]
-        out_ref[part * 12 : (part + 1) * 12, :] = rows
-        total += jnp.sum(jnp.abs(rows.astype(jnp.float32)), axis=0, keepdims=True)
-    sums_ref[...] = total
+def pack_tokens(tokens_ref, out_ref):
+    out_ref[:12, :] = tokens_ref[:, : BLOCK // 2]
+    out_ref[12:, :] = tokens_ref[:, BLOCK // 2 :]
+
+
+def join_tokens(*refs):
+    *parts, out_ref, sums_ref = refs
+    for half in range(2):
+        total = jnp.zeros((1, BLOCK // 2), jnp.float32)
+        lanes = slice(half * BLOCK // 2, (half + 1) * BLOCK // 2)
+        for at, part in enumerate(parts):
+            rows = part[half * 12 : (half + 1) * 12, :]
+            out_ref[at * 12 : (at + 1) * 12, lanes] = rows
+            total += jnp.sum(jnp.abs(rows.astype(jnp.float32)), axis=0, keepdims=True)
+        sums_ref[:, lanes] = total
 
 
 def mean_kernel(core_0, core_1, mean_ref):
@@ -109,9 +117,12 @@
                 tokens[at * 96 : (at + 1) * 96, :] = part[...]
         else:
             tokens, out_refs, deltas = refs[0], refs[1:5], refs[5:]
-        for unit in range(units):
-            delta = deltas[unit % 2]
-            quantize(columns_ref, pl.ds((first + unit) * UNIT, UNIT), scale_ref, inverse_ref, delta)
+
+        def compute(unit, delta):
+            row = (first + unit) * UNIT
+            if not isinstance(unit, int):
+                row = pl.multiple_of(row, UNIT)
+            quantize(columns_ref, pl.ds(row, UNIT), scale_ref, inverse_ref, delta)
             out = lax.dot_general(
                 delta[...], tokens[...], (((1,), (1,)), ((), ())), preferred_element_type=jnp.float32
             ).astype(jnp.bfloat16)
@@ -119,6 +130,19 @@
                 for hops in range(NX):
                     at = k * UNIT + hops * ROWS
                     out_refs[hops][unit, k] = out[at : at + ROWS, :]
+
+        def pair(at, carry):
+            compute(2 * at, deltas[0])
+            compute(2 * at + 1, deltas[1])
+            return carry
+
+        if units > 3:
+            lax.fori_loop(0, units // 2, pair, 0)
+            rest = range(units // 2 * 2, units)
+        else:
+            rest = range(units)
+        for unit in rest:
+            compute(unit, deltas[unit % 2])
 
     return body
 
@@ -163,6 +187,12 @@
     return lax.ppermute(value, axis, [(i, (i + hops) % size) for i in range(size)])
 
 
+def turned(value, hops):
+    where = [(x, z, y) for x in range(NX) for z in range(NZ) for y in range(NY)]
+    pairs = [((x * NZ + z) * NY + y, (y * NZ + (z + hops) % NZ) * NY + x) for x, z, y in where]
+    return lax.ppermute(value, ("dp_0", "dp_1", "tensor"), pairs)
+
+
 def after(value, *others):
     return lax.optimization_barrier((value, *others))[0]
 
@@ -170,16 +200,14 @@
 def search(activations, weight):
     array = jax.ShapeDtypeStruct
     f32, bf16 = jnp.float32, jnp.bfloat16
-    turn = [(x * NY + y, y * NY + x) for x in range(NX) for y in range(NY)]
-    turned = lax.ppermute(activations, ("dp_0", "tensor"), turn)
-    parts = spread(turned, "dp_1", NZ)
+    packed = kernel(pack_tokens, array((24, BLOCK // 2), bf16))(activations)
+    parts = [turned(packed, hops) for hops in (4, 3, 5, 2, 6, 1, 7, 0)]
     columns = kernel(
         split_columns,
         [array((NZ * NC, u * UNIT, GROUP), bf16) for u in SENDS],
         in_specs=[pl.BlockSpec(memory_space=pltpu.SMEM), pl.BlockSpec(memory_space=pltpu.VMEM)],
-    )(lax.axis_index("dp_0").reshape(1), after(weight, turned))
-    parts = after(parts, *columns)
-    joined, sums = kernel(join_tokens, [array((96, BLOCK), bf16), array((1, BLOCK), f32)])(parts)
+    )(lax.axis_index("dp_0").reshape(1), weight)
+    joined, sums = kernel(join_tokens, [array((96, BLOCK), bf16), array((1, BLOCK), f32)])(*parts)
 
     sums = sums.reshape(GROUPS, GROUP)
     around = [shifted(sums, "tensor", hops) for hops in (2, 1, 3)]
@@ -189,8 +217,9 @@
     scale, inverse = kernel(scale_kernel, [array((GRID, GROUPS, GROUP), f32)] * 2)(mean, *around)
 
     received = []
-    for part, gate in zip(columns, ([joined], [scale])):
-        part = after(part, *gate, *received)
+    for at, part in enumerate(columns):
+        if at:
+            part = after(part, scale, *received)
         received.append(lax.all_to_all(part, ZC, 0, 0, tiled=True))
 
     tokens = [joined] + [shifted(joined, "tensor", hops) for hops in (2, 1, 3)]
@@ -214,9 +243,9 @@
             tokens = partial[NX:]
         shares += [partial[0]] + [shifted(partial[hops], "dp_0", hops) for hops in (2, 1, 3)]
     sums, totals = kernel(error_kernel, [array((GRID, UNITS * ROWS), f32), array((1, GRID), f32)])(*shares)
-    totals = jnp.sum(spread(totals, ("dp_0", "tensor"), NX * NY), axis=0)
+    totals = totals + shifted(totals, "dp_2", 1)
     own_mean = lax.dynamic_slice_in_dim(after(mean, sums).reshape(-1), lax.axis_index(ZC) * GROUP, GROUP)
-    errors = jnp.sum(spread(totals, ZC, NZ * NC), axis=0).reshape(GRID) / (TOKENS * F)
+    errors = jnp.sum(spread(totals, ("dp_0", "dp_1", "tensor"), NX * NZ * NY), axis=0).reshape(GRID) / (TOKENS * F)
     column_errors = after(sums, totals) / TOKENS
     return (own_mean, column_errors, errors)
 

time: 169 us -> 186 us (1.10)
  starting transfers between devices: 66.1 us -> 79.5 us
  waiting for transfers between devices: 68.8 us -> 74.8 us
    ppermute x1 -> x8, starting transfers between devices: 3.46 us -> 26.1 us  [turned(): return lax.ppermute(value, ('dp_0', 'dp_1', 'tensor'), pairs)]
    all_to_all x3 -> x1, waiting for transfers between devices: 25.6 us -> 10.3 us  [spread(): return lax.all_to_all(wide, axes, 0, 0, tiled=True)]
    ppermute x1 -> x8, waiting for transfers between devices: 3.8 us -> 18.9 us  [turned(): return lax.ppermute(value, ('dp_0', 'dp_1', 'tensor'), pairs)]
    all_to_all x3 -> x1, starting transfers between devices: 20 us -> 10.7 us  [spread(): return lax.all_to_all(wide, axes, 0, 0, tiled=True)]
    ppermute x23 -> x21, waiting for transfers between devices: 38.9 us -> 45.5 us  [shifted(): lax.ppermute(value, axis, [(i, (i + hops) % size) for i in range(size)])]
    all_to_all x2, starting transfers between devices: 10.2 us -> 13.4 us  [search(): received.append(lax.all_to_all(part, ZC, 0, 0, tiled=True))]
    ppermute x23 -> x21, starting transfers between devices: 32.5 us -> 29.3 us  [shifted(): lax.ppermute(value, axis, [(i, (i + hops) % size) for i in range(size)])]
    pallas_call x3 -> x2, Pallas kernels: 19.6 us -> 19.4 us  [search(): kernel(piece_kernel(first, units, gathers), out_shape, limit=14, flops=3...]
  transfers between devices with their start and end apart: 29 -> 32, of which waited for: 19 -> 18; matrix products, arithmetic and copies ran while one was open for 1% -> 1% of each run, Pallas kernels for 13% -> 11%
where the time goes in v3:
time: 186 us; the launch traced here: 185 us
  starting transfers between devices  79.5 us (43%)
  waiting for transfers between devices  74.8 us (40%)
  Pallas kernels  22.4 us (12%)
  local copies, waits for them, and re-layouts  6.28 us (3%)
    ppermute x21, waiting for transfers between devices, shifted(): lax.ppermute(value, axis, [(i, (i + hops) % size) for i in range(size)])  45.5 us
    ppermute x21, starting transfers between devices, shifted(): lax.ppermute(value, axis, [(i, (i + hops) % size) for i in range(size)])  29.3 us
    ppermute x8, starting transfers between devices, turned(): return lax.ppermute(value, ('dp_0', 'dp_1', 'tensor'), pairs)  26.1 us
    pallas_call x2, Pallas kernels, search(): kernel(piece_kernel(first, units, gathers), out_shape, limit=14, flops=3...  19.4 us
    ppermute x8, waiting for transfers between devices, turned(): return lax.ppermute(value, ('dp_0', 'dp_1', 'tensor'), pairs)  18.9 us
    all_to_all x2, starting transfers between devices, search(): received.append(lax.all_to_all(part, ZC, 0, 0, tiled=True))  13.4 us
    all_to_all x1, starting transfers between devices, spread(): return lax.all_to_all(wide, axes, 0, 0, tiled=True)  10.7 us
    all_to_all x1, waiting for transfers between devices, spread(): return lax.all_to_all(wide, axes, 0, 0, tiled=True)  10.3 us
  transfers between devices with their start and end apart: 32, of which 18 were waited for; matrix products, arithmetic and copies ran while one was open for 1% of the time, Pallas kernels for 11%

profile of v3, /device:TPU:2, one launch (start us, length us, event | category | flops | bytes accessed | tf_op | source)
XLA Modules:
  0.0 185.0 jit_solution(9570549380095599000)
XLA Ops:
  0.6 1.5 copy-done
  2.1 1.8 shard_map.52
  4.0 8.6 %all-to-all-start = ((bf16[16,256,128]{2,1,0:T(8,128)(2,1)}), bf16[16,256,128]{2,1,0:T(8,128)(2,1)S(1)}, u32[]{:S(2)}, u32[]{:S(2)}) async-start(bf16[16,256,128]{2,1,0:T(8,128)(2,1)} %get-tuple-element.25), calls=%async_computation | async-start | bytes 2097152 | tf_op jit(solution)/shard_map/all_to_all | solution.py:223
  12.6 3.5 %collective-permute-start.7 = (bf16[24,1024]{1,0:T(8,128)(2,1)S(1)}, bf16[24,1024]{1,0:T(8,128)(2,1)S(1)}, u32[]{:S(2)}, u32[]{:S(2)}) collective-permute-start(bf16[24,1024]{1,0:T(8,128)(2,1)S(1)} %shard_map.49), channel_id=1, source_target_pairs={{0,0},{1,64},{2,128},{3,192},{8,8},{9,72},{10,136},{11,200},{16,16... | collective-permute-start | bytes 147464 | tf_op jit(solution)/shard_map/ppermute | solution.py:193
  16.0 4.0 %collective-permute-start.6 = (bf16[24,1024]{1,0:T(8,128)(2,1)S(1)}, bf16[24,1024]{1,0:T(8,128)(2,1)S(1)}, u32[]{:S(2)}, u32[]{:S(2)}) collective-permute-start(bf16[24,1024]{1,0:T(8,128)(2,1)S(1)} %shard_map.49), channel_id=1, source_target_pairs={{0,56},{1,120},{2,184},{3,248},{8,0},{9,64},{10,128},{11,192},{16,... | collective-permute-start | bytes 147464 | tf_op jit(solution)/shard_map/ppermute | solution.py:193
  20.1 4.7 %collective-permute-start.4 = (bf16[24,1024]{1,0:T(8,128)(2,1)S(1)}, bf16[24,1024]{1,0:T(8,128)(2,1)S(1)}, u32[]{:S(2)}, u32[]{:S(2)}) collective-permute-start(bf16[24,1024]{1,0:T(8,128)(2,1)S(1)} %shard_map.49), channel_id=1, source_target_pairs={{0,48},{1,112},{2,176},{3,240},{8,56},{9,120},{10,184},{11,248},{1... | collective-permute-start | bytes 147464 | tf_op jit(solution)/shard_map/ppermute | solution.py:193
  24.8 5.6 %collective-permute-start.2 = (bf16[24,1024]{1,0:T(8,128)(2,1)S(1)}, bf16[24,1024]{1,0:T(8,128)(2,1)S(1)}, u32[]{:S(2)}, u32[]{:S(2)}) collective-permute-start(bf16[24,1024]{1,0:T(8,128)(2,1)S(1)} %shard_map.49), channel_id=1, source_target_pairs={{0,40},{1,104},{2,168},{3,232},{8,48},{9,112},{10,176},{11,240},{1... | collective-permute-start | bytes 147464 | tf_op jit(solution)/shard_map/ppermute | solution.py:193
  30.4 11.0 %collective-permute-done.6.refs_6_ = bf16[24,1024]{1,0:T(8,128)(2,1)S(1)} collective-permute-done((bf16[24,1024]{1,0:T(8,128)(2,1)S(1)}, bf16[24,1024]{1,0:T(8,128)(2,1)S(1)}, u32[]{:S(2)}, u32[]{:S(2)}) %collective-permute-start.6) | collective-permute-done | bytes 49184 | tf_op jit(solution)/shard_map/ppermute | solution.py:193
  41.4 6.1 %collective-permute-start.1 = (bf16[24,1024]{1,0:T(8,128)(2,1)S(1)}, bf16[24,1024]{1,0:T(8,128)(2,1)S(1)}, u32[]{:S(2)}, u32[]{:S(2)}) collective-permute-start(bf16[24,1024]{1,0:T(8,128)(2,1)S(1)} %shard_map.49), channel_id=1, source_target_pairs={{0,24},{1,88},{2,152},{3,216},{8,32},{9,96},{10,160},{11,224},{16,... | collective-permute-start | bytes 147464 | tf_op jit(solution)/shard_map/ppermute | solution.py:193
  47.5 2.2 %collective-permute-start = (bf16[24,1024]{1,0:T(8,128)(2,1)S(1)}, bf16[24,1024]{1,0:T(8,128)(2,1)S(1)}, u32[]{:S(2)}, u32[]{:S(2)}) collective-permute-start(bf16[24,1024]{1,0:T(8,128)(2,1)S(1)} %shard_map.49), channel_id=1, source_target_pairs={{0,32},{1,96},{2,160},{3,224},{8,40},{9,104},{10,168},{11,232},{16... | collective-permute-start | bytes 147464 | tf_op jit(solution)/shard_map/ppermute | solution.py:193
  49.7 1.2 collective-permute-done.1.refs_1_
  50.9 6.7 %collective-permute-done.refs_0_ = bf16[24,1024]{1,0:T(8,128)(2,1)S(1)} collective-permute-done((bf16[24,1024]{1,0:T(8,128)(2,1)S(1)}, bf16[24,1024]{1,0:T(8,128)(2,1)S(1)}, u32[]{:S(2)}, u32[]{:S(2)}) %collective-permute-start) | collective-permute-done | bytes 49184 | tf_op jit(solution)/shard_map/ppermute | solution.py:193
  57.9 10.6 %collective-permute-start.10 = (f32[16,128]{1,0:T(8,128)S(1)}, f32[16,128]{1,0:T(8,128)S(1)}, u32[]{:S(2)}, u32[]{:S(2)}) collective-permute-start(f32[16,128]{1,0:T(8,128)S(1)} %bitcast.5), channel_id=1, source_target_pairs={{0,3},{1,0},{2,1},{3,2},{4,7},{5,4},{6,5},{7,6},{8,11},{9,8},{10,9... | collective-permute-start | bytes 24584 | tf_op jit(solution)/shard_map/ppermute | solution.py:187
  68.5 1.6 collective-permute-start.8
  70.0 3.3 %collective-permute-done.9 = f32[16,128]{1,0:T(8,128)S(1)} collective-permute-done((f32[16,128]{1,0:T(8,128)S(1)}, f32[16,128]{1,0:T(8,128)S(1)}, u32[]{:S(2)}, u32[]{:S(2)}) %collective-permute-start.9) | collective-permute-done | bytes 8224 | tf_op jit(solution)/shard_map/ppermute | solution.py:187
  73.6 1.2 collective-permute-done.11.core_1
  74.8 2.0 %collective-permute-start.13 = (f32[16,128]{1,0:T(8,128)S(1)}, f32[16,128]{1,0:T(8,128)S(1)}, u32[]{:S(2)}, u32[]{:S(2)}) collective-permute-start(f32[16,128]{1,0:T(8,128)S(1)} %shard_map.51.mean_0), channel_id=1, source_target_pairs={{0,64},{64,128},{128,192},{192,0},{1,65},{65,129},{129,193},{193,1... | collective-permute-start | bytes 24584 | tf_op jit(solution)/shard_map/ppermute | solution.py:187
  76.8 1.9 %collective-permute-start.12 = (f32[16,128]{1,0:T(8,128)S(1)}, f32[16,128]{1,0:T(8,128)S(1)}, u32[]{:S(2)}, u32[]{:S(2)}) collective-permute-start(f32[16,128]{1,0:T(8,128)S(1)} %shard_map.51.mean_0), channel_id=1, source_target_pairs={{0,128},{64,192},{128,0},{192,64},{1,129},{65,193},{129,1},{193,65... | collective-permute-start | bytes 24584 | tf_op jit(solution)/shard_map/ppermute | solution.py:187
  78.7 3.3 %collective-permute-done.12.mean_1 = f32[16,128]{1,0:T(8,128)S(1)} collective-permute-done((f32[16,128]{1,0:T(8,128)S(1)}, f32[16,128]{1,0:T(8,128)S(1)}, u32[]{:S(2)}, u32[]{:S(2)}) %collective-permute-start.12) | collective-permute-done | bytes 8224 | tf_op jit(solution)/shard_map/ppermute | solution.py:187
  82.3 4.9 %all-to-all-start.1 = ((bf16[16,192,128]{2,1,0:T(8,128)(2,1)}), bf16[16,192,128]{2,1,0:T(8,128)(2,1)S(1)}, u32[]{:S(2)}, u32[]{:S(2)}) async-start(bf16[16,192,128]{2,1,0:T(8,128)(2,1)} %get-tuple-element.34), calls=%async_computation.1 | async-start | bytes 1572864 | tf_op jit(solution)/shard_map/all_to_all | solution.py:223
  87.2 3.5 %collective-permute-start.17 = (bf16[96,2048]{1,0:T(8,128)(2,1)S(1)}, bf16[96,2048]{1,0:T(8,128)(2,1)S(1)}, u32[]{:S(2)}, u32[]{:S(2)}) collective-permute-start(bf16[96,2048]{1,0:T(8,128)(2,1)S(1)} %get-tuple-element.28.refs_0_), channel_id=1, source_target_pairs={{0,3},{1,0},{2,1},{3,2},{4,7},{5,4},{6,5},{7,6},{8,11},{9,8},{10,9... | collective-permute-start | bytes 1179656 | tf_op jit(solution)/shard_map/ppermute | solution.py:187
  90.7 1.6 collective-permute-start.15
  92.3 15.6 %collective-permute-done.17.refs_3_ = bf16[96,2048]{1,0:T(8,128)(2,1)S(1)} collective-permute-done((bf16[96,2048]{1,0:T(8,128)(2,1)S(1)}, bf16[96,2048]{1,0:T(8,128)(2,1)S(1)}, u32[]{:S(2)}, u32[]{:S(2)}) %collective-permute-start.17) | collective-permute-done | bytes 393248 | tf_op jit(solution)/shard_map/ppermute | solution.py:187
  107.8 3.4 %collective-permute-done.16.refs_2_ = bf16[96,2048]{1,0:T(8,128)(2,1)S(1)} collective-permute-done((bf16[96,2048]{1,0:T(8,128)(2,1)S(1)}, bf16[96,2048]{1,0:T(8,128)(2,1)S(1)}, u32[]{:S(2)}, u32[]{:S(2)}) %collective-permute-start.16) | collective-permute-done | bytes 393248 | tf_op jit(solution)/shard_map/ppermute | solution.py:187
  111.8 1.2 collective-permute-done.20.refs_6_
  113.0 0.6 collective-permute-done.19.refs_5_
  113.5 11.1 %shard_map.54 = (bf16[4,4,16,768]{3,2,1,0:T(8,128)(2,1)S(1)}, bf16[4,4,16,768]{3,2,1,0:T(8,128)(2,1)}, bf16[4,4,16,768]{3,2,1,0:T(8,128)(2,1)}, bf16[4,4,16,768]{3,2,1,0:T(8,128)(2,1)S(1)}, bf16[768,2048]{1,0:T(8,128)(2,1)S(1)}) custom-call(bf16[16,256,128]{2,1,0:T(8,128)(2,1)S(1)} %all-to-all-done.columns_ref, ...), custom_call_target="tpu_custom_call" | custom-call | flops 4831838208 | tf_op jit(solution)/shard_map/pallas_call | solution.py:235
  124.7 1.6 copy-done.2
  126.3 1.5 collective-permute-start.23
  127.8 0.5 collective-permute-start.24
  128.4 1.9 %copy-done.3 = bf16[768,2048]{1,0:T(8,128)(2,1)S(1)} copy-done((bf16[768,2048]{1,0:T(8,128)(2,1)S(1)}, bf16[768,2048]{1,0:T(8,128)(2,1)}, u32[]{:S(2)}) %copy-start.3) | copy-done | bytes 3145752
  130.3 8.3 %shard_map.55 = (bf16[3,4,16,768]{3,2,1,0:T(8,128)(2,1)S(1)}, bf16[3,4,16,768]{3,2,1,0:T(8,128)(2,1)}, bf16[3,4,16,768]{3,2,1,0:T(8,128)(2,1)}, bf16[3,4,16,768]{3,2,1,0:T(8,128)(2,1)}) custom-call(bf16[16,192,128]{2,1,0:T(8,128)(2,1)S(1)} %all-to-all-done.1.columns_ref, f32[4,16,128]{2,1,0:T(8,128)S(1)} %get-tuple-element.26.scale_ref, ...), custom_call_target="tpu_custom_call" | custom-call | flops 3623878656 | tf_op jit(solution)/shard_map/pallas_call | solution.py:235
  138.5 3.5 %collective-permute-start.25 = (bf16[3,4,16,768]{3,2,1,0:T(8,128)(2,1)}, bf16[3,4,16,768]{3,2,1,0:T(8,128)(2,1)S(1)}, u32[]{:S(2)}, u32[]{:S(2)}) collective-permute-start(bf16[3,4,16,768]{3,2,1,0:T(8,128)(2,1)} %get-tuple-element.38), channel_id=1, source_target_pairs={{0,128},{64,192},{128,0},{192,64},{1,129},{65,193},{129,1},{193,65... | collective-permute-start | bytes 884744 | tf_op jit(solution)/shard_map/ppermute | solution.py:187
  142.0 1.2 collective-permute-start.26
  143.2 0.8 collective-permute-start.27
  144.0 3.0 %collective-permute-done.23.refs_2_ = bf16[4,4,16,768]{3,2,1,0:T(8,128)(2,1)S(1)} collective-permute-done((bf16[4,4,16,768]{3,2,1,0:T(8,128)(2,1)}, bf16[4,4,16,768]{3,2,1,0:T(8,128)(2,1)S(1)}, u32[]{:S(2)}, u32[]{:S(2)}) %collective-permute-start.23) | collective-permute-done | bytes 393248 | tf_op jit(solution)/shard_map/ppermute | solution.py:187
  147.0 1.5 collective-permute-done.24.refs_3_
  148.5 6.3 %collective-permute-done.25.refs_5_ = bf16[3,4,16,768]{3,2,1,0:T(8,128)(2,1)S(1)} collective-permute-done((bf16[3,4,16,768]{3,2,1,0:T(8,128)(2,1)}, bf16[3,4,16,768]{3,2,1,0:T(8,128)(2,1)S(1)}, u32[]{:S(2)}, u32[]{:S(2)}) %collective-permute-start.25) | collective-permute-done | bytes 294944 | tf_op jit(solution)/shard_map/ppermute | solution.py:187
  154.8 4.0 %collective-permute-done.26.refs_6_ = bf16[3,4,16,768]{3,2,1,0:T(8,128)(2,1)S(1)} collective-permute-done((bf16[3,4,16,768]{3,2,1,0:T(8,128)(2,1)}, bf16[3,4,16,768]{3,2,1,0:T(8,128)(2,1)S(1)}, u32[]{:S(2)}, u32[]{:S(2)}) %collective-permute-start.26) | collective-permute-done | bytes 294944 | tf_op jit(solution)/shard_map/ppermute | solution.py:187
  158.9 1.4 collective-permute-done.27.refs_7_
  160.2 0.6 shard_map.56
  160.9 0.6 dynamic_slice.3
  161.5 0.6 collective-permute-done.28
  162.0 0.7 broadcast_in_dim.9
  162.7 10.7 %all-to-all-start.2 = ((f32[128,1,4]{2,1,0:T(1,128)}), f32[128,1,4]{2,1,0:T(1,128)S(1)}, u32[]{:S(2)}, u32[]{:S(2)}) async-start(f32[128,1,4]{2,1,0:T(1,128)} %broadcast_in_dim.9), calls=%async_computation.2 | async-start | bytes 131072 | tf_op jit(solution)/shard_map/all_to_all | solution.py:182
  173.4 0.6 broadcast_multiply_fusion
  174.0 10.3 %all-to-all-done.2 = f32[128,1,4]{2,1,0:T(1,128)S(1)} async-done(((f32[128,1,4]{2,1,0:T(1,128)}), f32[128,1,4]{2,1,0:T(1,128)S(1)}, u32[]{:S(2)}, u32[]{:S(2)}) %all-to-all-start.2) | async-done | bytes 2080 | tf_op jit(solution)/shard_map/all_to_all | solution.py:182
  184.5 0.5 broadcast_multiply_fusion.1
  (39 shorter events, 1.7 us)
Async XLA Ops:
  0.6 1.5 copy-start
  2.1 10.4 %copy-start.1 = (bf16[12,2048]{1,0:T(8,128)(2,1)S(1)}, bf16[12,2048]{1,0:T(8,128)(2,1)}, u32[]{:S(2)}) copy-start(bf16[12,2048]{1,0:T(8,128)(2,1)} %tokens_ref.1) | copy-start | bytes 147460
  4.0 78.4 %all-to-all-start = ((bf16[16,256,128]{2,1,0:T(8,128)(2,1)}), bf16[16,256,128]{2,1,0:T(8,128)(2,1)S(1)}, u32[]{:S(2)}, u32[]{:S(2)}) async-start(bf16[16,256,128]{2,1,0:T(8,128)(2,1)} %get-tuple-element.25), calls=%async_computation | async-start | bytes 2097152 | tf_op jit(solution)/shard_map/all_to_all | solution.py:223
  12.6 12.2 %collective-permute-start.7 = (bf16[24,1024]{1,0:T(8,128)(2,1)S(1)}, bf16[24,1024]{1,0:T(8,128)(2,1)S(1)}, u32[]{:S(2)}, u32[]{:S(2)}) collective-permute-start(bf16[24,1024]{1,0:T(8,128)(2,1)S(1)} %shard_map.49), channel_id=1, source_target_pairs={{0,0},{1,64},{2,128},{3,192},{8,8},{9,72},{10,136},{11,200},{16,16... | collective-permute-start | bytes 147464 | tf_op jit(solution)/shard_map/ppermute | solution.py:193
  16.0 25.4 %collective-permute-start.6 = (bf16[24,1024]{1,0:T(8,128)(2,1)S(1)}, bf16[24,1024]{1,0:T(8,128)(2,1)S(1)}, u32[]{:S(2)}, u32[]{:S(2)}) collective-permute-start(bf16[24,1024]{1,0:T(8,128)(2,1)S(1)} %shard_map.49), channel_id=1, source_target_pairs={{0,56},{1,120},{2,184},{3,248},{8,0},{9,64},{10,128},{11,192},{16,... | collective-permute-start | bytes 147464 | tf_op jit(solution)/shard_map/ppermute | solution.py:193
  20.1 27.5 %collective-permute-start.5 = (bf16[24,1024]{1,0:T(8,128)(2,1)S(1)}, bf16[24,1024]{1,0:T(8,128)(2,1)S(1)}, u32[]{:S(2)}, u32[]{:S(2)}) collective-permute-start(bf16[24,1024]{1,0:T(8,128)(2,1)S(1)} %shard_map.49), channel_id=1, source_target_pairs={{0,8},{1,72},{2,136},{3,200},{8,16},{9,80},{10,144},{11,208},{16,2... | collective-permute-start | bytes 147464 | tf_op jit(solution)/shard_map/ppermute | solution.py:193
  20.1 29.6 %collective-permute-start.4 = (bf16[24,1024]{1,0:T(8,128)(2,1)S(1)}, bf16[24,1024]{1,0:T(8,128)(2,1)S(1)}, u32[]{:S(2)}, u32[]{:S(2)}) collective-permute-start(bf16[24,1024]{1,0:T(8,128)(2,1)S(1)} %shard_map.49), channel_id=1, source_target_pairs={{0,48},{1,112},{2,176},{3,240},{8,56},{9,120},{10,184},{11,248},{1... | collective-permute-start | bytes 147464 | tf_op jit(solution)/shard_map/ppermute | solution.py:193
  24.8 24.9 %collective-permute-start.3 = (bf16[24,1024]{1,0:T(8,128)(2,1)S(1)}, bf16[24,1024]{1,0:T(8,128)(2,1)S(1)}, u32[]{:S(2)}, u32[]{:S(2)}) collective-permute-start(bf16[24,1024]{1,0:T(8,128)(2,1)S(1)} %shard_map.49), channel_id=1, source_target_pairs={{0,16},{1,80},{2,144},{3,208},{8,24},{9,88},{10,152},{11,216},{16,... | collective-permute-start | bytes 147464 | tf_op jit(solution)/shard_map/ppermute | solution.py:193
  24.8 24.9 %collective-permute-start.2 = (bf16[24,1024]{1,0:T(8,128)(2,1)S(1)}, bf16[24,1024]{1,0:T(8,128)(2,1)S(1)}, u32[]{:S(2)}, u32[]{:S(2)}) collective-permute-start(bf16[24,1024]{1,0:T(8,128)(2,1)S(1)} %shard_map.49), channel_id=1, source_target_pairs={{0,40},{1,104},{2,168},{3,232},{8,48},{9,112},{10,176},{11,240},{1... | collective-permute-start | bytes 147464 | tf_op jit(solution)/shard_map/ppermute | solution.py:193
  41.4 9.5 %collective-permute-start.1 = (bf16[24,1024]{1,0:T(8,128)(2,1)S(1)}, bf16[24,1024]{1,0:T(8,128)(2,1)S(1)}, u32[]{:S(2)}, u32[]{:S(2)}) collective-permute-start(bf16[24,1024]{1,0:T(8,128)(2,1)S(1)} %shard_map.49), channel_id=1, source_target_pairs={{0,24},{1,88},{2,152},{3,216},{8,32},{9,96},{10,160},{11,224},{16,... | collective-permute-start | bytes 147464 | tf_op jit(solution)/shard_map/ppermute | solution.py:193
  47.5 10.1 %collective-permute-start = (bf16[24,1024]{1,0:T(8,128)(2,1)S(1)}, bf16[24,1024]{1,0:T(8,128)(2,1)S(1)}, u32[]{:S(2)}, u32[]{:S(2)}) collective-permute-start(bf16[24,1024]{1,0:T(8,128)(2,1)S(1)} %shard_map.49), channel_id=1, source_target_pairs={{0,32},{1,96},{2,160},{3,224},{8,40},{9,104},{10,168},{11,232},{16... | collective-permute-start | bytes 147464 | tf_op jit(solution)/shard_map/ppermute | solution.py:193
  57.9 12.2 %collective-permute-start.10 = (f32[16,128]{1,0:T(8,128)S(1)}, f32[16,128]{1,0:T(8,128)S(1)}, u32[]{:S(2)}, u32[]{:S(2)}) collective-permute-start(f32[16,128]{1,0:T(8,128)S(1)} %bitcast.5), channel_id=1, source_target_pairs={{0,3},{1,0},{2,1},{3,2},{4,7},{5,4},{6,5},{7,6},{8,11},{9,8},{10,9... | collective-permute-start | bytes 24584 | tf_op jit(solution)/shard_map/ppermute | solution.py:187
  68.5 4.9 %collective-permute-start.9 = (f32[16,128]{1,0:T(8,128)S(1)}, f32[16,128]{1,0:T(8,128)S(1)}, u32[]{:S(2)}, u32[]{:S(2)}) collective-permute-start(f32[16,128]{1,0:T(8,128)S(1)} %bitcast.6), channel_id=1, source_target_pairs={{0,1},{1,2},{2,3},{3,0},{4,5},{5,6},{6,7},{7,4},{8,9},{9,10},{10,1... | collective-permute-start | bytes 24584 | tf_op jit(solution)/shard_map/ppermute | solution.py:187
  68.5 5.2 %collective-permute-start.8 = (f32[16,128]{1,0:T(8,128)S(1)}, f32[16,128]{1,0:T(8,128)S(1)}, u32[]{:S(2)}, u32[]{:S(2)}) collective-permute-start(f32[16,128]{1,0:T(8,128)S(1)} %bitcast.7), channel_id=1, source_target_pairs={{0,2},{1,3},{2,0},{3,1},{4,6},{5,7},{6,4},{7,5},{8,10},{9,11},{10,... | collective-permute-start | bytes 24584 | tf_op jit(solution)/shard_map/ppermute | solution.py:187
  73.6 1.2 collective-permute-start.11
  74.8 3.9 %collective-permute-start.14 = (f32[16,128]{1,0:T(8,128)S(1)}, f32[16,128]{1,0:T(8,128)S(1)}, u32[]{:S(2)}, u32[]{:S(2)}) collective-permute-start(f32[16,128]{1,0:T(8,128)S(1)} %shard_map.51.mean_0), channel_id=1, source_target_pairs={{0,192},{64,0},{128,64},{192,128},{1,193},{65,1},{129,65},{193,129... | collective-permute-start | bytes 24584 | tf_op jit(solution)/shard_map/ppermute | solution.py:187
  74.8 3.9 %collective-permute-start.13 = (f32[16,128]{1,0:T(8,128)S(1)}, f32[16,128]{1,0:T(8,128)S(1)}, u32[]{:S(2)}, u32[]{:S(2)}) collective-permute-start(f32[16,128]{1,0:T(8,128)S(1)} %shard_map.51.mean_0), channel_id=1, source_target_pairs={{0,64},{64,128},{128,192},{192,0},{1,65},{65,129},{129,193},{193,1... | collective-permute-start | bytes 24584 | tf_op jit(solution)/shard_map/ppermute | solution.py:187
  76.8 5.2 %collective-permute-start.12 = (f32[16,128]{1,0:T(8,128)S(1)}, f32[16,128]{1,0:T(8,128)S(1)}, u32[]{:S(2)}, u32[]{:S(2)}) collective-permute-start(f32[16,128]{1,0:T(8,128)S(1)} %shard_map.51.mean_0), channel_id=1, source_target_pairs={{0,128},{64,192},{128,0},{192,64},{1,129},{65,193},{129,1},{193,65... | collective-permute-start | bytes 24584 | tf_op jit(solution)/shard_map/ppermute | solution.py:187
  82.3 46.0 %all-to-all-start.1 = ((bf16[16,192,128]{2,1,0:T(8,128)(2,1)}), bf16[16,192,128]{2,1,0:T(8,128)(2,1)S(1)}, u32[]{:S(2)}, u32[]{:S(2)}) async-start(bf16[16,192,128]{2,1,0:T(8,128)(2,1)} %get-tuple-element.34), calls=%async_computation.1 | async-start | bytes 1572864 | tf_op jit(solution)/shard_map/all_to_all | solution.py:223
  87.2 20.6 %collective-permute-start.17 = (bf16[96,2048]{1,0:T(8,128)(2,1)S(1)}, bf16[96,2048]{1,0:T(8,128)(2,1)S(1)}, u32[]{:S(2)}, u32[]{:S(2)}) collective-permute-start(bf16[96,2048]{1,0:T(8,128)(2,1)S(1)} %get-tuple-element.28.refs_0_), channel_id=1, source_target_pairs={{0,3},{1,0},{2,1},{3,2},{4,7},{5,4},{6,5},{7,6},{8,11},{9,8},{10,9... | collective-permute-start | bytes 1179656 | tf_op jit(solution)/shard_map/ppermute | solution.py:187
  90.7 20.5 %collective-permute-start.16 = (bf16[96,2048]{1,0:T(8,128)(2,1)S(1)}, bf16[96,2048]{1,0:T(8,128)(2,1)S(1)}, u32[]{:S(2)}, u32[]{:S(2)}) collective-permute-start(bf16[96,2048]{1,0:T(8,128)(2,1)S(1)} %get-tuple-element.28.refs_0_), channel_id=1, source_target_pairs={{0,1},{1,2},{2,3},{3,0},{4,5},{5,6},{6,7},{7,4},{8,9},{9,10},{10,1... | collective-permute-start | bytes 1179656 | tf_op jit(solution)/shard_map/ppermute | solution.py:187
  90.7 20.5 %collective-permute-start.15 = (bf16[96,2048]{1,0:T(8,128)(2,1)S(1)}, bf16[96,2048]{1,0:T(8,128)(2,1)S(1)}, u32[]{:S(2)}, u32[]{:S(2)}) collective-permute-start(bf16[96,2048]{1,0:T(8,128)(2,1)S(1)} %get-tuple-element.28.refs_0_), channel_id=1, source_target_pairs={{0,2},{1,3},{2,0},{3,1},{4,6},{5,7},{6,4},{7,5},{8,10},{9,11},{10,... | collective-permute-start | bytes 1179656 | tf_op jit(solution)/shard_map/ppermute | solution.py:187
  92.3 19.5 %collective-permute-start.18 = (bf16[96,2048]{1,0:T(8,128)(2,1)S(1)}, bf16[96,2048]{1,0:T(8,128)(2,1)S(1)}, u32[]{:S(2)}, u32[]{:S(2)}) collective-permute-start(bf16[96,2048]{1,0:T(8,128)(2,1)S(1)} %get-tuple-element.28.refs_0_), channel_id=1, source_target_pairs={{0,4},{4,0},{1,5},{5,1},{2,6},{6,2},{3,7},{7,3},{8,12},{12,8},{9,1... | collective-permute-start | bytes 1179656 | tf_op jit(solution)/shard_map/ppermute | solution.py:187
  107.8 3.9 %collective-permute-start.21 = (bf16[96,2048]{1,0:T(8,128)(2,1)S(1)}, bf16[96,2048]{1,0:T(8,128)(2,1)S(1)}, u32[]{:S(2)}, u32[]{:S(2)}) collective-permute-start(bf16[96,2048]{1,0:T(8,128)(2,1)S(1)} %collective-permute-done.17.refs_3_), channel_id=1, source_target_pairs={{0,4},{4,0},{1,5},{5,1},{2,6},{6,2},{3,7},{7,3},{8,12},{12,8},{9,1... | collective-permute-start | bytes 1179656 | tf_op jit(solution)/shard_map/ppermute | solution.py:187
  111.2 1.7 collective-permute-start.20
  111.2 2.3 %collective-permute-start.19 = (bf16[96,2048]{1,0:T(8,128)(2,1)S(1)}, bf16[96,2048]{1,0:T(8,128)(2,1)S(1)}, u32[]{:S(2)}, u32[]{:S(2)}) collective-permute-start(bf16[96,2048]{1,0:T(8,128)(2,1)S(1)} %collective-permute-done.15.refs_1_), channel_id=1, source_target_pairs={{0,4},{4,0},{1,5},{5,1},{2,6},{6,2},{3,7},{7,3},{8,12},{12,8},{9,1... | collective-permute-start | bytes 1179656 | tf_op jit(solution)/shard_map/ppermute | solution.py:187
  124.7 1.6 copy-start.2
  126.3 16.9 %collective-permute-start.22 = (bf16[4,4,16,768]{3,2,1,0:T(8,128)(2,1)}, bf16[4,4,16,768]{3,2,1,0:T(8,128)(2,1)S(1)}, u32[]{:S(2)}, u32[]{:S(2)}) collective-permute-start(bf16[4,4,16,768]{3,2,1,0:T(8,128)(2,1)} %get-tuple-element.30), channel_id=1, source_target_pairs={{0,128},{64,192},{128,0},{192,64},{1,129},{65,193},{129,1},{193,65... | collective-permute-start | bytes 1179656 | tf_op jit(solution)/shard_map/ppermute | solution.py:187
  126.3 20.7 %collective-permute-start.23 = (bf16[4,4,16,768]{3,2,1,0:T(8,128)(2,1)}, bf16[4,4,16,768]{3,2,1,0:T(8,128)(2,1)S(1)}, u32[]{:S(2)}, u32[]{:S(2)}) collective-permute-start(bf16[4,4,16,768]{3,2,1,0:T(8,128)(2,1)} %get-tuple-element.31), channel_id=1, source_target_pairs={{0,64},{64,128},{128,192},{192,0},{1,65},{65,129},{129,193},{193,1... | collective-permute-start | bytes 1179656 | tf_op jit(solution)/shard_map/ppermute | solution.py:187
  127.8 20.7 %collective-permute-start.24 = (bf16[4,4,16,768]{3,2,1,0:T(8,128)(2,1)S(1)}, bf16[4,4,16,768]{3,2,1,0:T(8,128)(2,1)S(1)}, u32[]{:S(2)}, u32[]{:S(2)}) collective-permute-start(bf16[4,4,16,768]{3,2,1,0:T(8,128)(2,1)S(1)} %get-tuple-element.32), channel_id=1, source_target_pairs={{0,192},{64,0},{128,64},{192,128},{1,193},{65,1},{129,65},{193,129... | collective-permute-start | bytes 1179656 | tf_op jit(solution)/shard_map/ppermute | solution.py:187
  128.4 1.9 %copy-start.3 = (bf16[768,2048]{1,0:T(8,128)(2,1)S(1)}, bf16[768,2048]{1,0:T(8,128)(2,1)}, u32[]{:S(2)}) copy-start(bf16[768,2048]{1,0:T(8,128)(2,1)} %copy-done.2) | copy-start | bytes 9437188
  138.5 16.3 %collective-permute-start.25 = (bf16[3,4,16,768]{3,2,1,0:T(8,128)(2,1)}, bf16[3,4,16,768]{3,2,1,0:T(8,128)(2,1)S(1)}, u32[]{:S(2)}, u32[]{:S(2)}) collective-permute-start(bf16[3,4,16,768]{3,2,1,0:T(8,128)(2,1)} %get-tuple-element.38), channel_id=1, source_target_pairs={{0,128},{64,192},{128,0},{192,64},{1,129},{65,193},{129,1},{193,65... | collective-permute-start | bytes 884744 | tf_op jit(solution)/shard_map/ppermute | solution.py:187
  142.0 16.9 %collective-permute-start.26 = (bf16[3,4,16,768]{3,2,1,0:T(8,128)(2,1)}, bf16[3,4,16,768]{3,2,1,0:T(8,128)(2,1)S(1)}, u32[]{:S(2)}, u32[]{:S(2)}) collective-permute-start(bf16[3,4,16,768]{3,2,1,0:T(8,128)(2,1)} %get-tuple-element.39), channel_id=1, source_target_pairs={{0,64},{64,128},{128,192},{192,0},{1,65},{65,129},{129,193},{193,1... | collective-permute-start | bytes 884744 | tf_op jit(solution)/shard_map/ppermute | solution.py:187
  143.2 17.0 %collective-permute-start.27 = (bf16[3,4,16,768]{3,2,1,0:T(8,128)(2,1)}, bf16[3,4,16,768]{3,2,1,0:T(8,128)(2,1)S(1)}, u32[]{:S(2)}, u32[]{:S(2)}) collective-permute-start(bf16[3,4,16,768]{3,2,1,0:T(8,128)(2,1)} %get-tuple-element.40), channel_id=1, source_target_pairs={{0,192},{64,0},{128,64},{192,128},{1,193},{65,1},{129,65},{193,129... | collective-permute-start | bytes 884744 | tf_op jit(solution)/shard_map/ppermute | solution.py:187
  160.8 1.2 collective-permute-start.28
  162.7 21.6 %all-to-all-start.2 = ((f32[128,1,4]{2,1,0:T(1,128)}), f32[128,1,4]{2,1,0:T(1,128)S(1)}, u32[]{:S(2)}, u32[]{:S(2)}) async-start(f32[128,1,4]{2,1,0:T(1,128)} %broadcast_in_dim.9), calls=%async_computation.2 | async-start | bytes 131072 | tf_op jit(solution)/shard_map/all_to_all | solution.py:182

commit v4 on v2

--- a/solution.py
+++ b/solution.py
@@ -57,13 +57,21 @@
                     out[owner, pl.ds(at, ROWS), :] = turned[piece * ROWS : (piece + 1) * ROWS, :]
 
 
+def pack_tokens(tokens_ref, out_ref):
+    for at in range(NZ):
+        out_ref[at, :12, :] = tokens_ref[:, : BLOCK // 2]
+        out_ref[at, 12:, :] = tokens_ref[:, BLOCK // 2 :]
+
+
 def join_tokens(parts_ref, out_ref, sums_ref):
-    total = jnp.zeros((1, BLOCK), jnp.float32)
-    for part in range(NZ):
-        rows = parts_ref[part]
-        out_ref[part * 12 : (part + 1) * 12, :] = rows
-        total += jnp.sum(jnp.abs(rows.astype(jnp.float32)), axis=0, keepdims=True)
-    sums_ref[...] = total
+    for half in range(2):
+        total = jnp.zeros((1, BLOCK // 2), jnp.float32)
+        lanes = slice(half * BLOCK // 2, (half + 1) * BLOCK // 2)
+        for at in range(NZ):
+            rows = parts_ref[at, half * 12 : (half + 1) * 12, :]
+            out_ref[at * 12 : (at + 1) * 12, lanes] = rows
+            total += jnp.sum(jnp.abs(rows.astype(jnp.float32)), axis=0, keepdims=True)
+        sums_ref[:, lanes] = total
 
 
 def mean_kernel(core_0, core_1, mean_ref):
@@ -101,24 +109,42 @@
             delta_ref[k * UNIT : (k + 1) * UNIT, group * GROUP : (group + 1) * GROUP] = dequant - packed
 
 
-def piece_kernel(first, units, gathers):
-    def body(columns_ref, scale_ref, inverse_ref, *refs):
-        if gathers:
-            parts, out_refs, tokens, deltas = refs[:8], refs[8:12], refs[12], refs[13:]
-            for at, part in enumerate(parts):
-                tokens[at * 96 : (at + 1) * 96, :] = part[...]
-        else:
-            tokens, out_refs, deltas = refs[0], refs[1:5], refs[5:]
+def quantize_kernel(columns_ref, scale_ref, inverse_ref, deltas):
+    @pl.loop(0, deltas.shape[0])
+    def _(unit):
+        rows = pl.ds(pl.multiple_of(unit * UNIT, UNIT), UNIT)
+        quantize(columns_ref, rows, scale_ref, inverse_ref, deltas.at[unit])
+
+
+def multiply(delta, tokens, out_refs, unit):
+    out = lax.dot_general(
+        delta[...], tokens[...], (((1,), (1,)), ((), ())), preferred_element_type=jnp.float32
+    ).astype(jnp.bfloat16)
+    for k in range(GRID):
+        for hops in range(NX):
+            at = k * UNIT + hops * ROWS
+            out_refs[hops][unit, k] = out[at : at + ROWS, :]
+
+
+def first_kernel(units):
+    def body(*refs):
+        deltas, parts, out_refs, tokens = refs[0], refs[1:9], refs[9:13], refs[13]
+        for at, part in enumerate(parts):
+            tokens[at * 96 : (at + 1) * 96, :] = part[...]
+        for unit in range(units):
+            multiply(deltas.at[unit], tokens, out_refs, unit)
+
+    return body
+
+
+def piece_kernel(first, units):
+    def body(columns_ref, scale_ref, inverse_ref, tokens, *refs):
+        out_refs, deltas = refs[:NX], refs[NX:]
         for unit in range(units):
             delta = deltas[unit % 2]
-            quantize(columns_ref, pl.ds((first + unit) * UNIT, UNIT), scale_ref, inverse_ref, delta)
-            out = lax.dot_general(
-                delta[...], tokens[...], (((1,), (1,)), ((), ())), preferred_element_type=jnp.float32
-            ).astype(jnp.bfloat16)
-            for k in range(GRID):
-                for hops in range(NX):
-                    at = k * UNIT + hops * ROWS
-                    out_refs[hops][unit, k] = out[at : at + ROWS, :]
+            rows = slice((first + unit) * UNIT, (first + unit + 1) * UNIT)
+            quantize(columns_ref, rows, scale_ref, inverse_ref, delta)
+            multiply(delta, tokens, out_refs, unit)
 
     return body
 
@@ -146,7 +172,7 @@
         total_ref[:, k : k + 1] = jnp.sum(row, axis=1, keepdims=True)
 
 
-def kernel(body, out_shape, limit=8, flops=0, **more):
+def kernel(body, out_shape, limit=14, flops=0, **more):
     params = pltpu.CompilerParams(vmem_limit_bytes=limit * MIB)
     if flops:
         more["cost_estimate"] = pl.CostEstimate(flops=flops, transcendentals=0, bytes_accessed=0)
@@ -163,6 +189,11 @@
     return lax.ppermute(value, axis, [(i, (i + hops) % size) for i in range(size)])
 
 
+def turned(value, hops):
+    pairs = [(x * NY + y, y * NY + (x + hops) % NY) for x in range(NX) for y in range(NY)]
+    return lax.ppermute(value, ("dp_0", "tensor"), pairs)
+
+
 def after(value, *others):
     return lax.optimization_barrier((value, *others))[0]
 
@@ -170,20 +201,19 @@
 def search(activations, weight):
     array = jax.ShapeDtypeStruct
     f32, bf16 = jnp.float32, jnp.bfloat16
-    turn = [(x * NY + y, y * NY + x) for x in range(NX) for y in range(NY)]
-    turned = lax.ppermute(activations, ("dp_0", "tensor"), turn)
-    parts = spread(turned, "dp_1", NZ)
+    packed = kernel(pack_tokens, array((NZ, 24, BLOCK // 2), bf16))(activations)
+    parts = lax.all_to_all(packed, "dp_1", 0, 0, tiled=True)
     columns = kernel(
         split_columns,
         [array((NZ * NC, u * UNIT, GROUP), bf16) for u in SENDS],
         in_specs=[pl.BlockSpec(memory_space=pltpu.SMEM), pl.BlockSpec(memory_space=pltpu.VMEM)],
-    )(lax.axis_index("dp_0").reshape(1), after(weight, turned))
+    )(lax.axis_index("dp_0").reshape(1), after(weight, packed))
     parts = after(parts, *columns)
     joined, sums = kernel(join_tokens, [array((96, BLOCK), bf16), array((1, BLOCK), f32)])(parts)
 
     sums = sums.reshape(GROUPS, GROUP)
-    around = [shifted(sums, "tensor", hops) for hops in (2, 1, 3)]
-    sums = (sums + around[0]) + (around[1] + around[2])
+    around = [turned(sums, hops) for hops in range(NY)]
+    sums = (around[0] + around[2]) + (around[1] + around[3])
     mean = kernel(mean_kernel, array((GROUPS, GROUP), f32))(sums, shifted(sums, "dp_2", 1))
     around = [shifted(mean, "dp_0", hops) for hops in (2, 1, 3)]
     scale, inverse = kernel(scale_kernel, [array((GRID, GROUPS, GROUP), f32)] * 2)(mean, *around)
@@ -193,31 +223,31 @@
         part = after(part, *gate, *received)
         received.append(lax.all_to_all(part, ZC, 0, 0, tiled=True))
 
-    tokens = [joined] + [shifted(joined, "tensor", hops) for hops in (2, 1, 3)]
-    tokens += [shifted(part, "dp_2", 1) for part in tokens]
+    parts = [turned(joined, hops) for hops in range(NY)]
+    parts += [shifted(part, "dp_2", 1) for part in parts]
 
     shares = []
     for at, (source, first, units) in enumerate(PIECES):
-        gathers = at == 0
         out_shape = [array((units, GRID, ROWS, TOKENS), bf16)] * NX
-        if gathers:
-            out_shape.append(array((TOKENS, BLOCK), bf16))
-        columns = received[source] if gathers else after(received[source], shares[-NX])
-        partial = kernel(
-            piece_kernel(first, units, gathers),
-            out_shape,
-            limit=14,
-            flops=3 * units * GRID * UNIT * TOKENS * BLOCK,
-            scratch_shapes=[pltpu.VMEM((GRID * UNIT, BLOCK), bf16)] * min(units, 2),
-        )(columns, scale, inverse, *tokens)
-        if gathers:
-            tokens = partial[NX:]
+        work = units * GRID * UNIT * TOKENS * BLOCK
+        if at == 0:
+            quantized = array((units, GRID * UNIT, BLOCK), bf16)
+            deltas = kernel(quantize_kernel, quantized, flops=2 * work)(received[0], scale, inverse)
+            *partial, tokens = kernel(
+                first_kernel(units), out_shape + [array((TOKENS, BLOCK), bf16)], flops=work
+            )(deltas, *parts)
+        else:
+            partial = kernel(
+                piece_kernel(first, units),
+                out_shape,
+                flops=3 * work,
+                scratch_shapes=[pltpu.VMEM((GRID * UNIT, BLOCK), bf16)] * min(units, 2),
+            )(after(received[source], shares[-NX]), scale, inverse, tokens)
         shares += [partial[0]] + [shifted(partial[hops], "dp_0", hops) for hops in (2, 1, 3)]
     sums, totals = kernel(error_kernel, [array((GRID, UNITS * ROWS), f32), array((1, GRID), f32)])(*shares)
-    totals = jnp.sum(spread(totals, ("dp_0", "tensor"), NX * NY), axis=0)
     own_mean = lax.dynamic_slice_in_dim(after(mean, sums).reshape(-1), lax.axis_index(ZC) * GROUP, GROUP)
-    errors = jnp.sum(spread(totals, ZC, NZ * NC), axis=0).reshape(GRID) / (TOKENS * F)
-    column_errors = after(sums, totals) / TOKENS
+    errors = jnp.sum(spread(totals, ("dp_0", "dp_1", "dp_2", "tensor"), NX * NZ * NC * NY), axis=0).reshape(GRID) / (TOKENS * F)
+    column_errors = sums / TOKENS
     return (own_mean, column_errors, errors)
 
 

time: 169 us -> 215 us (1.27)
  waiting for transfers between devices: 68.8 us -> 93.8 us
  starting transfers between devices: 66.1 us -> 85.7 us
    ppermute x1 -> x8, waiting for transfers between devices: 3.8 us -> 52.8 us  [turned(): return lax.ppermute(value, ('dp_0', 'tensor'), pairs)]
    ppermute x23 -> x17, waiting for transfers between devices: 38.9 us -> 18.6 us  [shifted(): lax.ppermute(value, axis, [(i, (i + hops) % size) for i in range(size)])]
    ppermute x1 -> x8, starting transfers between devices: 3.46 us -> 19.4 us  [turned(): return lax.ppermute(value, ('dp_0', 'tensor'), pairs)]
    all_to_all x3 -> x1, waiting for transfers between devices: 25.6 us -> 11.1 us  [spread(): return lax.all_to_all(wide, axes, 0, 0, tiled=True)]
    all_to_all x0 -> x1, waiting for transfers between devices: none -> 11.4 us  [search(): parts = lax.all_to_all(packed, 'dp_1', 0, 0, tiled=True)]
    all_to_all x0 -> x1, starting transfers between devices: none -> 8.47 us  [search(): parts = lax.all_to_all(packed, 'dp_1', 0, 0, tiled=True)]
    all_to_all x3 -> x1, starting transfers between devices: 20 us -> 14 us  [spread(): return lax.all_to_all(wide, axes, 0, 0, tiled=True)]
    pallas_call x3 -> x5, Pallas kernels: 19.6 us -> 21.3 us  [the longest x2 11.6 us: search(): kernel(piece_kernel(first, units), out_shape, flops=3 * work, scratch_sha...]
  transfers between devices with their start and end apart: 29 -> 29, of which waited for: 19 -> 15; matrix products, arithmetic and copies ran while one was open for 1% -> 1% of each run, Pallas kernels for 13% -> 11%
where the time goes in v4:
time: 215 us; the launch traced here: 213 us
  waiting for transfers between devices  93.8 us (44%)
  starting transfers between devices  85.7 us (40%)
  Pallas kernels  24.3 us (11%)
  local copies, waits for them, and re-layouts  7.17 us (3%)
    ppermute x8, waiting for transfers between devices, turned(): return lax.ppermute(value, ('dp_0', 'tensor'), pairs)  52.8 us
    ppermute x17, starting transfers between devices, shifted(): lax.ppermute(value, axis, [(i, (i + hops) % size) for i in range(size)])  33.2 us
    ppermute x8, starting transfers between devices, turned(): return lax.ppermute(value, ('dp_0', 'tensor'), pairs)  19.4 us
    ppermute x17, waiting for transfers between devices, shifted(): lax.ppermute(value, axis, [(i, (i + hops) % size) for i in range(size)])  18.6 us
    all_to_all x1, starting transfers between devices, spread(): return lax.all_to_all(wide, axes, 0, 0, tiled=True)  14 us
    pallas_call x2, Pallas kernels, search(): kernel(piece_kernel(first, units), out_shape, flops=3 * work, scratch_sha...  11.6 us
    all_to_all x1, waiting for transfers between devices, search(): parts = lax.all_to_all(packed, 'dp_1', 0, 0, tiled=True)  11.4 us
    all_to_all x1, waiting for transfers between devices, spread(): return lax.all_to_all(wide, axes, 0, 0, tiled=True)  11.1 us
  transfers between devices with their start and end apart: 29, of which 15 were waited for; matrix products, arithmetic and copies ran while one was open for 1% of the time, Pallas kernels for 11%

profile of v4, /device:TPU:2, one launch (start us, length us, event | category | flops | bytes accessed | tf_op | source)
XLA Modules:
  0.0 213.2 jit_solution(7394004680492966936)
XLA Ops:
  0.6 0.8 copy-done.1
  1.5 0.8 shard_map.49
  2.3 8.5 %all-to-all-start = ((bf16[8,24,1024]{2,1,0:T(8,128)(2,1)}), bf16[8,24,1024]{2,1,0:T(8,128)(2,1)S(1)}, u32[]{:S(2)}, u32[]{:S(2)}) async-start(bf16[8,24,1024]{2,1,0:T(8,128)(2,1)} %shard_map.49), calls=%async_computation | async-start | bytes 786432 | tf_op jit(solution)/shard_map/all_to_all | solution.py:205
  10.7 1.5 copy-done
  12.2 1.8 shard_map.50
  14.0 11.4 %all-to-all-done.parts_ref = bf16[8,24,1024]{2,1,0:T(8,128)(2,1)S(1)} async-done(((bf16[8,24,1024]{2,1,0:T(8,128)(2,1)}), bf16[8,24,1024]{2,1,0:T(8,128)(2,1)S(1)}, u32[]{:S(2)}, u32[]{:S(2)}) %all-to-all-start) | async-done | bytes 393248 | tf_op jit(solution)/shard_map/all_to_all | solution.py:205
  25.7 3.6 %all-to-all-start.1 = ((bf16[16,192,128]{2,1,0:T(8,128)(2,1)}), bf16[16,192,128]{2,1,0:T(8,128)(2,1)S(1)}, u32[]{:S(2)}, u32[]{:S(2)}) async-start(bf16[16,192,128]{2,1,0:T(8,128)(2,1)} %get-tuple-element.37), calls=%async_computation.1 | async-start | bytes 1572864 | tf_op jit(solution)/shard_map/all_to_all | solution.py:224
  29.3 0.6 collective-permute-start.3
  29.9 6.4 %collective-permute-start.2 = (f32[16,128]{1,0:T(8,128)S(1)}, f32[16,128]{1,0:T(8,128)S(1)}, u32[]{:S(2)}, u32[]{:S(2)}) collective-permute-start(f32[16,128]{1,0:T(8,128)S(1)} %bitcast.7), channel_id=1, source_target_pairs={{0,1},{1,65},{2,129},{3,193},{64,2},{65,66},{66,130},{67,194},{128... | collective-permute-start | bytes 24584 | tf_op jit(solution)/shard_map/ppermute | solution.py:194
  36.3 1.9 collective-permute-start.1
  38.2 1.9 collective-permute-start
  40.2 0.7 collective-permute-done.1
  40.9 3.9 %collective-permute-done = f32[16,128]{1,0:T(8,128)S(1)} collective-permute-done((f32[16,128]{1,0:T(8,128)S(1)}, f32[16,128]{1,0:T(8,128)S(1)}, u32[]{:S(2)}, u32[]{:S(2)}) %collective-permute-start) | collective-permute-done | bytes 8224 | tf_op jit(solution)/shard_map/ppermute | solution.py:194
  44.7 1.2 collective-permute-done.4.core_1
  45.9 2.0 collective-permute-start.6
  47.9 1.6 collective-permute-start.5
  49.6 3.5 %collective-permute-done.5.mean_1 = f32[16,128]{1,0:T(8,128)S(1)} collective-permute-done((f32[16,128]{1,0:T(8,128)S(1)}, f32[16,128]{1,0:T(8,128)S(1)}, u32[]{:S(2)}, u32[]{:S(2)}) %collective-permute-start.5) | collective-permute-done | bytes 8224 | tf_op jit(solution)/shard_map/ppermute | solution.py:189
  53.4 7.1 %all-to-all-start.2 = ((bf16[16,256,128]{2,1,0:T(8,128)(2,1)}), bf16[16,256,128]{2,1,0:T(8,128)(2,1)S(1)}, u32[]{:S(2)}, u32[]{:S(2)}) async-start(bf16[16,256,128]{2,1,0:T(8,128)(2,1)} %get-tuple-element.44), calls=%async_computation.2 | async-start | bytes 2097152 | tf_op jit(solution)/shard_map/all_to_all | solution.py:224
  60.7 3.6 %collective-permute-start.10 = (bf16[96,2048]{1,0:T(8,128)(2,1)S(1)}, bf16[96,2048]{1,0:T(8,128)(2,1)S(1)}, u32[]{:S(2)}, u32[]{:S(2)}) collective-permute-start(bf16[96,2048]{1,0:T(8,128)(2,1)S(1)} %get-tuple-element.36), channel_id=1, source_target_pairs={{0,2},{1,66},{2,130},{3,194},{64,3},{65,67},{66,131},{67,195},{128... | collective-permute-start | bytes 1179656 | tf_op jit(solution)/shard_map/ppermute | solution.py:194
  64.2 1.4 collective-permute-start.9
  65.7 3.4 %collective-permute-start.8 = (bf16[96,2048]{1,0:T(8,128)(2,1)S(1)}, bf16[96,2048]{1,0:T(8,128)(2,1)S(1)}, u32[]{:S(2)}, u32[]{:S(2)}) collective-permute-start(bf16[96,2048]{1,0:T(8,128)(2,1)S(1)} %get-tuple-element.36), channel_id=1, source_target_pairs={{0,0},{1,64},{2,128},{3,192},{64,1},{65,65},{66,129},{67,193},{128... | collective-permute-start | bytes 1179656 | tf_op jit(solution)/shard_map/ppermute | solution.py:194
  69.1 11.9 %collective-permute-done.11.refs_4_ = bf16[96,2048]{1,0:T(8,128)(2,1)S(1)} collective-permute-done((bf16[96,2048]{1,0:T(8,128)(2,1)S(1)}, bf16[96,2048]{1,0:T(8,128)(2,1)S(1)}, u32[]{:S(2)}, u32[]{:S(2)}) %collective-permute-start.11) | collective-permute-done | bytes 393248 | tf_op jit(solution)/shard_map/ppermute | solution.py:194
  81.0 36.3 %collective-permute-done.10.refs_3_ = bf16[96,2048]{1,0:T(8,128)(2,1)S(1)} collective-permute-done((bf16[96,2048]{1,0:T(8,128)(2,1)S(1)}, bf16[96,2048]{1,0:T(8,128)(2,1)S(1)}, u32[]{:S(2)}, u32[]{:S(2)}) %collective-permute-start.10) | collective-permute-done | bytes 393248 | tf_op jit(solution)/shard_map/ppermute | solution.py:194
  118.1 5.6 %shard_map.54.refs_0_ = bf16[3,256,2048]{2,1,0:T(8,128)(2,1)S(1)} custom-call(bf16[16,192,128]{2,1,0:T(8,128)(2,1)S(1)} %all-to-all-done.1.columns_ref, f32[4,16,128]{2,1,0:T(8,128)S(1)} %get-tuple-element.38.scale_ref, f32[4,16,128]{2,1,0:T(8,128)S(1)} %get-tuple-element.39.inverse_ref), custom_call_target="tpu_custom_call" | custom-call | flops 2415919104 | tf_op jit(solution)/shard_map/pallas_call | solution.py:235
  123.7 3.4 %shard_map.55 = (bf16[3,4,16,768]{3,2,1,0:T(8,128)(2,1)S(1)}, bf16[3,4,16,768]{3,2,1,0:T(8,128)(2,1)S(1)}, bf16[3,4,16,768]{3,2,1,0:T(8,128)(2,1)}, bf16[3,4,16,...) custom-call(bf16[3,256,2048]{2,1,0:T(8,128)(2,1)S(1)} %shard_map.54.refs_0_, ...), custom_call_target="tpu_custom_call" | custom-call | flops 1207959552 | tf_op jit(solution)/shard_map/pallas_call | solution.py:236
  127.1 1.6 copy-done.2
  128.7 20.0 %collective-permute-start.16 = (bf16[3,4,16,768]{3,2,1,0:T(8,128)(2,1)}, bf16[3,4,16,768]{3,2,1,0:T(8,128)(2,1)S(1)}, u32[]{:S(2)}, u32[]{:S(2)}) collective-permute-start(bf16[3,4,16,768]{3,2,1,0:T(8,128)(2,1)} %get-tuple-element.41), channel_id=1, source_target_pairs={{0,128},{64,192},{128,0},{192,64},{1,129},{65,193},{129,1},{193,65... | collective-permute-start | bytes 884744 | tf_op jit(solution)/shard_map/ppermute | solution.py:189
  148.7 2.0 collective-permute-start.18
  150.8 1.9 copy-done.3
  152.7 5.8 %shard_map.56 = (bf16[2,4,16,768]{3,2,1,0:T(8,128)(2,1)S(1)}, bf16[2,4,16,768]{3,2,1,0:T(8,128)(2,1)}, bf16[2,4,16,768]{3,2,1,0:T(8,128)(2,1)}, bf16[2,4,16,768]{3,2,1,0:T(8,128)(2,1)}) custom-call(bf16[16,256,128]{2,1,0:T(8,128)(2,1)S(1)} %all-to-all-done.2.columns_ref, f32[4,16,128]{2,1,0:T(8,128)S(1)} %get-tuple-element.38.scale_ref, ...), custom_call_target="tpu_custom_call" | custom-call | flops 2415919104 | tf_op jit(solution)/shard_map/pallas_call | solution.py:240
  158.5 5.7 %shard_map.57 = (bf16[2,4,16,768]{3,2,1,0:T(8,128)(2,1)S(1)}, bf16[2,4,16,768]{3,2,1,0:T(8,128)(2,1)}, bf16[2,4,16,768]{3,2,1,0:T(8,128)(2,1)S(1)}, bf16[2,4,16,768]{3,2,1,0:T(8,128)(2,1)}) custom-call(bf16[16,256,128]{2,1,0:T(8,128)(2,1)S(1)} %all-to-all-done.2.columns_ref, f32[4,16,128]{2,1,0:T(8,128)S(1)} %get-tuple-element.38.scale_ref, ...), custom_call_target="tpu_custom_call" | custom-call | flops 2415919104 | tf_op jit(solution)/shard_map/pallas_call | solution.py:240
  164.2 1.5 collective-permute-start.23
  165.7 0.6 collective-permute-start.24
  166.3 3.5 %collective-permute-start.19 = (bf16[2,4,16,768]{3,2,1,0:T(8,128)(2,1)}, bf16[2,4,16,768]{3,2,1,0:T(8,128)(2,1)S(1)}, u32[]{:S(2)}, u32[]{:S(2)}) collective-permute-start(bf16[2,4,16,768]{3,2,1,0:T(8,128)(2,1)} %get-tuple-element.48), channel_id=1, source_target_pairs={{0,128},{64,192},{128,0},{192,64},{1,129},{65,193},{129,1},{193,65... | collective-permute-start | bytes 589832 | tf_op jit(solution)/shard_map/ppermute | solution.py:189
  169.8 1.2 collective-permute-start.20
  171.0 2.5 %collective-permute-done.22.refs_9_ = bf16[2,4,16,768]{3,2,1,0:T(8,128)(2,1)S(1)} collective-permute-done((bf16[2,4,16,768]{3,2,1,0:T(8,128)(2,1)S(1)}, bf16[2,4,16,768]{3,2,1,0:T(8,128)(2,1)S(1)}, u32[]{:S(2)}, u32[]{:S(2)}) %collective-permute-start.22) | collective-permute-done | bytes 196640 | tf_op jit(solution)/shard_map/ppermute | solution.py:189
  173.5 2.7 %collective-permute-done.23.refs_10_ = bf16[2,4,16,768]{3,2,1,0:T(8,128)(2,1)S(1)} collective-permute-done((bf16[2,4,16,768]{3,2,1,0:T(8,128)(2,1)}, bf16[2,4,16,768]{3,2,1,0:T(8,128)(2,1)S(1)}, u32[]{:S(2)}, u32[]{:S(2)}) %collective-permute-start.23) | collective-permute-done | bytes 196640 | tf_op jit(solution)/shard_map/ppermute | solution.py:189
  176.2 1.6 collective-permute-done.24.refs_11_
  177.8 4.2 %collective-permute-done.19.refs_5_ = bf16[2,4,16,768]{3,2,1,0:T(8,128)(2,1)S(1)} collective-permute-done((bf16[2,4,16,768]{3,2,1,0:T(8,128)(2,1)}, bf16[2,4,16,768]{3,2,1,0:T(8,128)(2,1)S(1)}, u32[]{:S(2)}, u32[]{:S(2)}) %collective-permute-start.19) | collective-permute-done | bytes 196640 | tf_op jit(solution)/shard_map/ppermute | solution.py:189
  182.0 1.7 collective-permute-done.20.refs_6_
  183.7 1.1 collective-permute-done.21.refs_7_
  184.8 0.6 shard_map.58
  185.4 0.7 broadcast_in_dim.9
  186.1 14.0 %all-to-all-start.3 = ((f32[256,1,4]{2,1,0:T(1,128)}), f32[256,1,4]{2,1,0:T(1,128)S(1)}, u32[]{:S(2)}, u32[]{:S(2)}) async-start(f32[256,1,4]{2,1,0:T(1,128)} %broadcast_in_dim.9), calls=%async_computation.3 | async-start | bytes 262144 | tf_op jit(solution)/shard_map/all_to_all | solution.py:184
  200.2 0.6 broadcast_multiply_fusion
  200.7 0.6 dynamic_slice.3
  201.3 11.1 %all-to-all-done.3 = f32[256,1,4]{2,1,0:T(1,128)S(1)} async-done(((f32[256,1,4]{2,1,0:T(1,128)}), f32[256,1,4]{2,1,0:T(1,128)S(1)}, u32[]{:S(2)}, u32[]{:S(2)}) %all-to-all-start.3) | async-done | bytes 4128 | tf_op jit(solution)/shard_map/all_to_all | solution.py:184
  212.7 0.5 broadcast_multiply_fusion.1
  (34 shorter events, 2.0 us)
Async XLA Ops:
  0.6 0.8 copy-start.1
  2.3 23.2 %all-to-all-start = ((bf16[8,24,1024]{2,1,0:T(8,128)(2,1)}), bf16[8,24,1024]{2,1,0:T(8,128)(2,1)S(1)}, u32[]{:S(2)}, u32[]{:S(2)}) async-start(bf16[8,24,1024]{2,1,0:T(8,128)(2,1)} %shard_map.49), calls=%async_computation | async-start | bytes 786432 | tf_op jit(solution)/shard_map/all_to_all | solution.py:205
  10.7 1.5 copy-start
  25.7 27.7 %all-to-all-start.1 = ((bf16[16,192,128]{2,1,0:T(8,128)(2,1)}), bf16[16,192,128]{2,1,0:T(8,128)(2,1)S(1)}, u32[]{:S(2)}, u32[]{:S(2)}) async-start(bf16[16,192,128]{2,1,0:T(8,128)(2,1)} %get-tuple-element.37), calls=%async_computation.1 | async-start | bytes 1572864 | tf_op jit(solution)/shard_map/all_to_all | solution.py:224
  29.3 10.8 %collective-permute-start.3 = (f32[16,128]{1,0:T(8,128)S(1)}, f32[16,128]{1,0:T(8,128)S(1)}, u32[]{:S(2)}, u32[]{:S(2)}) collective-permute-start(f32[16,128]{1,0:T(8,128)S(1)} %bitcast.6), channel_id=1, source_target_pairs={{0,3},{1,67},{2,131},{3,195},{64,0},{65,64},{66,128},{67,192},{128... | collective-permute-start | bytes 24584 | tf_op jit(solution)/shard_map/ppermute | solution.py:194
  29.9 10.2 %collective-permute-start.2 = (f32[16,128]{1,0:T(8,128)S(1)}, f32[16,128]{1,0:T(8,128)S(1)}, u32[]{:S(2)}, u32[]{:S(2)}) collective-permute-start(f32[16,128]{1,0:T(8,128)S(1)} %bitcast.7), channel_id=1, source_target_pairs={{0,1},{1,65},{2,129},{3,193},{64,2},{65,66},{66,130},{67,194},{128... | collective-permute-start | bytes 24584 | tf_op jit(solution)/shard_map/ppermute | solution.py:194
  36.3 4.5 %collective-permute-start.1 = (f32[16,128]{1,0:T(8,128)S(1)}, f32[16,128]{1,0:T(8,128)S(1)}, u32[]{:S(2)}, u32[]{:S(2)}) collective-permute-start(f32[16,128]{1,0:T(8,128)S(1)} %bitcast.8), channel_id=1, source_target_pairs={{0,2},{1,66},{2,130},{3,194},{64,3},{65,67},{66,131},{67,195},{128... | collective-permute-start | bytes 24584 | tf_op jit(solution)/shard_map/ppermute | solution.py:194
  38.2 6.5 %collective-permute-start = (f32[16,128]{1,0:T(8,128)S(1)}, f32[16,128]{1,0:T(8,128)S(1)}, u32[]{:S(2)}, u32[]{:S(2)}) collective-permute-start(f32[16,128]{1,0:T(8,128)S(1)} %bitcast.9), channel_id=1, source_target_pairs={{0,0},{1,64},{2,128},{3,192},{64,1},{65,65},{66,129},{67,193},{128... | collective-permute-start | bytes 24584 | tf_op jit(solution)/shard_map/ppermute | solution.py:194
  44.7 1.2 collective-permute-start.4
  45.9 3.7 %collective-permute-start.7 = (f32[16,128]{1,0:T(8,128)S(1)}, f32[16,128]{1,0:T(8,128)S(1)}, u32[]{:S(2)}, u32[]{:S(2)}) collective-permute-start(f32[16,128]{1,0:T(8,128)S(1)} %shard_map.52.mean_0), channel_id=1, source_target_pairs={{0,192},{64,0},{128,64},{192,128},{1,193},{65,1},{129,65},{193,129... | collective-permute-start | bytes 24584 | tf_op jit(solution)/shard_map/ppermute | solution.py:189
  45.9 3.7 %collective-permute-start.6 = (f32[16,128]{1,0:T(8,128)S(1)}, f32[16,128]{1,0:T(8,128)S(1)}, u32[]{:S(2)}, u32[]{:S(2)}) collective-permute-start(f32[16,128]{1,0:T(8,128)S(1)} %shard_map.52.mean_0), channel_id=1, source_target_pairs={{0,64},{64,128},{128,192},{192,0},{1,65},{65,129},{129,193},{193,1... | collective-permute-start | bytes 24584 | tf_op jit(solution)/shard_map/ppermute | solution.py:189
  47.9 5.2 %collective-permute-start.5 = (f32[16,128]{1,0:T(8,128)S(1)}, f32[16,128]{1,0:T(8,128)S(1)}, u32[]{:S(2)}, u32[]{:S(2)}) collective-permute-start(f32[16,128]{1,0:T(8,128)S(1)} %shard_map.52.mean_0), channel_id=1, source_target_pairs={{0,128},{64,192},{128,0},{192,64},{1,129},{65,193},{129,1},{193,65... | collective-permute-start | bytes 24584 | tf_op jit(solution)/shard_map/ppermute | solution.py:189
  53.4 97.3 %all-to-all-start.2 = ((bf16[16,256,128]{2,1,0:T(8,128)(2,1)}), bf16[16,256,128]{2,1,0:T(8,128)(2,1)S(1)}, u32[]{:S(2)}, u32[]{:S(2)}) async-start(bf16[16,256,128]{2,1,0:T(8,128)(2,1)} %get-tuple-element.44), calls=%async_computation.2 | async-start | bytes 2097152 | tf_op jit(solution)/shard_map/all_to_all | solution.py:224
  60.5 20.5 %collective-permute-start.11 = (bf16[96,2048]{1,0:T(8,128)(2,1)S(1)}, bf16[96,2048]{1,0:T(8,128)(2,1)S(1)}, u32[]{:S(2)}, u32[]{:S(2)}) collective-permute-start(bf16[96,2048]{1,0:T(8,128)(2,1)S(1)} %get-tuple-element.36), channel_id=1, source_target_pairs={{0,3},{1,67},{2,131},{3,195},{64,0},{65,64},{66,128},{67,192},{128... | collective-permute-start | bytes 1179656 | tf_op jit(solution)/shard_map/ppermute | solution.py:194
  60.7 56.6 %collective-permute-start.10 = (bf16[96,2048]{1,0:T(8,128)(2,1)S(1)}, bf16[96,2048]{1,0:T(8,128)(2,1)S(1)}, u32[]{:S(2)}, u32[]{:S(2)}) collective-permute-start(bf16[96,2048]{1,0:T(8,128)(2,1)S(1)} %get-tuple-element.36), channel_id=1, source_target_pairs={{0,2},{1,66},{2,130},{3,194},{64,3},{65,67},{66,131},{67,195},{128... | collective-permute-start | bytes 1179656 | tf_op jit(solution)/shard_map/ppermute | solution.py:194
  64.2 53.0 %collective-permute-start.9 = (bf16[96,2048]{1,0:T(8,128)(2,1)S(1)}, bf16[96,2048]{1,0:T(8,128)(2,1)S(1)}, u32[]{:S(2)}, u32[]{:S(2)}) collective-permute-start(bf16[96,2048]{1,0:T(8,128)(2,1)S(1)} %get-tuple-element.36), channel_id=1, source_target_pairs={{0,1},{1,65},{2,129},{3,193},{64,2},{65,66},{66,130},{67,194},{128... | collective-permute-start | bytes 1179656 | tf_op jit(solution)/shard_map/ppermute | solution.py:194
  65.7 52.1 %collective-permute-start.8 = (bf16[96,2048]{1,0:T(8,128)(2,1)S(1)}, bf16[96,2048]{1,0:T(8,128)(2,1)S(1)}, u32[]{:S(2)}, u32[]{:S(2)}) collective-permute-start(bf16[96,2048]{1,0:T(8,128)(2,1)S(1)} %get-tuple-element.36), channel_id=1, source_target_pairs={{0,0},{1,64},{2,128},{3,192},{64,1},{65,65},{66,129},{67,193},{128... | collective-permute-start | bytes 1179656 | tf_op jit(solution)/shard_map/ppermute | solution.py:194
  81.0 42.6 %collective-permute-start.15 = (bf16[96,2048]{1,0:T(8,128)(2,1)S(1)}, bf16[96,2048]{1,0:T(8,128)(2,1)S(1)}, u32[]{:S(2)}, u32[]{:S(2)}) collective-permute-start(bf16[96,2048]{1,0:T(8,128)(2,1)S(1)} %collective-permute-done.11.refs_4_), channel_id=1, source_target_pairs={{0,4},{4,0},{1,5},{5,1},{2,6},{6,2},{3,7},{7,3},{8,12},{12,8},{9,1... | collective-permute-start | bytes 1179656 | tf_op jit(solution)/shard_map/ppermute | solution.py:189
  117.3 6.4 %collective-permute-start.14 = (bf16[96,2048]{1,0:T(8,128)(2,1)S(1)}, bf16[96,2048]{1,0:T(8,128)(2,1)S(1)}, u32[]{:S(2)}, u32[]{:S(2)}) collective-permute-start(bf16[96,2048]{1,0:T(8,128)(2,1)S(1)} %collective-permute-done.10.refs_3_), channel_id=1, source_target_pairs={{0,4},{4,0},{1,5},{5,1},{2,6},{6,2},{3,7},{7,3},{8,12},{12,8},{9,1... | collective-permute-start | bytes 1179656 | tf_op jit(solution)/shard_map/ppermute | solution.py:189
  117.3 6.4 %collective-permute-start.13 = (bf16[96,2048]{1,0:T(8,128)(2,1)S(1)}, bf16[96,2048]{1,0:T(8,128)(2,1)S(1)}, u32[]{:S(2)}, u32[]{:S(2)}) collective-permute-start(bf16[96,2048]{1,0:T(8,128)(2,1)S(1)} %collective-permute-done.9.refs_2_), channel_id=1, source_target_pairs={{0,4},{4,0},{1,5},{5,1},{2,6},{6,2},{3,7},{7,3},{8,12},{12,8},{9,1... | collective-permute-start | bytes 1179656 | tf_op jit(solution)/shard_map/ppermute | solution.py:189
  117.8 5.9 %collective-permute-start.12 = (bf16[96,2048]{1,0:T(8,128)(2,1)S(1)}, bf16[96,2048]{1,0:T(8,128)(2,1)S(1)}, u32[]{:S(2)}, u32[]{:S(2)}) collective-permute-start(bf16[96,2048]{1,0:T(8,128)(2,1)S(1)} %collective-permute-done.8.refs_1_), channel_id=1, source_target_pairs={{0,4},{4,0},{1,5},{5,1},{2,6},{6,2},{3,7},{7,3},{8,12},{12,8},{9,1... | collective-permute-start | bytes 1179656 | tf_op jit(solution)/shard_map/ppermute | solution.py:189
  127.1 1.6 copy-start.2
  128.7 36.9 %collective-permute-start.16 = (bf16[3,4,16,768]{3,2,1,0:T(8,128)(2,1)}, bf16[3,4,16,768]{3,2,1,0:T(8,128)(2,1)S(1)}, u32[]{:S(2)}, u32[]{:S(2)}) collective-permute-start(bf16[3,4,16,768]{3,2,1,0:T(8,128)(2,1)} %get-tuple-element.41), channel_id=1, source_target_pairs={{0,128},{64,192},{128,0},{192,64},{1,129},{65,193},{129,1},{193,65... | collective-permute-start | bytes 884744 | tf_op jit(solution)/shard_map/ppermute | solution.py:189
  148.7 17.6 %collective-permute-start.17 = (bf16[3,4,16,768]{3,2,1,0:T(8,128)(2,1)S(1)}, bf16[3,4,16,768]{3,2,1,0:T(8,128)(2,1)S(1)}, u32[]{:S(2)}, u32[]{:S(2)}) collective-permute-start(bf16[3,4,16,768]{3,2,1,0:T(8,128)(2,1)S(1)} %get-tuple-element.42), channel_id=1, source_target_pairs={{0,64},{64,128},{128,192},{192,0},{1,65},{65,129},{129,193},{193,1... | collective-permute-start | bytes 884744 | tf_op jit(solution)/shard_map/ppermute | solution.py:189
  148.7 21.0 %collective-permute-start.18 = (bf16[3,4,16,768]{3,2,1,0:T(8,128)(2,1)S(1)}, bf16[3,4,16,768]{3,2,1,0:T(8,128)(2,1)S(1)}, u32[]{:S(2)}, u32[]{:S(2)}) collective-permute-start(bf16[3,4,16,768]{3,2,1,0:T(8,128)(2,1)S(1)} %get-tuple-element.43), channel_id=1, source_target_pairs={{0,192},{64,0},{128,64},{192,128},{1,193},{65,1},{129,65},{193,129... | collective-permute-start | bytes 884744 | tf_op jit(solution)/shard_map/ppermute | solution.py:189
  150.8 1.9 copy-start.3
  164.2 9.3 %collective-permute-start.22 = (bf16[2,4,16,768]{3,2,1,0:T(8,128)(2,1)S(1)}, bf16[2,4,16,768]{3,2,1,0:T(8,128)(2,1)S(1)}, u32[]{:S(2)}, u32[]{:S(2)}) collective-permute-start(bf16[2,4,16,768]{3,2,1,0:T(8,128)(2,1)S(1)} %get-tuple-element.53), channel_id=1, source_target_pairs={{0,128},{64,192},{128,0},{192,64},{1,129},{65,193},{129,1},{193,65... | collective-permute-start | bytes 589832 | tf_op jit(solution)/shard_map/ppermute | solution.py:189
  164.2 12.0 %collective-permute-start.23 = (bf16[2,4,16,768]{3,2,1,0:T(8,128)(2,1)}, bf16[2,4,16,768]{3,2,1,0:T(8,128)(2,1)S(1)}, u32[]{:S(2)}, u32[]{:S(2)}) collective-permute-start(bf16[2,4,16,768]{3,2,1,0:T(8,128)(2,1)} %get-tuple-element.54), channel_id=1, source_target_pairs={{0,64},{64,128},{128,192},{192,0},{1,65},{65,129},{129,193},{193,1... | collective-permute-start | bytes 589832 | tf_op jit(solution)/shard_map/ppermute | solution.py:189
  165.7 12.1 %collective-permute-start.24 = (bf16[2,4,16,768]{3,2,1,0:T(8,128)(2,1)}, bf16[2,4,16,768]{3,2,1,0:T(8,128)(2,1)S(1)}, u32[]{:S(2)}, u32[]{:S(2)}) collective-permute-start(bf16[2,4,16,768]{3,2,1,0:T(8,128)(2,1)} %get-tuple-element.55), channel_id=1, source_target_pairs={{0,192},{64,0},{128,64},{192,128},{1,193},{65,1},{129,65},{193,129... | collective-permute-start | bytes 589832 | tf_op jit(solution)/shard_map/ppermute | solution.py:189
  166.3 15.7 %collective-permute-start.19 = (bf16[2,4,16,768]{3,2,1,0:T(8,128)(2,1)}, bf16[2,4,16,768]{3,2,1,0:T(8,128)(2,1)S(1)}, u32[]{:S(2)}, u32[]{:S(2)}) collective-permute-start(bf16[2,4,16,768]{3,2,1,0:T(8,128)(2,1)} %get-tuple-element.48), channel_id=1, source_target_pairs={{0,128},{64,192},{128,0},{192,64},{1,129},{65,193},{129,1},{193,65... | collective-permute-start | bytes 589832 | tf_op jit(solution)/shard_map/ppermute | solution.py:189
  169.8 13.9 %collective-permute-start.20 = (bf16[2,4,16,768]{3,2,1,0:T(8,128)(2,1)}, bf16[2,4,16,768]{3,2,1,0:T(8,128)(2,1)S(1)}, u32[]{:S(2)}, u32[]{:S(2)}) collective-permute-start(bf16[2,4,16,768]{3,2,1,0:T(8,128)(2,1)} %get-tuple-element.49), channel_id=1, source_target_pairs={{0,64},{64,128},{128,192},{192,0},{1,65},{65,129},{129,193},{193,1... | collective-permute-start | bytes 589832 | tf_op jit(solution)/shard_map/ppermute | solution.py:189
  173.5 11.3 %collective-permute-start.21 = (bf16[2,4,16,768]{3,2,1,0:T(8,128)(2,1)}, bf16[2,4,16,768]{3,2,1,0:T(8,128)(2,1)S(1)}, u32[]{:S(2)}, u32[]{:S(2)}) collective-permute-start(bf16[2,4,16,768]{3,2,1,0:T(8,128)(2,1)} %get-tuple-element.50), channel_id=1, source_target_pairs={{0,192},{64,0},{128,64},{192,128},{1,193},{65,1},{129,65},{193,129... | collective-permute-start | bytes 589832 | tf_op jit(solution)/shard_map/ppermute | solution.py:189
  186.1 26.3 %all-to-all-start.3 = ((f32[256,1,4]{2,1,0:T(1,128)}), f32[256,1,4]{2,1,0:T(1,128)S(1)}, u32[]{:S(2)}, u32[]{:S(2)}) async-start(f32[256,1,4]{2,1,0:T(1,128)} %broadcast_in_dim.9), calls=%async_computation.3 | async-start | bytes 262144 | tf_op jit(solution)/shard_map/all_to_all | solution.py:184

commit v5 on v4

--- a/solution.py
+++ b/solution.py
@@ -20,9 +20,12 @@
 UNIT = NX * ROWS
 BLOCK = D // NX
 GROUPS = BLOCK // GROUP
-SENDS = (3, 4)
-PIECES = ((0, 0, 3), (1, 0, 2), (1, 2, 2))
+SENDS = (2, 5)
+PIECES = ((0, 0, 2), (1, 0, 3), (1, 3, 2))
 MIB = 1 << 20
+HALF = BLOCK // 2
+OWN = TOKENS // (NX * NZ * NC)
+LEAD = OWN * HALF // GROUP
 
 SINE = (
     0.9999996039230294,
@@ -58,24 +61,36 @@
 
 
 def pack_tokens(tokens_ref, out_ref):
-    for at in range(NZ):
-        out_ref[at, :12, :] = tokens_ref[:, : BLOCK // 2]
-        out_ref[at, 12:, :] = tokens_ref[:, BLOCK // 2 :]
+    out_ref[:OWN, :] = tokens_ref[:, :HALF]
+    out_ref[OWN:, :] = tokens_ref[:, HALF:]
+
+
+def merge_kernel(tokens_ref, columns_ref, out_ref):
+    for half in range(NC):
+        for block in range(HALF // GROUP):
+            rows = tokens_ref[half * OWN : (half + 1) * OWN, block * GROUP : (block + 1) * GROUP]
+            for z in range(NZ):
+                out_ref[z * NC + half, block * OWN : (block + 1) * OWN, :] = rows
+    out_ref[:, LEAD:, :] = columns_ref[...]
 
 
 def join_tokens(parts_ref, out_ref, sums_ref):
-    for half in range(2):
-        total = jnp.zeros((1, BLOCK // 2), jnp.float32)
-        lanes = slice(half * BLOCK // 2, (half + 1) * BLOCK // 2)
-        for at in range(NZ):
-            rows = parts_ref[at, half * 12 : (half + 1) * 12, :]
-            out_ref[at * 12 : (at + 1) * 12, lanes] = rows
-            total += jnp.sum(jnp.abs(rows.astype(jnp.float32)), axis=0, keepdims=True)
-        sums_ref[:, lanes] = total
-
-
-def mean_kernel(core_0, core_1, mean_ref):
-    mean_ref[...] = (core_0[...] + core_1[...]) / TOKENS + 1e-06
+    for block in range(HALF // GROUP):
+        lanes = slice(block * GROUP, (block + 1) * GROUP)
+        total = jnp.zeros((OWN, GROUP), jnp.float32)
+        for at in range(NZ * NC):
+            rows = parts_ref[at, block * OWN : (block + 1) * OWN, :]
+            out_ref[at * OWN : (at + 1) * OWN, lanes] = rows
+            total += jnp.abs(rows.astype(jnp.float32))
+        sums_ref[block : block + 1, :] = jnp.sum(total, axis=0, keepdims=True)
+
+
+def mean_kernel(core_ref, own_ref, other_ref, mean_ref):
+    rows = HALF // GROUP
+    own = pl.multiple_of(core_ref[0] * rows, rows)
+    other = pl.multiple_of((1 - core_ref[0]) * rows, rows)
+    mean_ref[pl.ds(own, rows), :] = own_ref[...] / TOKENS + 1e-06
+    mean_ref[pl.ds(other, rows), :] = other_ref[...] / TOKENS + 1e-06
 
 
 def scale_kernel(mean_0, mean_1, mean_2, mean_3, scale_ref, inverse_ref):
@@ -112,7 +127,7 @@
 def quantize_kernel(columns_ref, scale_ref, inverse_ref, deltas):
     @pl.loop(0, deltas.shape[0])
     def _(unit):
-        rows = pl.ds(pl.multiple_of(unit * UNIT, UNIT), UNIT)
+        rows = pl.ds(pl.multiple_of(LEAD + unit * UNIT, 32), UNIT)
         quantize(columns_ref, rows, scale_ref, inverse_ref, deltas.at[unit])
 
 
@@ -128,9 +143,14 @@
 
 def first_kernel(units):
     def body(*refs):
-        deltas, parts, out_refs, tokens = refs[0], refs[1:9], refs[9:13], refs[13]
-        for at, part in enumerate(parts):
-            tokens[at * 96 : (at + 1) * 96, :] = part[...]
+        core_ref, deltas, own, other = refs[0], refs[1], refs[2:6], refs[6:10]
+        out_refs, tokens = refs[10:14], refs[14]
+        at_own = pl.multiple_of(core_ref[0] * HALF, HALF)
+        at_other = pl.multiple_of((1 - core_ref[0]) * HALF, HALF)
+        count = TOKENS // NY
+        for at in range(NY):
+            tokens[at * count : (at + 1) * count, pl.ds(at_own, HALF)] = own[at][...]
+            tokens[at * count : (at + 1) * count, pl.ds(at_other, HALF)] = other[at][...]
         for unit in range(units):
             multiply(deltas.at[unit], tokens, out_refs, unit)
 
@@ -189,11 +209,6 @@
     return lax.ppermute(value, axis, [(i, (i + hops) % size) for i in range(size)])
 
 
-def turned(value, hops):
-    pairs = [(x * NY + y, y * NY + (x + hops) % NY) for x in range(NX) for y in range(NY)]
-    return lax.ppermute(value, ("dp_0", "tensor"), pairs)
-
-
 def after(value, *others):
     return lax.optimization_barrier((value, *others))[0]
 
@@ -201,29 +216,30 @@
 def search(activations, weight):
     array = jax.ShapeDtypeStruct
     f32, bf16 = jnp.float32, jnp.bfloat16
-    packed = kernel(pack_tokens, array((NZ, 24, BLOCK // 2), bf16))(activations)
-    parts = lax.all_to_all(packed, "dp_1", 0, 0, tiled=True)
+    smem, local = pl.BlockSpec(memory_space=pltpu.SMEM), pl.BlockSpec(memory_space=pltpu.VMEM)
+    core = lax.axis_index("dp_2").reshape(1)
+    packed = kernel(pack_tokens, array((NC * OWN, HALF), bf16))(activations)
+    turn = [(x * NY + y, y * NY + x) for x in range(NX) for y in range(NY)]
+    turned = lax.ppermute(packed, ("dp_0", "tensor"), turn)
     columns = kernel(
-        split_columns,
-        [array((NZ * NC, u * UNIT, GROUP), bf16) for u in SENDS],
-        in_specs=[pl.BlockSpec(memory_space=pltpu.SMEM), pl.BlockSpec(memory_space=pltpu.VMEM)],
-    )(lax.axis_index("dp_0").reshape(1), after(weight, packed))
-    parts = after(parts, *columns)
-    joined, sums = kernel(join_tokens, [array((96, BLOCK), bf16), array((1, BLOCK), f32)])(parts)
-
-    sums = sums.reshape(GROUPS, GROUP)
-    around = [turned(sums, hops) for hops in range(NY)]
-    sums = (around[0] + around[2]) + (around[1] + around[3])
-    mean = kernel(mean_kernel, array((GROUPS, GROUP), f32))(sums, shifted(sums, "dp_2", 1))
+        split_columns, [array((NZ * NC, u * UNIT, GROUP), bf16) for u in SENDS], in_specs=[smem, local]
+    )(lax.axis_index("dp_0").reshape(1), weight)
+    merged = array((NZ * NC, LEAD + SENDS[0] * UNIT, GROUP), bf16)
+    merged = kernel(merge_kernel, merged)(turned, columns[0])
+    received = [lax.all_to_all(merged, ZC, 0, 0, tiled=True)]
+    half = array((HALF // GROUP, GROUP), f32)
+    joined, sums = kernel(join_tokens, [array((TOKENS // NY, HALF), bf16), half])(received[0])
+    received.append(lax.all_to_all(after(columns[1], joined), ZC, 0, 0, tiled=True))
+
+    around = [shifted(sums, "tensor", hops) for hops in (2, 1, 3)]
+    sums = (sums + around[0]) + (around[1] + around[2])
+    mean = kernel(
+        mean_kernel, array((GROUPS, GROUP), f32), in_specs=[smem, local, local]
+    )(core, sums, shifted(sums, "dp_2", 1))
     around = [shifted(mean, "dp_0", hops) for hops in (2, 1, 3)]
     scale, inverse = kernel(scale_kernel, [array((GRID, GROUPS, GROUP), f32)] * 2)(mean, *around)
 
-    received = []
-    for part, gate in zip(columns, ([joined], [scale])):
-        part = after(part, *gate, *received)
-        received.append(lax.all_to_all(part, ZC, 0, 0, tiled=True))
-
-    parts = [turned(joined, hops) for hops in range(NY)]
+    parts = [joined] + [shifted(joined, "tensor", hops) for hops in (2, 1, 3)]
     parts += [shifted(part, "dp_2", 1) for part in parts]
 
     shares = []
@@ -234,8 +250,9 @@
             quantized = array((units, GRID * UNIT, BLOCK), bf16)
             deltas = kernel(quantize_kernel, quantized, flops=2 * work)(received[0], scale, inverse)
             *partial, tokens = kernel(
-                first_kernel(units), out_shape + [array((TOKENS, BLOCK), bf16)], flops=work
-            )(deltas, *parts)
+                first_kernel(units), out_shape + [array((TOKENS, BLOCK), bf16)], flops=work,
+                in_specs=[smem] + [local] * 9,
+            )(core, deltas, *parts)
         else:
             partial = kernel(
                 piece_kernel(first, units),

time: 215 us -> 169 us (0.79)
  waiting for transfers between devices: 93.8 us -> 52.5 us
  starting transfers between devices: 85.7 us -> 46.8 us
  blocking collectives: 0 us -> 33.1 us
    ppermute x8 -> x1, waiting for transfers between devices: 52.8 us -> 0.31 us  [search(): turned = lax.ppermute(packed, ('dp_0', 'tensor'), turn)]
    all_to_all x0 -> x1, blocking collectives: none -> 33.1 us  [search(): received = [lax.all_to_all(merged, ZC, 0, 0, tiled=True)]]
    ppermute x17 -> x23, waiting for transfers between devices: 18.6 us -> 41.1 us  [shifted(): lax.ppermute(value, axis, [(i, (i + hops) % size) for i in range(size)])]
    ppermute x8 -> x1, starting transfers between devices: 19.4 us -> 3.46 us  [search(): turned = lax.ppermute(packed, ('dp_0', 'tensor'), turn)]
    all_to_all x3 -> x1, starting transfers between devices: 19.2 us -> 3.84 us  [search(): lax.all_to_all(after(columns[1], joined), ZC, 0, 0, tiled=True)]
    all_to_all x3 -> x1, waiting for transfers between devices: 11.4 us -> 0.01 us  [search(): lax.all_to_all(after(columns[1], joined), ZC, 0, 0, tiled=True)]
    ppermute x17 -> x23, starting transfers between devices: 33.2 us -> 27.8 us  [shifted(): lax.ppermute(value, axis, [(i, (i + hops) % size) for i in range(size)])]
    pallas_call x2, Pallas kernels: 11.6 us -> 13.9 us  [search(): kernel(piece_kernel(first, units), out_shape, flops=3 * work, scratch_sha...]
  transfers between devices with their start and end apart: 29 -> 26, of which waited for: 15 -> 12; matrix products, arithmetic and copies ran while one was open for 1% -> 1% of each run, Pallas kernels for 11% -> 14%
where the time goes in v5:
time: 169 us; the launch traced here: 167 us
  waiting for transfers between devices  52.5 us (31%)
  starting transfers between devices  46.8 us (28%)
  blocking collectives  33.1 us (20%)
  Pallas kernels  24.8 us (15%)
  local copies, waits for them, and re-layouts  7.87 us (5%)
    ppermute x23, waiting for transfers between devices, shifted(): lax.ppermute(value, axis, [(i, (i + hops) % size) for i in range(size)])  41.1 us
    all_to_all x1, blocking collectives, search(): received = [lax.all_to_all(merged, ZC, 0, 0, tiled=True)]  33.1 us
    ppermute x23, starting transfers between devices, shifted(): lax.ppermute(value, axis, [(i, (i + hops) % size) for i in range(size)])  27.8 us
    pallas_call x2, Pallas kernels, search(): kernel(piece_kernel(first, units), out_shape, flops=3 * work, scratch_sha...  13.9 us
    all_to_all x1, starting transfers between devices, spread(): return lax.all_to_all(wide, axes, 0, 0, tiled=True)  11.7 us
    all_to_all x1, waiting for transfers between devices, spread(): return lax.all_to_all(wide, axes, 0, 0, tiled=True)  11.1 us
    unnamed x12, local copies, waits for them, and re-layouts  6.54 us
    pallas_call x1, Pallas kernels, search(): kernel(first_kernel(units), out_shape + [array((TOKENS, BLOCK), bf16)], f...  4.26 us
  transfers between devices with their start and end apart: 26, of which 12 were waited for; matrix products, arithmetic and copies ran while one was open for 1% of the time, Pallas kernels for 14%

profile of v5, /device:TPU:2, one launch (start us, length us, event | category | flops | bytes accessed | tf_op | source)
XLA Modules:
  0.0 167.3 jit_solution(17931211564896364628)
XLA Ops:
  0.6 0.8 copy-done.3
  1.5 3.5 %collective-permute-start = (bf16[24,1024]{1,0:T(8,128)(2,1)S(1)}, bf16[24,1024]{1,0:T(8,128)(2,1)S(1)}, u32[]{:S(2)}, u32[]{:S(2)}) collective-permute-start(bf16[24,1024]{1,0:T(8,128)(2,1)S(1)} %shard_map.49), channel_id=1, source_target_pairs={{0,0},{1,64},{2,128},{3,192},{64,1},{65,65},{66,129},{67,193},{128... | collective-permute-start | bytes 147464 | tf_op jit(solution)/shard_map/ppermute | solution.py:223
  5.0 1.5 copy-done
  6.5 1.6 shard_map.50
  8.5 33.1 %all_to_all.15.parts_ref.columns_ref = bf16[16,224,128]{2,1,0:T(8,128)(2,1)S(1)} all-to-all(bf16[16,224,128]{2,1,0:T(8,128)(2,1)S(1)} %shard_map.51), channel_id=1, replica_groups=mesh['dp_0'=4,'dp_1'=8,'dp_2'=2,'tensor'=4] {'dp_1','dp_2'}, dimensions={0} | all-to-all | bytes 1835008 | tf_op jit(solution)/shard_map/all_to_all | solution.py:229
  41.8 3.8 %all-to-all-start.1 = ((bf16[16,320,128]{2,1,0:T(8,128)(2,1)}), bf16[16,320,128]{2,1,0:T(8,128)(2,1)S(1)}, u32[]{:S(2)}, u32[]{:S(2)}) async-start(bf16[16,320,128]{2,1,0:T(8,128)(2,1)} %get-tuple-element.38), calls=%async_computation.1 | async-start | bytes 2621440 | tf_op jit(solution)/shard_map/all_to_all | solution.py:232
  45.7 6.1 %collective-permute-start.10 = (bf16[192,1024]{1,0:T(8,128)(2,1)S(1)}, bf16[192,1024]{1,0:T(8,128)(2,1)S(1)}, u32[]{:S(2)}, u32[]{:S(2)}) collective-permute-start(bf16[192,1024]{1,0:T(8,128)(2,1)S(1)} %get-tuple-element.32.refs_2_), channel_id=1, source_target_pairs={{0,3},{1,0},{2,1},{3,2},{4,7},{5,4},{6,5},{7,6},{8,11},{9,8},{10,9... | collective-permute-start | bytes 1179656 | tf_op jit(solution)/shard_map/ppermute | solution.py:209
  51.8 1.6 collective-permute-start.8
  53.3 1.7 %collective-permute-start.3 = (f32[8,128]{1,0:T(8,128)S(1)}, f32[8,128]{1,0:T(8,128)S(1)}, u32[]{:S(2)}, u32[]{:S(2)}) collective-permute-start(f32[8,128]{1,0:T(8,128)S(1)} %get-tuple-element.29), channel_id=1, source_target_pairs={{0,3},{1,0},{2,1},{3,2},{4,7},{5,4},{6,5},{7,6},{8,11},{9,8},{10,9... | collective-permute-start | bytes 12296 | tf_op jit(solution)/shard_map/ppermute | solution.py:209
  55.0 0.9 collective-permute-start.2
  55.9 13.9 %collective-permute-done.3 = f32[8,128]{1,0:T(8,128)S(1)} collective-permute-done((f32[8,128]{1,0:T(8,128)S(1)}, f32[8,128]{1,0:T(8,128)S(1)}, u32[]{:S(2)}, u32[]{:S(2)}) %collective-permute-start.3) | collective-permute-done | bytes 4128 | tf_op jit(solution)/shard_map/ppermute | solution.py:209
  69.7 1.6 collective-permute-start.1
  71.4 1.9 %collective-permute-done.2 = f32[8,128]{1,0:T(8,128)S(1)} collective-permute-done((f32[8,128]{1,0:T(8,128)S(1)}, f32[8,128]{1,0:T(8,128)S(1)}, u32[]{:S(2)}, u32[]{:S(2)}) %collective-permute-start.2) | collective-permute-done | bytes 4128 | tf_op jit(solution)/shard_map/ppermute | solution.py:209
  73.3 0.5 collective-permute-start.14
  73.9 0.4 collective-permute-start.12
  74.3 0.5 collective-permute-done.1
  74.9 2.0 %collective-permute-done.4.other_ref = f32[8,128]{1,0:T(8,128)S(1)} collective-permute-done((f32[8,128]{1,0:T(8,128)S(1)}, f32[8,128]{1,0:T(8,128)S(1)}, u32[]{:S(2)}, u32[]{:S(2)}) %collective-permute-start.4) | collective-permute-done | bytes 4128 | tf_op jit(solution)/shard_map/ppermute | solution.py:209
  76.8 0.5 collective-permute-start.7
  77.3 3.2 %collective-permute-done.7.mean_3 = f32[16,128]{1,0:T(8,128)S(1)} collective-permute-done((f32[16,128]{1,0:T(8,128)S(1)}, f32[16,128]{1,0:T(8,128)S(1)}, u32[]{:S(2)}, u32[]{:S(2)}) %collective-permute-start.7) | collective-permute-done | bytes 8224 | tf_op jit(solution)/shard_map/ppermute | solution.py:209
  80.7 3.5 %collective-permute-done.6.mean_2 = f32[16,128]{1,0:T(8,128)S(1)} collective-permute-done((f32[16,128]{1,0:T(8,128)S(1)}, f32[16,128]{1,0:T(8,128)S(1)}, u32[]{:S(2)}, u32[]{:S(2)}) %collective-permute-start.6) | collective-permute-done | bytes 8224 | tf_op jit(solution)/shard_map/ppermute | solution.py:209
  84.1 1.9 %collective-permute-start.5 = (f32[16,128]{1,0:T(8,128)S(1)}, f32[16,128]{1,0:T(8,128)S(1)}, u32[]{:S(2)}, u32[]{:S(2)}) collective-permute-start(f32[16,128]{1,0:T(8,128)S(1)} %shard_map.53.mean_0), channel_id=1, source_target_pairs={{0,128},{64,192},{128,0},{192,64},{1,129},{65,193},{129,1},{193,65... | collective-permute-start | bytes 24584 | tf_op jit(solution)/shard_map/ppermute | solution.py:209
  86.1 3.2 %collective-permute-done.5.mean_1 = f32[16,128]{1,0:T(8,128)S(1)} collective-permute-done((f32[16,128]{1,0:T(8,128)S(1)}, f32[16,128]{1,0:T(8,128)S(1)}, u32[]{:S(2)}, u32[]{:S(2)}) %collective-permute-start.5) | collective-permute-done | bytes 8224 | tf_op jit(solution)/shard_map/ppermute | solution.py:209
  89.3 0.3 shard_map.54
  89.6 3.7 %shard_map.55.refs_1_ = bf16[2,256,2048]{2,1,0:T(8,128)(2,1)S(1)} custom-call(bf16[16,224,128]{2,1,0:T(8,128)(2,1)S(1)} %all_to_all.15.parts_ref.columns_ref, f32[4,16,128]{2,1,0:T(8,128)S(1)} %get-tuple-element.30.scale_ref, f32[4,16,128]{2,1,0:T(8,128)S(1)} %get-tuple-element.31.inverse_ref), custom_call_target="tpu_custom_call" | custom-call | flops 1610612736 | tf_op jit(solution)/shard_map/pallas_call | solution.py:251
  93.4 4.3 %shard_map.56 = (bf16[2,4,16,768]{3,2,1,0:T(8,128)(2,1)S(1)}, bf16[2,4,16,768]{3,2,1,0:T(8,128)(2,1)}, bf16[2,4,16,768]{3,2,1,0:T(8,128)(2,1)S(1)}, bf16[2,4,16,768]{3,2,1,0:T(8,128)(2,1)}, bf16[768,2048]{1,0:T(8,128)(2,1)S(1)}) custom-call(s32[1]{0:T(128)} %bitcast.core_ref.refs_0_, bf16[2,256,2048]{2,1,0:T(8,128)(2,1)S(1)} %shard_map.55.refs_1_, ...), custom_call_target="tpu_custom_call" | custom-call | flops 805306368 | tf_op jit(solution)/shard_map/pallas_call | solution.py:252
  97.6 0.7 copy-done.1
  98.3 1.6 copy-done.4
  100.0 1.9 %collective-permute-start.15 = (bf16[2,4,16,768]{3,2,1,0:T(8,128)(2,1)S(1)}, bf16[2,4,16,768]{3,2,1,0:T(8,128)(2,1)S(1)}, u32[]{:S(2)}, u32[]{:S(2)}) collective-permute-start(bf16[2,4,16,768]{3,2,1,0:T(8,128)(2,1)S(1)} %get-tuple-element.34), channel_id=1, source_target_pairs={{0,128},{64,192},{128,0},{192,64},{1,129},{65,193},{129,1},{193,65... | collective-permute-start | bytes 589832 | tf_op jit(solution)/shard_map/ppermute | solution.py:209
  101.9 1.2 collective-permute-start.16
  103.1 0.8 collective-permute-start.17
  103.9 1.9 %copy-done.5 = bf16[768,2048]{1,0:T(8,128)(2,1)S(1)} copy-done((bf16[768,2048]{1,0:T(8,128)(2,1)S(1)}, bf16[768,2048]{1,0:T(8,128)(2,1)}, u32[]{:S(2)}) %copy-start.5) | copy-done | bytes 3145752
  105.8 8.3 %shard_map.57 = (bf16[3,4,16,768]{3,2,1,0:T(8,128)(2,1)S(1)}, bf16[3,4,16,768]{3,2,1,0:T(8,128)(2,1)}, bf16[3,4,16,768]{3,2,1,0:T(8,128)(2,1)}, bf16[3,4,16,768]{3,2,1,0:T(8,128)(2,1)}) custom-call(bf16[16,320,128]{2,1,0:T(8,128)(2,1)S(1)} %all-to-all-done.1.columns_ref, f32[4,16,128]{2,1,0:T(8,128)S(1)} %get-tuple-element.30.scale_ref, ...), custom_call_target="tpu_custom_call" | custom-call | flops 3623878656 | tf_op jit(solution)/shard_map/pallas_call | solution.py:257
  114.1 5.7 %shard_map.58 = (bf16[2,4,16,768]{3,2,1,0:T(8,128)(2,1)S(1)}, bf16[2,4,16,768]{3,2,1,0:T(8,128)(2,1)}, bf16[2,4,16,768]{3,2,1,0:T(8,128)(2,1)S(1)}, bf16[2,4,16,768]{3,2,1,0:T(8,128)(2,1)S(1)}) custom-call(bf16[16,320,128]{2,1,0:T(8,128)(2,1)S(1)} %all-to-all-done.1.columns_ref, f32[4,16,128]{2,1,0:T(8,128)S(1)} %get-tuple-element.30.scale_ref, ...), custom_call_target="tpu_custom_call" | custom-call | flops 2415919104 | tf_op jit(solution)/shard_map/pallas_call | solution.py:257
  119.8 1.6 collective-permute-start.21
  121.4 1.9 %collective-permute-start.18 = (bf16[3,4,16,768]{3,2,1,0:T(8,128)(2,1)}, bf16[3,4,16,768]{3,2,1,0:T(8,128)(2,1)S(1)}, u32[]{:S(2)}, u32[]{:S(2)}) collective-permute-start(bf16[3,4,16,768]{3,2,1,0:T(8,128)(2,1)} %get-tuple-element.42), channel_id=1, source_target_pairs={{0,128},{64,192},{128,0},{192,64},{1,129},{65,193},{129,1},{193,65... | collective-permute-start | bytes 884744 | tf_op jit(solution)/shard_map/ppermute | solution.py:209
  123.3 1.2 collective-permute-start.19
  124.5 0.8 collective-permute-start.20
  125.3 1.2 collective-permute-start.22
  126.5 2.5 %collective-permute-done.21.refs_9_ = bf16[2,4,16,768]{3,2,1,0:T(8,128)(2,1)S(1)} collective-permute-done((bf16[2,4,16,768]{3,2,1,0:T(8,128)(2,1)S(1)}, bf16[2,4,16,768]{3,2,1,0:T(8,128)(2,1)S(1)}, u32[]{:S(2)}, u32[]{:S(2)}) %collective-permute-start.21) | collective-permute-done | bytes 196640 | tf_op jit(solution)/shard_map/ppermute | solution.py:209
  129.0 1.6 collective-permute-start.23
  130.6 10.2 %collective-permute-done.22.refs_10_ = bf16[2,4,16,768]{3,2,1,0:T(8,128)(2,1)S(1)} collective-permute-done((bf16[2,4,16,768]{3,2,1,0:T(8,128)(2,1)}, bf16[2,4,16,768]{3,2,1,0:T(8,128)(2,1)S(1)}, u32[]{:S(2)}, u32[]{:S(2)}) %collective-permute-start.22) | collective-permute-done | bytes 196640 | tf_op jit(solution)/shard_map/ppermute | solution.py:209
  141.1 0.6 shard_map.59
  141.7 0.7 broadcast_in_dim.9
  142.5 11.7 %all-to-all-start.2 = ((f32[256,1,4]{2,1,0:T(1,128)}), f32[256,1,4]{2,1,0:T(1,128)S(1)}, u32[]{:S(2)}, u32[]{:S(2)}) async-start(f32[256,1,4]{2,1,0:T(1,128)} %broadcast_in_dim.9), calls=%async_computation.2 | async-start | bytes 262144 | tf_op jit(solution)/shard_map/all_to_all | solution.py:204
  154.2 0.6 broadcast_multiply_fusion
  154.8 0.6 dynamic_slice.3
  155.4 11.1 %all-to-all-done.2 = f32[256,1,4]{2,1,0:T(1,128)S(1)} async-done(((f32[256,1,4]{2,1,0:T(1,128)}), f32[256,1,4]{2,1,0:T(1,128)S(1)}, u32[]{:S(2)}, u32[]{:S(2)}) %all-to-all-start.2) | async-done | bytes 4128 | tf_op jit(solution)/shard_map/all_to_all | solution.py:204
  166.8 0.5 broadcast_multiply_fusion.1
  (34 shorter events, 1.6 us)
Async XLA Ops:
  0.6 0.8 copy-start.3
  1.5 6.9 %collective-permute-start = (bf16[24,1024]{1,0:T(8,128)(2,1)S(1)}, bf16[24,1024]{1,0:T(8,128)(2,1)S(1)}, u32[]{:S(2)}, u32[]{:S(2)}) collective-permute-start(bf16[24,1024]{1,0:T(8,128)(2,1)S(1)} %shard_map.49), channel_id=1, source_target_pairs={{0,0},{1,64},{2,128},{3,192},{64,1},{65,65},{66,129},{67,193},{128... | collective-permute-start | bytes 147464 | tf_op jit(solution)/shard_map/ppermute | solution.py:223
  5.0 1.5 copy-start
  41.8 62.1 %all-to-all-start.1 = ((bf16[16,320,128]{2,1,0:T(8,128)(2,1)}), bf16[16,320,128]{2,1,0:T(8,128)(2,1)S(1)}, u32[]{:S(2)}, u32[]{:S(2)}) async-start(bf16[16,320,128]{2,1,0:T(8,128)(2,1)} %get-tuple-element.38), calls=%async_computation.1 | async-start | bytes 2621440 | tf_op jit(solution)/shard_map/all_to_all | solution.py:232
  45.7 27.6 %collective-permute-start.10 = (bf16[192,1024]{1,0:T(8,128)(2,1)S(1)}, bf16[192,1024]{1,0:T(8,128)(2,1)S(1)}, u32[]{:S(2)}, u32[]{:S(2)}) collective-permute-start(bf16[192,1024]{1,0:T(8,128)(2,1)S(1)} %get-tuple-element.32.refs_2_), channel_id=1, source_target_pairs={{0,3},{1,0},{2,1},{3,2},{4,7},{5,4},{6,5},{7,6},{8,11},{9,8},{10,9... | collective-permute-start | bytes 1179656 | tf_op jit(solution)/shard_map/ppermute | solution.py:209
  51.8 22.0 %collective-permute-start.9 = (bf16[192,1024]{1,0:T(8,128)(2,1)S(1)}, bf16[192,1024]{1,0:T(8,128)(2,1)S(1)}, u32[]{:S(2)}, u32[]{:S(2)}) collective-permute-start(bf16[192,1024]{1,0:T(8,128)(2,1)S(1)} %get-tuple-element.32.refs_2_), channel_id=1, source_target_pairs={{0,1},{1,2},{2,3},{3,0},{4,5},{5,6},{6,7},{7,4},{8,9},{9,10},{10,1... | collective-permute-start | bytes 1179656 | tf_op jit(solution)/shard_map/ppermute | solution.py:209
  51.8 22.1 %collective-permute-start.8 = (bf16[192,1024]{1,0:T(8,128)(2,1)S(1)}, bf16[192,1024]{1,0:T(8,128)(2,1)}, u32[]{:S(2)}, u32[]{:S(2)}) collective-permute-start(bf16[192,1024]{1,0:T(8,128)(2,1)S(1)} %get-tuple-element.32.refs_2_), channel_id=1, source_target_pairs={{0,2},{1,3},{2,0},{3,1},{4,6},{5,7},{6,4},{7,5},{8,10},{9,11},{10,... | collective-permute-start | bytes 1179656 | tf_op jit(solution)/shard_map/ppermute | solution.py:209
  53.3 16.4 %collective-permute-start.3 = (f32[8,128]{1,0:T(8,128)S(1)}, f32[8,128]{1,0:T(8,128)S(1)}, u32[]{:S(2)}, u32[]{:S(2)}) collective-permute-start(f32[8,128]{1,0:T(8,128)S(1)} %get-tuple-element.29), channel_id=1, source_target_pairs={{0,3},{1,0},{2,1},{3,2},{4,7},{5,4},{6,5},{7,6},{8,11},{9,8},{10,9... | collective-permute-start | bytes 12296 | tf_op jit(solution)/shard_map/ppermute | solution.py:209
  55.0 18.3 %collective-permute-start.2 = (f32[8,128]{1,0:T(8,128)S(1)}, f32[8,128]{1,0:T(8,128)S(1)}, u32[]{:S(2)}, u32[]{:S(2)}) collective-permute-start(f32[8,128]{1,0:T(8,128)S(1)} %get-tuple-element.29), channel_id=1, source_target_pairs={{0,1},{1,2},{2,3},{3,0},{4,5},{5,6},{6,7},{7,4},{8,9},{9,10},{10,1... | collective-permute-start | bytes 12296 | tf_op jit(solution)/shard_map/ppermute | solution.py:209
  69.7 5.1 %collective-permute-start.1 = (f32[8,128]{1,0:T(8,128)S(1)}, f32[8,128]{1,0:T(8,128)S(1)}, u32[]{:S(2)}, u32[]{:S(2)}) collective-permute-start(f32[8,128]{1,0:T(8,128)S(1)} %get-tuple-element.29), channel_id=1, source_target_pairs={{0,2},{1,3},{2,0},{3,1},{4,6},{5,7},{6,4},{7,5},{8,10},{9,11},{10,... | collective-permute-start | bytes 12296 | tf_op jit(solution)/shard_map/ppermute | solution.py:209
  73.3 20.1 %collective-permute-start.11 = (bf16[192,1024]{1,0:T(8,128)(2,1)S(1)}, bf16[192,1024]{1,0:T(8,128)(2,1)}, u32[]{:S(2)}, u32[]{:S(2)}) collective-permute-start(bf16[192,1024]{1,0:T(8,128)(2,1)S(1)} %get-tuple-element.32.refs_2_), channel_id=1, source_target_pairs={{0,4},{4,0},{1,5},{5,1},{2,6},{6,2},{3,7},{7,3},{8,12},{12,8},{9,1... | collective-permute-start | bytes 1179656 | tf_op jit(solution)/shard_map/ppermute | solution.py:209
  73.3 20.1 %collective-permute-start.14 = (bf16[192,1024]{1,0:T(8,128)(2,1)S(1)}, bf16[192,1024]{1,0:T(8,128)(2,1)}, u32[]{:S(2)}, u32[]{:S(2)}) collective-permute-start(bf16[192,1024]{1,0:T(8,128)(2,1)S(1)} %collective-permute-done.10.refs_5_), channel_id=1, source_target_pairs={{0,4},{4,0},{1,5},{5,1},{2,6},{6,2},{3,7},{7,3},{8,12},{12,8},{9,1... | collective-permute-start | bytes 1179656 | tf_op jit(solution)/shard_map/ppermute | solution.py:209
  73.8 19.6 %collective-permute-start.13 = (bf16[192,1024]{1,0:T(8,128)(2,1)S(1)}, bf16[192,1024]{1,0:T(8,128)(2,1)}, u32[]{:S(2)}, u32[]{:S(2)}) collective-permute-start(bf16[192,1024]{1,0:T(8,128)(2,1)S(1)} %collective-permute-done.9.refs_4_), channel_id=1, source_target_pairs={{0,4},{4,0},{1,5},{5,1},{2,6},{6,2},{3,7},{7,3},{8,12},{12,8},{9,1... | collective-permute-start | bytes 1179656 | tf_op jit(solution)/shard_map/ppermute | solution.py:209
  73.9 19.5 %collective-permute-start.12 = (bf16[192,1024]{1,0:T(8,128)(2,1)}, bf16[192,1024]{1,0:T(8,128)(2,1)}, u32[]{:S(2)}, u32[]{:S(2)}) collective-permute-start(bf16[192,1024]{1,0:T(8,128)(2,1)} %collective-permute-done.8.refs_3_), channel_id=1, source_target_pairs={{0,4},{4,0},{1,5},{5,1},{2,6},{6,2},{3,7},{7,3},{8,12},{12,8},{9,1... | collective-permute-start | bytes 1179656 | tf_op jit(solution)/shard_map/ppermute | solution.py:209
  74.9 2.0 %collective-permute-start.4 = (f32[8,128]{1,0:T(8,128)S(1)}, f32[8,128]{1,0:T(8,128)S(1)}, u32[]{:S(2)}, u32[]{:S(2)}) collective-permute-start(f32[8,128]{1,0:T(8,128)S(1)} %add_add_fusion.own_ref), channel_id=1, source_target_pairs={{0,4},{4,0},{1,5},{5,1},{2,6},{6,2},{3,7},{7,3},{8,12},{12,8},{9,1... | collective-permute-start | bytes 12296 | tf_op jit(solution)/shard_map/ppermute | solution.py:209
  76.8 3.7 %collective-permute-start.7 = (f32[16,128]{1,0:T(8,128)S(1)}, f32[16,128]{1,0:T(8,128)S(1)}, u32[]{:S(2)}, u32[]{:S(2)}) collective-permute-start(f32[16,128]{1,0:T(8,128)S(1)} %shard_map.53.mean_0), channel_id=1, source_target_pairs={{0,192},{64,0},{128,64},{192,128},{1,193},{65,1},{129,65},{193,129... | collective-permute-start | bytes 24584 | tf_op jit(solution)/shard_map/ppermute | solution.py:209
  80.5 3.7 %collective-permute-start.6 = (f32[16,128]{1,0:T(8,128)S(1)}, f32[16,128]{1,0:T(8,128)S(1)}, u32[]{:S(2)}, u32[]{:S(2)}) collective-permute-start(f32[16,128]{1,0:T(8,128)S(1)} %shard_map.53.mean_0), channel_id=1, source_target_pairs={{0,64},{64,128},{128,192},{192,0},{1,65},{65,129},{129,193},{193,1... | collective-permute-start | bytes 24584 | tf_op jit(solution)/shard_map/ppermute | solution.py:209
  84.1 5.2 %collective-permute-start.5 = (f32[16,128]{1,0:T(8,128)S(1)}, f32[16,128]{1,0:T(8,128)S(1)}, u32[]{:S(2)}, u32[]{:S(2)}) collective-permute-start(f32[16,128]{1,0:T(8,128)S(1)} %shard_map.53.mean_0), channel_id=1, source_target_pairs={{0,128},{64,192},{128,0},{192,64},{1,129},{65,193},{129,1},{193,65... | collective-permute-start | bytes 24584 | tf_op jit(solution)/shard_map/ppermute | solution.py:209
  97.6 0.7 copy-start.1
  98.3 1.6 copy-start.4
  100.0 23.3 %collective-permute-start.15 = (bf16[2,4,16,768]{3,2,1,0:T(8,128)(2,1)S(1)}, bf16[2,4,16,768]{3,2,1,0:T(8,128)(2,1)S(1)}, u32[]{:S(2)}, u32[]{:S(2)}) collective-permute-start(bf16[2,4,16,768]{3,2,1,0:T(8,128)(2,1)S(1)} %get-tuple-element.34), channel_id=1, source_target_pairs={{0,128},{64,192},{128,0},{192,64},{1,129},{65,193},{129,1},{193,65... | collective-permute-start | bytes 589832 | tf_op jit(solution)/shard_map/ppermute | solution.py:209
  101.9 22.6 %collective-permute-start.16 = (bf16[2,4,16,768]{3,2,1,0:T(8,128)(2,1)}, bf16[2,4,16,768]{3,2,1,0:T(8,128)(2,1)S(1)}, u32[]{:S(2)}, u32[]{:S(2)}) collective-permute-start(bf16[2,4,16,768]{3,2,1,0:T(8,128)(2,1)} %get-tuple-element.35), channel_id=1, source_target_pairs={{0,64},{64,128},{128,192},{192,0},{1,65},{65,129},{129,193},{193,1... | collective-permute-start | bytes 589832 | tf_op jit(solution)/shard_map/ppermute | solution.py:209
  103.1 22.2 %collective-permute-start.17 = (bf16[2,4,16,768]{3,2,1,0:T(8,128)(2,1)}, bf16[2,4,16,768]{3,2,1,0:T(8,128)(2,1)S(1)}, u32[]{:S(2)}, u32[]{:S(2)}) collective-permute-start(bf16[2,4,16,768]{3,2,1,0:T(8,128)(2,1)} %get-tuple-element.36), channel_id=1, source_target_pairs={{0,192},{64,0},{128,64},{192,128},{1,193},{65,1},{129,65},{193,129... | collective-permute-start | bytes 589832 | tf_op jit(solution)/shard_map/ppermute | solution.py:209
  103.9 1.9 %copy-start.5 = (bf16[768,2048]{1,0:T(8,128)(2,1)S(1)}, bf16[768,2048]{1,0:T(8,128)(2,1)}, u32[]{:S(2)}) copy-start(bf16[768,2048]{1,0:T(8,128)(2,1)} %copy-done.4) | copy-start | bytes 9437188
  114.1 27.0 %copy-start.2 = (bf16[2,4,16,768]{3,2,1,0:T(8,128)(2,1)S(1)}, bf16[2,4,16,768]{3,2,1,0:T(8,128)(2,1)}, u32[]{:S(2)}) copy-start(bf16[2,4,16,768]{3,2,1,0:T(8,128)(2,1)} %copy-done.1) | copy-start | bytes 589828
  119.8 9.3 %collective-permute-start.21 = (bf16[2,4,16,768]{3,2,1,0:T(8,128)(2,1)S(1)}, bf16[2,4,16,768]{3,2,1,0:T(8,128)(2,1)S(1)}, u32[]{:S(2)}, u32[]{:S(2)}) collective-permute-start(bf16[2,4,16,768]{3,2,1,0:T(8,128)(2,1)S(1)} %get-tuple-element.47), channel_id=1, source_target_pairs={{0,128},{64,192},{128,0},{192,64},{1,129},{65,193},{129,1},{193,65... | collective-permute-start | bytes 589832 | tf_op jit(solution)/shard_map/ppermute | solution.py:209
  121.4 19.8 %collective-permute-start.18 = (bf16[3,4,16,768]{3,2,1,0:T(8,128)(2,1)}, bf16[3,4,16,768]{3,2,1,0:T(8,128)(2,1)S(1)}, u32[]{:S(2)}, u32[]{:S(2)}) collective-permute-start(bf16[3,4,16,768]{3,2,1,0:T(8,128)(2,1)} %get-tuple-element.42), channel_id=1, source_target_pairs={{0,128},{64,192},{128,0},{192,64},{1,129},{65,193},{129,1},{193,65... | collective-permute-start | bytes 884744 | tf_op jit(solution)/shard_map/ppermute | solution.py:209
  123.3 17.8 %collective-permute-start.19 = (bf16[3,4,16,768]{3,2,1,0:T(8,128)(2,1)}, bf16[3,4,16,768]{3,2,1,0:T(8,128)(2,1)S(1)}, u32[]{:S(2)}, u32[]{:S(2)}) collective-permute-start(bf16[3,4,16,768]{3,2,1,0:T(8,128)(2,1)} %get-tuple-element.43), channel_id=1, source_target_pairs={{0,64},{64,128},{128,192},{192,0},{1,65},{65,129},{129,193},{193,1... | collective-permute-start | bytes 884744 | tf_op jit(solution)/shard_map/ppermute | solution.py:209
  124.5 16.6 %collective-permute-start.20 = (bf16[3,4,16,768]{3,2,1,0:T(8,128)(2,1)}, bf16[3,4,16,768]{3,2,1,0:T(8,128)(2,1)S(1)}, u32[]{:S(2)}, u32[]{:S(2)}) collective-permute-start(bf16[3,4,16,768]{3,2,1,0:T(8,128)(2,1)} %get-tuple-element.44), channel_id=1, source_target_pairs={{0,192},{64,0},{128,64},{192,128},{1,193},{65,1},{129,65},{193,129... | collective-permute-start | bytes 884744 | tf_op jit(solution)/shard_map/ppermute | solution.py:209
  125.3 15.5 %collective-permute-start.22 = (bf16[2,4,16,768]{3,2,1,0:T(8,128)(2,1)}, bf16[2,4,16,768]{3,2,1,0:T(8,128)(2,1)S(1)}, u32[]{:S(2)}, u32[]{:S(2)}) collective-permute-start(bf16[2,4,16,768]{3,2,1,0:T(8,128)(2,1)} %get-tuple-element.48), channel_id=1, source_target_pairs={{0,64},{64,128},{128,192},{192,0},{1,65},{65,129},{129,193},{193,1... | collective-permute-start | bytes 589832 | tf_op jit(solution)/shard_map/ppermute | solution.py:209
  129.0 12.1 %collective-permute-start.23 = (bf16[2,4,16,768]{3,2,1,0:T(8,128)(2,1)S(1)}, bf16[2,4,16,768]{3,2,1,0:T(8,128)(2,1)S(1)}, u32[]{:S(2)}, u32[]{:S(2)}) collective-permute-start(bf16[2,4,16,768]{3,2,1,0:T(8,128)(2,1)S(1)} %get-tuple-element.49), channel_id=1, source_target_pairs={{0,192},{64,0},{128,64},{192,128},{1,193},{65,1},{129,65},{193,129... | collective-permute-start | bytes 589832 | tf_op jit(solution)/shard_map/ppermute | solution.py:209
  142.5 24.0 %all-to-all-start.2 = ((f32[256,1,4]{2,1,0:T(1,128)}), f32[256,1,4]{2,1,0:T(1,128)S(1)}, u32[]{:S(2)}, u32[]{:S(2)}) async-start(f32[256,1,4]{2,1,0:T(1,128)} %broadcast_in_dim.9), calls=%async_computation.2 | async-start | bytes 262144 | tf_op jit(solution)/shard_map/all_to_all | solution.py:204

commit v6 on v5

--- a/solution.py
+++ b/solution.py
@@ -144,26 +144,33 @@
 def first_kernel(units):
     def body(*refs):
         core_ref, deltas, own, other = refs[0], refs[1], refs[2:6], refs[6:10]
-        out_refs, tokens = refs[10:14], refs[14]
+        out_refs, kept, tokens, done = refs[10:14], *refs[14:]
         at_own = pl.multiple_of(core_ref[0] * HALF, HALF)
         at_other = pl.multiple_of((1 - core_ref[0]) * HALF, HALF)
         count = TOKENS // NY
         for at in range(NY):
             tokens[at * count : (at + 1) * count, pl.ds(at_own, HALF)] = own[at][...]
             tokens[at * count : (at + 1) * count, pl.ds(at_other, HALF)] = other[at][...]
+        keep = pltpu.make_async_copy(tokens, kept, done)
+        keep.start()
         for unit in range(units):
             multiply(deltas.at[unit], tokens, out_refs, unit)
+        keep.wait()
 
     return body
 
 
 def piece_kernel(first, units):
-    def body(columns_ref, scale_ref, inverse_ref, tokens, *refs):
-        out_refs, deltas = refs[:NX], refs[NX:]
+    def body(columns_ref, scale_ref, inverse_ref, kept, *refs):
+        out_refs, (tokens, done), deltas = refs[:NX], refs[NX : NX + 2], refs[NX + 2 :]
+        fetch = pltpu.make_async_copy(kept, tokens, done)
+        fetch.start()
         for unit in range(units):
             delta = deltas[unit % 2]
             rows = slice((first + unit) * UNIT, (first + unit + 1) * UNIT)
             quantize(columns_ref, rows, scale_ref, inverse_ref, delta)
+            if unit == 0:
+                fetch.wait()
             multiply(delta, tokens, out_refs, unit)
 
     return body
@@ -242,6 +249,8 @@
     parts = [joined] + [shifted(joined, "tensor", hops) for hops in (2, 1, 3)]
     parts += [shifted(part, "dp_2", 1) for part in parts]
 
+    far = pl.BlockSpec(memory_space=pltpu.HBM)
+    gathered = [pltpu.VMEM((TOKENS, BLOCK), bf16), pltpu.SemaphoreType.DMA]
     shares = []
     for at, (source, first, units) in enumerate(PIECES):
         out_shape = [array((units, GRID, ROWS, TOKENS), bf16)] * NX
@@ -250,16 +259,19 @@
             quantized = array((units, GRID * UNIT, BLOCK), bf16)
             deltas = kernel(quantize_kernel, quantized, flops=2 * work)(received[0], scale, inverse)
             *partial, tokens = kernel(
-                first_kernel(units), out_shape + [array((TOKENS, BLOCK), bf16)], flops=work,
+                first_kernel(units), out_shape + [pltpu.HBM((TOKENS, BLOCK), bf16)], flops=work,
                 in_specs=[smem] + [local] * 9,
+                out_specs=[local] * NX + [far],
+                scratch_shapes=gathered,
             )(core, deltas, *parts)
         else:
             partial = kernel(
                 piece_kernel(first, units),
                 out_shape,
                 flops=3 * work,
-                scratch_shapes=[pltpu.VMEM((GRID * UNIT, BLOCK), bf16)] * min(units, 2),
-            )(after(received[source], shares[-NX]), scale, inverse, tokens)
+                in_specs=[local] * 3 + [far],
+                scratch_shapes=gathered + [pltpu.VMEM((GRID * UNIT, BLOCK), bf16)] * min(units, 2),
+            )(after(received[source], shares[-NX]), scale, inverse, pltpu.with_memory_space_constraint(tokens, pltpu.HBM))
         shares += [partial[0]] + [shifted(partial[hops], "dp_0", hops) for hops in (2, 1, 3)]
     sums, totals = kernel(error_kernel, [array((GRID, UNITS * ROWS), f32), array((1, GRID), f32)])(*shares)
     own_mean = lax.dynamic_slice_in_dim(after(mean, sums).reshape(-1), lax.axis_index(ZC) * GROUP, GROUP)

time: 169 us -> 166 us (0.982)
  local copies, waits for them, and re-layouts: 7.87 us -> 4.34 us
    unnamed x12 -> x8, local copies, waits for them, and re-layouts: 6.54 us -> 3.01 us
  transfers between devices with their start and end apart: 26 -> 26, of which waited for: 12 -> 12; matrix products, arithmetic and copies ran while one was open for 1% -> 1% of each run, Pallas kernels for 14% -> 15%
where the time goes in v6:
time: 166 us; the launch traced here: 165 us
  waiting for transfers between devices  52.6 us (32%)
  starting transfers between devices  46.9 us (28%)
  blocking collectives  33.1 us (20%)
  Pallas kernels  25.4 us (15%)
  local copies, waits for them, and re-layouts  4.34 us (3%)
    ppermute x23, waiting for transfers between devices, shifted(): lax.ppermute(value, axis, [(i, (i + hops) % size) for i in range(size)])  41.1 us
    all_to_all x1, blocking collectives, search(): received = [lax.all_to_all(merged, ZC, 0, 0, tiled=True)]  33.1 us
    ppermute x23, starting transfers between devices, shifted(): lax.ppermute(value, axis, [(i, (i + hops) % size) for i in range(size)])  27.9 us
    pallas_call x2, Pallas kernels, search(): kernel(piece_kernel(first, units), out_shape, flops=3 * work, in_specs=[l...  14.5 us
    all_to_all x1, starting transfers between devices, spread(): return lax.all_to_all(wide, axes, 0, 0, tiled=True)  11.7 us
    all_to_all x1, waiting for transfers between devices, spread(): return lax.all_to_all(wide, axes, 0, 0, tiled=True)  11.1 us
    pallas_call x1, Pallas kernels, search(): kernel(first_kernel(units), out_shape + [pltpu.HBM((TOKENS, BLOCK), bf16)...  4.36 us
    all_to_all x1, starting transfers between devices, search(): lax.all_to_all(after(columns[1], joined), ZC, 0, 0, tiled=True)  3.84 us
  transfers between devices with their start and end apart: 26, of which 12 were waited for; matrix products, arithmetic and copies ran while one was open for 1% of the time, Pallas kernels for 15%

profile of v6, /device:TPU:2, one launch (start us, length us, event | category | flops | bytes accessed | tf_op | source)
XLA Modules:
  0.0 164.5 jit_solution(14992115484936869097)
XLA Ops:
  0.6 0.8 copy-done.3
  1.5 3.5 %collective-permute-start = (bf16[24,1024]{1,0:T(8,128)(2,1)S(1)}, bf16[24,1024]{1,0:T(8,128)(2,1)S(1)}, u32[]{:S(2)}, u32[]{:S(2)}) collective-permute-start(bf16[24,1024]{1,0:T(8,128)(2,1)S(1)} %shard_map.49), channel_id=1, source_target_pairs={{0,0},{1,64},{2,128},{3,192},{64,1},{65,65},{66,129},{67,193},{128... | collective-permute-start | bytes 147464 | tf_op jit(solution)/shard_map/ppermute | solution.py:230
  5.0 1.5 copy-done
  6.5 1.6 shard_map.50
  8.0 0.3 collective-permute-done.tokens_ref
  8.5 33.1 %all_to_all.15.parts_ref.columns_ref = bf16[16,224,128]{2,1,0:T(8,128)(2,1)S(1)} all-to-all(bf16[16,224,128]{2,1,0:T(8,128)(2,1)S(1)} %shard_map.51), channel_id=1, replica_groups=mesh['dp_0'=4,'dp_1'=8,'dp_2'=2,'tensor'=4] {'dp_1','dp_2'}, dimensions={0} | all-to-all | bytes 1835008 | tf_op jit(solution)/shard_map/all_to_all | solution.py:236
  41.8 3.8 %all-to-all-start.1 = ((bf16[16,320,128]{2,1,0:T(8,128)(2,1)}), bf16[16,320,128]{2,1,0:T(8,128)(2,1)S(1)}, u32[]{:S(2)}, u32[]{:S(2)}) async-start(bf16[16,320,128]{2,1,0:T(8,128)(2,1)} %get-tuple-element.38), calls=%async_computation.1 | async-start | bytes 2621440 | tf_op jit(solution)/shard_map/all_to_all | solution.py:239
  45.7 6.1 %collective-permute-start.10 = (bf16[192,1024]{1,0:T(8,128)(2,1)S(1)}, bf16[192,1024]{1,0:T(8,128)(2,1)S(1)}, u32[]{:S(2)}, u32[]{:S(2)}) collective-permute-start(bf16[192,1024]{1,0:T(8,128)(2,1)S(1)} %get-tuple-element.32.refs_2_), channel_id=1, source_target_pairs={{0,3},{1,0},{2,1},{3,2},{4,7},{5,4},{6,5},{7,6},{8,11},{9,8},{10,9... | collective-permute-start | bytes 1179656 | tf_op jit(solution)/shard_map/ppermute | solution.py:216
  51.8 1.6 collective-permute-start.8
  53.3 1.7 %collective-permute-start.3 = (f32[8,128]{1,0:T(8,128)S(1)}, f32[8,128]{1,0:T(8,128)S(1)}, u32[]{:S(2)}, u32[]{:S(2)}) collective-permute-start(f32[8,128]{1,0:T(8,128)S(1)} %get-tuple-element.29), channel_id=1, source_target_pairs={{0,3},{1,0},{2,1},{3,2},{4,7},{5,4},{6,5},{7,6},{8,11},{9,8},{10,9... | collective-permute-start | bytes 12296 | tf_op jit(solution)/shard_map/ppermute | solution.py:216
  55.0 0.9 collective-permute-start.2
  55.9 13.9 %collective-permute-done.3 = f32[8,128]{1,0:T(8,128)S(1)} collective-permute-done((f32[8,128]{1,0:T(8,128)S(1)}, f32[8,128]{1,0:T(8,128)S(1)}, u32[]{:S(2)}, u32[]{:S(2)}) %collective-permute-start.3) | collective-permute-done | bytes 4128 | tf_op jit(solution)/shard_map/ppermute | solution.py:216
  69.7 1.6 collective-permute-start.1
  71.4 1.9 %collective-permute-done.2 = f32[8,128]{1,0:T(8,128)S(1)} collective-permute-done((f32[8,128]{1,0:T(8,128)S(1)}, f32[8,128]{1,0:T(8,128)S(1)}, u32[]{:S(2)}, u32[]{:S(2)}) %collective-permute-start.2) | collective-permute-done | bytes 4128 | tf_op jit(solution)/shard_map/ppermute | solution.py:216
  73.3 0.5 collective-permute-start.14
  73.9 0.4 collective-permute-start.12
  74.3 0.5 collective-permute-done.1
  74.9 2.0 %collective-permute-done.4.other_ref = f32[8,128]{1,0:T(8,128)S(1)} collective-permute-done((f32[8,128]{1,0:T(8,128)S(1)}, f32[8,128]{1,0:T(8,128)S(1)}, u32[]{:S(2)}, u32[]{:S(2)}) %collective-permute-start.4) | collective-permute-done | bytes 4128 | tf_op jit(solution)/shard_map/ppermute | solution.py:216
  76.8 0.5 collective-permute-start.7
  77.3 3.2 %collective-permute-done.7.mean_3 = f32[16,128]{1,0:T(8,128)S(1)} collective-permute-done((f32[16,128]{1,0:T(8,128)S(1)}, f32[16,128]{1,0:T(8,128)S(1)}, u32[]{:S(2)}, u32[]{:S(2)}) %collective-permute-start.7) | collective-permute-done | bytes 8224 | tf_op jit(solution)/shard_map/ppermute | solution.py:216
  80.7 3.5 %collective-permute-done.6.mean_2 = f32[16,128]{1,0:T(8,128)S(1)} collective-permute-done((f32[16,128]{1,0:T(8,128)S(1)}, f32[16,128]{1,0:T(8,128)S(1)}, u32[]{:S(2)}, u32[]{:S(2)}) %collective-permute-start.6) | collective-permute-done | bytes 8224 | tf_op jit(solution)/shard_map/ppermute | solution.py:216
  84.1 1.9 %collective-permute-start.5 = (f32[16,128]{1,0:T(8,128)S(1)}, f32[16,128]{1,0:T(8,128)S(1)}, u32[]{:S(2)}, u32[]{:S(2)}) collective-permute-start(f32[16,128]{1,0:T(8,128)S(1)} %shard_map.53.mean_0), channel_id=1, source_target_pairs={{0,128},{64,192},{128,0},{192,64},{1,129},{65,193},{129,1},{193,65... | collective-permute-start | bytes 24584 | tf_op jit(solution)/shard_map/ppermute | solution.py:216
  86.1 3.2 %collective-permute-done.5.mean_1 = f32[16,128]{1,0:T(8,128)S(1)} collective-permute-done((f32[16,128]{1,0:T(8,128)S(1)}, f32[16,128]{1,0:T(8,128)S(1)}, u32[]{:S(2)}, u32[]{:S(2)}) %collective-permute-start.5) | collective-permute-done | bytes 8224 | tf_op jit(solution)/shard_map/ppermute | solution.py:216
  89.3 0.3 shard_map.54
  89.6 3.7 %shard_map.55.refs_1_ = bf16[2,256,2048]{2,1,0:T(8,128)(2,1)S(1)} custom-call(bf16[16,224,128]{2,1,0:T(8,128)(2,1)S(1)} %all_to_all.15.parts_ref.columns_ref, f32[4,16,128]{2,1,0:T(8,128)S(1)} %get-tuple-element.30.scale_ref, f32[4,16,128]{2,1,0:T(8,128)S(1)} %get-tuple-element.31.inverse_ref), custom_call_target="tpu_custom_call" | custom-call | flops 1610612736 | tf_op jit(solution)/shard_map/pallas_call | solution.py:260
  93.4 4.4 %shard_map.56 = (bf16[2,4,16,768]{3,2,1,0:T(8,128)(2,1)S(1)}, bf16[2,4,16,768]{3,2,1,0:T(8,128)(2,1)}, bf16[2,4,16,768]{3,2,1,0:T(8,128)(2,1)S(1)}, bf16[2,4,16,768]{3,2,1,0:T(8,128)(2,1)}, bf16[768,2048]{1,0:T(8,128)(2,1)}) custom-call(s32[1]{0:T(128)} %bitcast.core_ref.refs_0_, bf16[2,256,2048]{2,1,0:T(8,128)(2,1)S(1)} %shard_map.55.refs_1_, ...), custom_call_target="tpu_custom_call" | custom-call | flops 805306368 | tf_op jit(solution)/shard_map/pallas_call | solution.py:261
  97.8 0.7 copy-done.1
  98.4 1.9 %collective-permute-start.15 = (bf16[2,4,16,768]{3,2,1,0:T(8,128)(2,1)S(1)}, bf16[2,4,16,768]{3,2,1,0:T(8,128)(2,1)S(1)}, u32[]{:S(2)}, u32[]{:S(2)}) collective-permute-start(bf16[2,4,16,768]{3,2,1,0:T(8,128)(2,1)S(1)} %get-tuple-element.34), channel_id=1, source_target_pairs={{0,128},{64,192},{128,0},{192,64},{1,129},{65,193},{129,1},{193,65... | collective-permute-start | bytes 589832 | tf_op jit(solution)/shard_map/ppermute | solution.py:216
  100.4 1.2 collective-permute-start.16
  101.6 0.8 collective-permute-start.17
  102.4 8.6 %shard_map.57 = (bf16[3,4,16,768]{3,2,1,0:T(8,128)(2,1)S(1)}, bf16[3,4,16,768]{3,2,1,0:T(8,128)(2,1)}, bf16[3,4,16,768]{3,2,1,0:T(8,128)(2,1)}, bf16[3,4,16,768]{3,2,1,0:T(8,128)(2,1)}) custom-call(bf16[16,320,128]{2,1,0:T(8,128)(2,1)S(1)} %all-to-all-done.1.columns_ref, f32[4,16,128]{2,1,0:T(8,128)S(1)} %get-tuple-element.30.scale_ref, ...), custom_call_target="tpu_custom_call" | custom-call | flops 3623878656 | tf_op jit(solution)/shard_map/pallas_call | solution.py:268
  111.0 5.9 %shard_map.58 = (bf16[2,4,16,768]{3,2,1,0:T(8,128)(2,1)S(1)}, bf16[2,4,16,768]{3,2,1,0:T(8,128)(2,1)}, bf16[2,4,16,768]{3,2,1,0:T(8,128)(2,1)S(1)}, bf16[2,4,16,768]{3,2,1,0:T(8,128)(2,1)S(1)}) custom-call(bf16[16,320,128]{2,1,0:T(8,128)(2,1)S(1)} %all-to-all-done.1.columns_ref, f32[4,16,128]{2,1,0:T(8,128)S(1)} %get-tuple-element.30.scale_ref, ...), custom_call_target="tpu_custom_call" | custom-call | flops 2415919104 | tf_op jit(solution)/shard_map/pallas_call | solution.py:268
  116.9 1.7 %collective-permute-start.21 = (bf16[2,4,16,768]{3,2,1,0:T(8,128)(2,1)S(1)}, bf16[2,4,16,768]{3,2,1,0:T(8,128)(2,1)S(1)}, u32[]{:S(2)}, u32[]{:S(2)}) collective-permute-start(bf16[2,4,16,768]{3,2,1,0:T(8,128)(2,1)S(1)} %get-tuple-element.47), channel_id=1, source_target_pairs={{0,128},{64,192},{128,0},{192,64},{1,129},{65,193},{129,1},{193,65... | collective-permute-start | bytes 589832 | tf_op jit(solution)/shard_map/ppermute | solution.py:216
  118.6 1.9 %collective-permute-start.18 = (bf16[3,4,16,768]{3,2,1,0:T(8,128)(2,1)}, bf16[3,4,16,768]{3,2,1,0:T(8,128)(2,1)S(1)}, u32[]{:S(2)}, u32[]{:S(2)}) collective-permute-start(bf16[3,4,16,768]{3,2,1,0:T(8,128)(2,1)} %get-tuple-element.42), channel_id=1, source_target_pairs={{0,128},{64,192},{128,0},{192,64},{1,129},{65,193},{129,1},{193,65... | collective-permute-start | bytes 884744 | tf_op jit(solution)/shard_map/ppermute | solution.py:216
  120.5 1.2 collective-permute-start.19
  121.7 0.8 collective-permute-start.20
  122.6 1.2 collective-permute-start.22
  123.8 2.5 %collective-permute-done.21.refs_9_ = bf16[2,4,16,768]{3,2,1,0:T(8,128)(2,1)S(1)} collective-permute-done((bf16[2,4,16,768]{3,2,1,0:T(8,128)(2,1)S(1)}, bf16[2,4,16,768]{3,2,1,0:T(8,128)(2,1)S(1)}, u32[]{:S(2)}, u32[]{:S(2)}) %collective-permute-start.21) | collective-permute-done | bytes 196640 | tf_op jit(solution)/shard_map/ppermute | solution.py:216
  126.3 1.6 collective-permute-start.23
  127.9 10.1 %collective-permute-done.22.refs_10_ = bf16[2,4,16,768]{3,2,1,0:T(8,128)(2,1)S(1)} collective-permute-done((bf16[2,4,16,768]{3,2,1,0:T(8,128)(2,1)}, bf16[2,4,16,768]{3,2,1,0:T(8,128)(2,1)S(1)}, u32[]{:S(2)}, u32[]{:S(2)}) %collective-permute-start.22) | collective-permute-done | bytes 196640 | tf_op jit(solution)/shard_map/ppermute | solution.py:216
  138.0 0.3 collective-permute-done.23.refs_11_
  138.4 0.6 shard_map.59
  139.0 0.7 broadcast_in_dim.9
  139.7 11.7 %all-to-all-start.2 = ((f32[256,1,4]{2,1,0:T(1,128)}), f32[256,1,4]{2,1,0:T(1,128)S(1)}, u32[]{:S(2)}, u32[]{:S(2)}) async-start(f32[256,1,4]{2,1,0:T(1,128)} %broadcast_in_dim.9), calls=%async_computation.2 | async-start | bytes 262144 | tf_op jit(solution)/shard_map/all_to_all | solution.py:211
  151.4 0.6 broadcast_multiply_fusion
  152.0 0.6 dynamic_slice.3
  152.6 11.1 %all-to-all-done.2 = f32[256,1,4]{2,1,0:T(1,128)S(1)} async-done(((f32[256,1,4]{2,1,0:T(1,128)}), f32[256,1,4]{2,1,0:T(1,128)S(1)}, u32[]{:S(2)}, u32[]{:S(2)}) %all-to-all-start.2) | async-done | bytes 4128 | tf_op jit(solution)/shard_map/all_to_all | solution.py:211
  164.0 0.5 broadcast_multiply_fusion.1
  (30 shorter events, 0.9 us)
Async XLA Ops:
  0.6 0.8 copy-start.3
  1.5 6.9 %collective-permute-start = (bf16[24,1024]{1,0:T(8,128)(2,1)S(1)}, bf16[24,1024]{1,0:T(8,128)(2,1)S(1)}, u32[]{:S(2)}, u32[]{:S(2)}) collective-permute-start(bf16[24,1024]{1,0:T(8,128)(2,1)S(1)} %shard_map.49), channel_id=1, source_target_pairs={{0,0},{1,64},{2,128},{3,192},{64,1},{65,65},{66,129},{67,193},{128... | collective-permute-start | bytes 147464 | tf_op jit(solution)/shard_map/ppermute | solution.py:230
  5.0 1.5 copy-start
  41.8 60.6 %all-to-all-start.1 = ((bf16[16,320,128]{2,1,0:T(8,128)(2,1)}), bf16[16,320,128]{2,1,0:T(8,128)(2,1)S(1)}, u32[]{:S(2)}, u32[]{:S(2)}) async-start(bf16[16,320,128]{2,1,0:T(8,128)(2,1)} %get-tuple-element.38), calls=%async_computation.1 | async-start | bytes 2621440 | tf_op jit(solution)/shard_map/all_to_all | solution.py:239
  45.7 27.6 %collective-permute-start.10 = (bf16[192,1024]{1,0:T(8,128)(2,1)S(1)}, bf16[192,1024]{1,0:T(8,128)(2,1)S(1)}, u32[]{:S(2)}, u32[]{:S(2)}) collective-permute-start(bf16[192,1024]{1,0:T(8,128)(2,1)S(1)} %get-tuple-element.32.refs_2_), channel_id=1, source_target_pairs={{0,3},{1,0},{2,1},{3,2},{4,7},{5,4},{6,5},{7,6},{8,11},{9,8},{10,9... | collective-permute-start | bytes 1179656 | tf_op jit(solution)/shard_map/ppermute | solution.py:216
  51.8 22.0 %collective-permute-start.9 = (bf16[192,1024]{1,0:T(8,128)(2,1)S(1)}, bf16[192,1024]{1,0:T(8,128)(2,1)S(1)}, u32[]{:S(2)}, u32[]{:S(2)}) collective-permute-start(bf16[192,1024]{1,0:T(8,128)(2,1)S(1)} %get-tuple-element.32.refs_2_), channel_id=1, source_target_pairs={{0,1},{1,2},{2,3},{3,0},{4,5},{5,6},{6,7},{7,4},{8,9},{9,10},{10,1... | collective-permute-start | bytes 1179656 | tf_op jit(solution)/shard_map/ppermute | solution.py:216
  51.8 22.1 %collective-permute-start.8 = (bf16[192,1024]{1,0:T(8,128)(2,1)S(1)}, bf16[192,1024]{1,0:T(8,128)(2,1)}, u32[]{:S(2)}, u32[]{:S(2)}) collective-permute-start(bf16[192,1024]{1,0:T(8,128)(2,1)S(1)} %get-tuple-element.32.refs_2_), channel_id=1, source_target_pairs={{0,2},{1,3},{2,0},{3,1},{4,6},{5,7},{6,4},{7,5},{8,10},{9,11},{10,... | collective-permute-start | bytes 1179656 | tf_op jit(solution)/shard_map/ppermute | solution.py:216
  53.3 16.4 %collective-permute-start.3 = (f32[8,128]{1,0:T(8,128)S(1)}, f32[8,128]{1,0:T(8,128)S(1)}, u32[]{:S(2)}, u32[]{:S(2)}) collective-permute-start(f32[8,128]{1,0:T(8,128)S(1)} %get-tuple-element.29), channel_id=1, source_target_pairs={{0,3},{1,0},{2,1},{3,2},{4,7},{5,4},{6,5},{7,6},{8,11},{9,8},{10,9... | collective-permute-start | bytes 12296 | tf_op jit(solution)/shard_map/ppermute | solution.py:216
  55.0 18.3 %collective-permute-start.2 = (f32[8,128]{1,0:T(8,128)S(1)}, f32[8,128]{1,0:T(8,128)S(1)}, u32[]{:S(2)}, u32[]{:S(2)}) collective-permute-start(f32[8,128]{1,0:T(8,128)S(1)} %get-tuple-element.29), channel_id=1, source_target_pairs={{0,1},{1,2},{2,3},{3,0},{4,5},{5,6},{6,7},{7,4},{8,9},{9,10},{10,1... | collective-permute-start | bytes 12296 | tf_op jit(solution)/shard_map/ppermute | solution.py:216
  69.7 5.1 %collective-permute-start.1 = (f32[8,128]{1,0:T(8,128)S(1)}, f32[8,128]{1,0:T(8,128)S(1)}, u32[]{:S(2)}, u32[]{:S(2)}) collective-permute-start(f32[8,128]{1,0:T(8,128)S(1)} %get-tuple-element.29), channel_id=1, source_target_pairs={{0,2},{1,3},{2,0},{3,1},{4,6},{5,7},{6,4},{7,5},{8,10},{9,11},{10,... | collective-permute-start | bytes 12296 | tf_op jit(solution)/shard_map/ppermute | solution.py:216
  73.3 20.1 %collective-permute-start.11 = (bf16[192,1024]{1,0:T(8,128)(2,1)S(1)}, bf16[192,1024]{1,0:T(8,128)(2,1)}, u32[]{:S(2)}, u32[]{:S(2)}) collective-permute-start(bf16[192,1024]{1,0:T(8,128)(2,1)S(1)} %get-tuple-element.32.refs_2_), channel_id=1, source_target_pairs={{0,4},{4,0},{1,5},{5,1},{2,6},{6,2},{3,7},{7,3},{8,12},{12,8},{9,1... | collective-permute-start | bytes 1179656 | tf_op jit(solution)/shard_map/ppermute | solution.py:216
  73.3 20.1 %collective-permute-start.14 = (bf16[192,1024]{1,0:T(8,128)(2,1)S(1)}, bf16[192,1024]{1,0:T(8,128)(2,1)}, u32[]{:S(2)}, u32[]{:S(2)}) collective-permute-start(bf16[192,1024]{1,0:T(8,128)(2,1)S(1)} %collective-permute-done.10.refs_5_), channel_id=1, source_target_pairs={{0,4},{4,0},{1,5},{5,1},{2,6},{6,2},{3,7},{7,3},{8,12},{12,8},{9,1... | collective-permute-start | bytes 1179656 | tf_op jit(solution)/shard_map/ppermute | solution.py:216
  73.8 19.6 %collective-permute-start.13 = (bf16[192,1024]{1,0:T(8,128)(2,1)S(1)}, bf16[192,1024]{1,0:T(8,128)(2,1)}, u32[]{:S(2)}, u32[]{:S(2)}) collective-permute-start(bf16[192,1024]{1,0:T(8,128)(2,1)S(1)} %collective-permute-done.9.refs_4_), channel_id=1, source_target_pairs={{0,4},{4,0},{1,5},{5,1},{2,6},{6,2},{3,7},{7,3},{8,12},{12,8},{9,1... | collective-permute-start | bytes 1179656 | tf_op jit(solution)/shard_map/ppermute | solution.py:216
  73.9 19.5 %collective-permute-start.12 = (bf16[192,1024]{1,0:T(8,128)(2,1)}, bf16[192,1024]{1,0:T(8,128)(2,1)}, u32[]{:S(2)}, u32[]{:S(2)}) collective-permute-start(bf16[192,1024]{1,0:T(8,128)(2,1)} %collective-permute-done.8.refs_3_), channel_id=1, source_target_pairs={{0,4},{4,0},{1,5},{5,1},{2,6},{6,2},{3,7},{7,3},{8,12},{12,8},{9,1... | collective-permute-start | bytes 1179656 | tf_op jit(solution)/shard_map/ppermute | solution.py:216
  74.9 2.0 %collective-permute-start.4 = (f32[8,128]{1,0:T(8,128)S(1)}, f32[8,128]{1,0:T(8,128)S(1)}, u32[]{:S(2)}, u32[]{:S(2)}) collective-permute-start(f32[8,128]{1,0:T(8,128)S(1)} %add_add_fusion.own_ref), channel_id=1, source_target_pairs={{0,4},{4,0},{1,5},{5,1},{2,6},{6,2},{3,7},{7,3},{8,12},{12,8},{9,1... | collective-permute-start | bytes 12296 | tf_op jit(solution)/shard_map/ppermute | solution.py:216
  76.8 3.7 %collective-permute-start.7 = (f32[16,128]{1,0:T(8,128)S(1)}, f32[16,128]{1,0:T(8,128)S(1)}, u32[]{:S(2)}, u32[]{:S(2)}) collective-permute-start(f32[16,128]{1,0:T(8,128)S(1)} %shard_map.53.mean_0), channel_id=1, source_target_pairs={{0,192},{64,0},{128,64},{192,128},{1,193},{65,1},{129,65},{193,129... | collective-permute-start | bytes 24584 | tf_op jit(solution)/shard_map/ppermute | solution.py:216
  80.5 3.7 %collective-permute-start.6 = (f32[16,128]{1,0:T(8,128)S(1)}, f32[16,128]{1,0:T(8,128)S(1)}, u32[]{:S(2)}, u32[]{:S(2)}) collective-permute-start(f32[16,128]{1,0:T(8,128)S(1)} %shard_map.53.mean_0), channel_id=1, source_target_pairs={{0,64},{64,128},{128,192},{192,0},{1,65},{65,129},{129,193},{193,1... | collective-permute-start | bytes 24584 | tf_op jit(solution)/shard_map/ppermute | solution.py:216
  84.1 5.2 %collective-permute-start.5 = (f32[16,128]{1,0:T(8,128)S(1)}, f32[16,128]{1,0:T(8,128)S(1)}, u32[]{:S(2)}, u32[]{:S(2)}) collective-permute-start(f32[16,128]{1,0:T(8,128)S(1)} %shard_map.53.mean_0), channel_id=1, source_target_pairs={{0,128},{64,192},{128,0},{192,64},{1,129},{65,193},{129,1},{193,65... | collective-permute-start | bytes 24584 | tf_op jit(solution)/shard_map/ppermute | solution.py:216
  97.8 0.7 copy-start.1
  98.4 22.1 %collective-permute-start.15 = (bf16[2,4,16,768]{3,2,1,0:T(8,128)(2,1)S(1)}, bf16[2,4,16,768]{3,2,1,0:T(8,128)(2,1)S(1)}, u32[]{:S(2)}, u32[]{:S(2)}) collective-permute-start(bf16[2,4,16,768]{3,2,1,0:T(8,128)(2,1)S(1)} %get-tuple-element.34), channel_id=1, source_target_pairs={{0,128},{64,192},{128,0},{192,64},{1,129},{65,193},{129,1},{193,65... | collective-permute-start | bytes 589832 | tf_op jit(solution)/shard_map/ppermute | solution.py:216
  100.4 21.3 %collective-permute-start.16 = (bf16[2,4,16,768]{3,2,1,0:T(8,128)(2,1)}, bf16[2,4,16,768]{3,2,1,0:T(8,128)(2,1)S(1)}, u32[]{:S(2)}, u32[]{:S(2)}) collective-permute-start(bf16[2,4,16,768]{3,2,1,0:T(8,128)(2,1)} %get-tuple-element.35), channel_id=1, source_target_pairs={{0,64},{64,128},{128,192},{192,0},{1,65},{65,129},{129,193},{193,1... | collective-permute-start | bytes 589832 | tf_op jit(solution)/shard_map/ppermute | solution.py:216
  101.6 21.0 %collective-permute-start.17 = (bf16[2,4,16,768]{3,2,1,0:T(8,128)(2,1)}, bf16[2,4,16,768]{3,2,1,0:T(8,128)(2,1)S(1)}, u32[]{:S(2)}, u32[]{:S(2)}) collective-permute-start(bf16[2,4,16,768]{3,2,1,0:T(8,128)(2,1)} %get-tuple-element.36), channel_id=1, source_target_pairs={{0,192},{64,0},{128,64},{192,128},{1,193},{65,1},{129,65},{193,129... | collective-permute-start | bytes 589832 | tf_op jit(solution)/shard_map/ppermute | solution.py:216
  111.0 27.3 %copy-start.2 = (bf16[2,4,16,768]{3,2,1,0:T(8,128)(2,1)S(1)}, bf16[2,4,16,768]{3,2,1,0:T(8,128)(2,1)}, u32[]{:S(2)}) copy-start(bf16[2,4,16,768]{3,2,1,0:T(8,128)(2,1)} %copy-done.1) | copy-start | bytes 589828
  116.9 9.4 %collective-permute-start.21 = (bf16[2,4,16,768]{3,2,1,0:T(8,128)(2,1)S(1)}, bf16[2,4,16,768]{3,2,1,0:T(8,128)(2,1)S(1)}, u32[]{:S(2)}, u32[]{:S(2)}) collective-permute-start(bf16[2,4,16,768]{3,2,1,0:T(8,128)(2,1)S(1)} %get-tuple-element.47), channel_id=1, source_target_pairs={{0,128},{64,192},{128,0},{192,64},{1,129},{65,193},{129,1},{193,65... | collective-permute-start | bytes 589832 | tf_op jit(solution)/shard_map/ppermute | solution.py:216
  118.6 19.8 %collective-permute-start.18 = (bf16[3,4,16,768]{3,2,1,0:T(8,128)(2,1)}, bf16[3,4,16,768]{3,2,1,0:T(8,128)(2,1)S(1)}, u32[]{:S(2)}, u32[]{:S(2)}) collective-permute-start(bf16[3,4,16,768]{3,2,1,0:T(8,128)(2,1)} %get-tuple-element.42), channel_id=1, source_target_pairs={{0,128},{64,192},{128,0},{192,64},{1,129},{65,193},{129,1},{193,65... | collective-permute-start | bytes 884744 | tf_op jit(solution)/shard_map/ppermute | solution.py:216
  120.5 17.8 %collective-permute-start.19 = (bf16[3,4,16,768]{3,2,1,0:T(8,128)(2,1)}, bf16[3,4,16,768]{3,2,1,0:T(8,128)(2,1)S(1)}, u32[]{:S(2)}, u32[]{:S(2)}) collective-permute-start(bf16[3,4,16,768]{3,2,1,0:T(8,128)(2,1)} %get-tuple-element.43), channel_id=1, source_target_pairs={{0,64},{64,128},{128,192},{192,0},{1,65},{65,129},{129,193},{193,1... | collective-permute-start | bytes 884744 | tf_op jit(solution)/shard_map/ppermute | solution.py:216
  121.7 16.6 %collective-permute-start.20 = (bf16[3,4,16,768]{3,2,1,0:T(8,128)(2,1)}, bf16[3,4,16,768]{3,2,1,0:T(8,128)(2,1)S(1)}, u32[]{:S(2)}, u32[]{:S(2)}) collective-permute-start(bf16[3,4,16,768]{3,2,1,0:T(8,128)(2,1)} %get-tuple-element.44), channel_id=1, source_target_pairs={{0,192},{64,0},{128,64},{192,128},{1,193},{65,1},{129,65},{193,129... | collective-permute-start | bytes 884744 | tf_op jit(solution)/shard_map/ppermute | solution.py:216
  122.6 15.5 %collective-permute-start.22 = (bf16[2,4,16,768]{3,2,1,0:T(8,128)(2,1)}, bf16[2,4,16,768]{3,2,1,0:T(8,128)(2,1)S(1)}, u32[]{:S(2)}, u32[]{:S(2)}) collective-permute-start(bf16[2,4,16,768]{3,2,1,0:T(8,128)(2,1)} %get-tuple-element.48), channel_id=1, source_target_pairs={{0,64},{64,128},{128,192},{192,0},{1,65},{65,129},{129,193},{193,1... | collective-permute-start | bytes 589832 | tf_op jit(solution)/shard_map/ppermute | solution.py:216
  126.3 12.1 %collective-permute-start.23 = (bf16[2,4,16,768]{3,2,1,0:T(8,128)(2,1)S(1)}, bf16[2,4,16,768]{3,2,1,0:T(8,128)(2,1)S(1)}, u32[]{:S(2)}, u32[]{:S(2)}) collective-permute-start(bf16[2,4,16,768]{3,2,1,0:T(8,128)(2,1)S(1)} %get-tuple-element.49), channel_id=1, source_target_pairs={{0,192},{64,0},{128,64},{192,128},{1,193},{65,1},{129,65},{193,129... | collective-permute-start | bytes 589832 | tf_op jit(solution)/shard_map/ppermute | solution.py:216
  139.7 24.0 %all-to-all-start.2 = ((f32[256,1,4]{2,1,0:T(1,128)}), f32[256,1,4]{2,1,0:T(1,128)S(1)}, u32[]{:S(2)}, u32[]{:S(2)}) async-start(f32[256,1,4]{2,1,0:T(1,128)} %broadcast_in_dim.9), calls=%async_computation.2 | async-start | bytes 262144 | tf_op jit(solution)/shard_map/all_to_all | solution.py:211

commit v7 on v6

--- a/solution.py
+++ b/solution.py
@@ -20,8 +20,8 @@
 UNIT = NX * ROWS
 BLOCK = D // NX
 GROUPS = BLOCK // GROUP
-SENDS = (2, 5)
-PIECES = ((0, 0, 2), (1, 0, 3), (1, 3, 2))
+SENDS = (1, 2, 4)
+PIECES = ((None, 0, 3), (2, 0, 2), (2, 2, 2))
 MIB = 1 << 20
 HALF = BLOCK // 2
 OWN = TOKENS // (NX * NZ * NC)
@@ -104,31 +104,38 @@
         inverse_ref[k] = 1.0 / scale
 
 
-def quantize(columns_ref, rows, scale_ref, inverse_ref, delta_ref):
-    for group in range(GROUPS):
-        packed = columns_ref[group, rows, :]
-        wide = packed.astype(jnp.float32)
-        for k in range(GRID):
-            scaled = wide if k == 0 else wide * scale_ref[k, group : group + 1, :]
-            top = jnp.max(jnp.abs(scaled), axis=1, keepdims=True) + 1e-06
-            v = scaled * (7.0 / top)
-            r = v - jnp.round(v)
-            square = r * r
-            poly = jnp.full_like(square, SINE[-1])
-            for coefficient in SINE[-2::-1]:
-                poly = poly * square + coefficient
-            shift = (r * poly) * (top * (1.0 / 7.0))
-            if k:
-                shift = shift * inverse_ref[k, group : group + 1, :]
-            dequant = (wide - shift).astype(jnp.bfloat16)
-            delta_ref[k * UNIT : (k + 1) * UNIT, group * GROUP : (group + 1) * GROUP] = dequant - packed
-
-
-def quantize_kernel(columns_ref, scale_ref, inverse_ref, deltas):
-    @pl.loop(0, deltas.shape[0])
-    def _(unit):
-        rows = pl.ds(pl.multiple_of(LEAD + unit * UNIT, 32), UNIT)
-        quantize(columns_ref, rows, scale_ref, inverse_ref, deltas.at[unit])
+def quantize(columns_ref, rows, scale_ref, inverse_ref, delta_ref, group):
+    packed = columns_ref[group, rows, :]
+    wide = packed.astype(jnp.float32)
+    for k in range(GRID):
+        scaled = wide if k == 0 else wide * scale_ref[k, pl.ds(group, 1), :]
+        top = jnp.max(jnp.abs(scaled), axis=1, keepdims=True) + 1e-06
+        v = scaled * (7.0 / top)
+        r = v - jnp.round(v)
+        square = r * r
+        poly = jnp.full_like(square, SINE[-1])
+        for coefficient in SINE[-2::-1]:
+            poly = poly * square + coefficient
+        shift = (r * poly) * (top * (1.0 / 7.0))
+        if k:
+            shift = shift * inverse_ref[k, pl.ds(group, 1), :]
+        dequant = (wide - shift).astype(jnp.bfloat16)
+        lanes = group * GROUP if isinstance(group, int) else pl.multiple_of(group * GROUP, GROUP)
+        delta_ref[k * UNIT : (k + 1) * UNIT, pl.ds(lanes, GROUP)] = dequant - packed
+
+
+def quantize_kernel(lead):
+    def body(columns_ref, scale_ref, inverse_ref, deltas):
+        @pl.loop(0, deltas.shape[0])
+        def _(unit):
+            rows = pl.ds(pl.multiple_of(lead + unit * UNIT, 32), UNIT)
+
+            @pl.loop(0, GROUPS, step=4)
+            def _(group):
+                for at in range(4):
+                    quantize(columns_ref, rows, scale_ref, inverse_ref, deltas.at[unit], group + at)
+
+    return body
 
 
 def multiply(delta, tokens, out_refs, unit):
@@ -141,10 +148,10 @@
             out_refs[hops][unit, k] = out[at : at + ROWS, :]
 
 
-def first_kernel(units):
+def first_kernel():
     def body(*refs):
-        core_ref, deltas, own, other = refs[0], refs[1], refs[2:6], refs[6:10]
-        out_refs, kept, tokens, done = refs[10:14], *refs[14:]
+        core_ref, deltas, own, other = refs[0], refs[1:3], refs[3:7], refs[7:11]
+        out_refs, kept, tokens, done = refs[11:15], *refs[15:]
         at_own = pl.multiple_of(core_ref[0] * HALF, HALF)
         at_other = pl.multiple_of((1 - core_ref[0]) * HALF, HALF)
         count = TOKENS // NY
@@ -153,8 +160,11 @@
             tokens[at * count : (at + 1) * count, pl.ds(at_other, HALF)] = other[at][...]
         keep = pltpu.make_async_copy(tokens, kept, done)
         keep.start()
-        for unit in range(units):
-            multiply(deltas.at[unit], tokens, out_refs, unit)
+        unit = 0
+        for delta in deltas:
+            for at in range(delta.shape[0]):
+                multiply(delta.at[at], tokens, out_refs, unit)
+                unit += 1
         keep.wait()
 
     return body
@@ -168,7 +178,8 @@
         for unit in range(units):
             delta = deltas[unit % 2]
             rows = slice((first + unit) * UNIT, (first + unit + 1) * UNIT)
-            quantize(columns_ref, rows, scale_ref, inverse_ref, delta)
+            for group in range(GROUPS):
+                quantize(columns_ref, rows, scale_ref, inverse_ref, delta, group)
             if unit == 0:
                 fetch.wait()
             multiply(delta, tokens, out_refs, unit)
@@ -236,7 +247,9 @@
     received = [lax.all_to_all(merged, ZC, 0, 0, tiled=True)]
     half = array((HALF // GROUP, GROUP), f32)
     joined, sums = kernel(join_tokens, [array((TOKENS // NY, HALF), bf16), half])(received[0])
-    received.append(lax.all_to_all(after(columns[1], joined), ZC, 0, 0, tiled=True))
+    for at in (1, 2):
+        part = after(columns[at], joined, received[-1])
+        received.append(lax.all_to_all(part, ZC, 0, 0, tiled=True))
 
     around = [shifted(sums, "tensor", hops) for hops in (2, 1, 3)]
     sums = (sums + around[0]) + (around[1] + around[2])
@@ -256,14 +269,17 @@
         out_shape = [array((units, GRID, ROWS, TOKENS), bf16)] * NX
         work = units * GRID * UNIT * TOKENS * BLOCK
         if at == 0:
-            quantized = array((units, GRID * UNIT, BLOCK), bf16)
-            deltas = kernel(quantize_kernel, quantized, flops=2 * work)(received[0], scale, inverse)
+            deltas = []
+            for send, lead in ((0, LEAD), (1, 0)):
+                quantized = array((SENDS[send], GRID * UNIT, BLOCK), bf16)
+                step = kernel(quantize_kernel(lead), quantized, flops=2 * work)
+                deltas.append(step(received[send], scale, inverse))
             *partial, tokens = kernel(
-                first_kernel(units), out_shape + [pltpu.HBM((TOKENS, BLOCK), bf16)], flops=work,
-                in_specs=[smem] + [local] * 9,
+                first_kernel(), out_shape + [pltpu.HBM((TOKENS, BLOCK), bf16)], flops=work,
+                in_specs=[smem] + [local] * 10,
                 out_specs=[local] * NX + [far],
                 scratch_shapes=gathered,
-            )(core, deltas, *parts)
+            )(core, *deltas, *parts)
         else:
             partial = kernel(
                 piece_kernel(first, units),

time: 166 us -> 177 us (1.066)
  blocking collectives: 33.1 us -> 47.1 us
  waiting for transfers between devices: 52.6 us -> 46.1 us
  starting transfers between devices: 46.9 us -> 49.7 us
    all_to_all x0 -> x1, blocking collectives: none -> 18.8 us  [search(): received.append(lax.all_to_all(part, ZC, 0, 0, tiled=True))]
    ppermute x23, waiting for transfers between devices: 41.1 us -> 34.6 us  [shifted(): lax.ppermute(value, axis, [(i, (i + hops) % size) for i in range(size)])]
    all_to_all x1, blocking collectives: 33.1 us -> 28.3 us  [search(): received = [lax.all_to_all(merged, ZC, 0, 0, tiled=True)]]
    pallas_call x2 -> x3, Pallas kernels: 8.09 us -> 11.3 us  [the longest x2 6.34 us: search(): deltas.append(step(received[send], scale, inverse))]
    ppermute x23, starting transfers between devices: 27.9 us -> 30.7 us  [shifted(): lax.ppermute(value, axis, [(i, (i + hops) % size) for i in range(size)])]
    pallas_call x2, Pallas kernels: 14.5 us -> 11.7 us  [search(): kernel(piece_kernel(first, units), out_shape, flops=3 * work, in_specs=[l...]
  transfers between devices with their start and end apart: 26 -> 26, of which waited for: 12 -> 14; matrix products, arithmetic and copies ran while one was open for 1% -> 1% of each run, Pallas kernels for 15% -> 14%
where the time goes in v7:
time: 177 us; the launch traced here: 175 us
  starting transfers between devices  49.7 us (28%)
  blocking collectives  47.1 us (27%)
  waiting for transfers between devices  46.1 us (26%)
  Pallas kernels  25.7 us (15%)
  local copies, waits for them, and re-layouts  3.65 us (2%)
    ppermute x23, waiting for transfers between devices, shifted(): lax.ppermute(value, axis, [(i, (i + hops) % size) for i in range(size)])  34.6 us
    ppermute x23, starting transfers between devices, shifted(): lax.ppermute(value, axis, [(i, (i + hops) % size) for i in range(size)])  30.7 us
    all_to_all x1, blocking collectives, search(): received = [lax.all_to_all(merged, ZC, 0, 0, tiled=True)]  28.3 us
    all_to_all x1, blocking collectives, search(): received.append(lax.all_to_all(part, ZC, 0, 0, tiled=True))  18.8 us
    pallas_call x2, Pallas kernels, search(): kernel(piece_kernel(first, units), out_shape, flops=3 * work, in_specs=[l...  11.7 us
    all_to_all x1, starting transfers between devices, spread(): return lax.all_to_all(wide, axes, 0, 0, tiled=True)  11.3 us
    all_to_all x1, waiting for transfers between devices, spread(): return lax.all_to_all(wide, axes, 0, 0, tiled=True)  11.1 us
    pallas_call x2, Pallas kernels, search(): deltas.append(step(received[send], scale, inverse))  6.34 us
  transfers between devices with their start and end apart: 26, of which 14 were waited for; matrix products, arithmetic and copies ran while one was open for 1% of the time, Pallas kernels for 14%

profile of v7, /device:TPU:2, one launch (start us, length us, event | category | flops | bytes accessed | tf_op | source)
XLA Modules:
  0.0 174.5 jit_solution(1538039304294774708)
XLA Ops:
  0.6 0.8 copy-done.1
  1.5 3.5 %collective-permute-start = (bf16[24,1024]{1,0:T(8,128)(2,1)S(1)}, bf16[24,1024]{1,0:T(8,128)(2,1)S(1)}, u32[]{:S(2)}, u32[]{:S(2)}) collective-permute-start(bf16[24,1024]{1,0:T(8,128)(2,1)S(1)} %shard_map.49), channel_id=1, source_target_pairs={{0,0},{1,64},{2,128},{3,192},{64,1},{65,65},{66,129},{67,193},{128... | collective-permute-start | bytes 147464 | tf_op jit(solution)/shard_map/ppermute | solution.py:241
  5.0 1.5 copy-done
  6.5 1.5 shard_map.50
  8.0 0.4 collective-permute-done.tokens_ref
  8.5 28.3 %all_to_all.20.parts_ref.columns_ref = bf16[16,160,128]{2,1,0:T(8,128)(2,1)S(1)} all-to-all(bf16[16,160,128]{2,1,0:T(8,128)(2,1)S(1)} %shard_map.51), channel_id=1, replica_groups=mesh['dp_0'=4,'dp_1'=8,'dp_2'=2,'tensor'=4] {'dp_1','dp_2'}, dimensions={0} | all-to-all | bytes 1310720 | tf_op jit(solution)/shard_map/all_to_all | solution.py:247
  37.0 18.8 %all_to_all.21.columns_ref = bf16[16,128,128]{2,1,0:T(8,128)(2,1)S(1)} all-to-all(bf16[16,128,128]{2,1,0:T(8,128)(2,1)S(1)} %get-tuple-element.36), channel_id=1, replica_groups=mesh['dp_0'=4,'dp_1'=8,'dp_2'=2,'tensor'=4] {'dp_1','dp_2'}, dimensions={0} | all-to-all | bytes 1048576 | tf_op jit(solution)/shard_map/all_to_all | solution.py:252
  55.8 4.2 %all-to-all-start.2 = ((bf16[16,256,128]{2,1,0:T(8,128)(2,1)}), bf16[16,256,128]{2,1,0:T(8,128)(2,1)S(1)}, u32[]{:S(2)}, u32[]{:S(2)}) async-start(bf16[16,256,128]{2,1,0:T(8,128)(2,1)} %get-tuple-element.42), calls=%async_computation.2 | async-start | bytes 2097152 | tf_op jit(solution)/shard_map/all_to_all | solution.py:252
  60.0 6.1 %collective-permute-start.10 = (bf16[192,1024]{1,0:T(8,128)(2,1)S(1)}, bf16[192,1024]{1,0:T(8,128)(2,1)S(1)}, u32[]{:S(2)}, u32[]{:S(2)}) collective-permute-start(bf16[192,1024]{1,0:T(8,128)(2,1)S(1)} %get-tuple-element.35.refs_3_), channel_id=1, source_target_pairs={{0,3},{1,0},{2,1},{3,2},{4,7},{5,4},{6,5},{7,6},{8,11},{9,8},{10,9... | collective-permute-start | bytes 1179656 | tf_op jit(solution)/shard_map/ppermute | solution.py:227
  66.1 1.6 collective-permute-start.8
  67.7 1.7 collective-permute-start.3
  69.4 0.9 collective-permute-start.2
  70.2 13.9 %collective-permute-done.3 = f32[8,128]{1,0:T(8,128)S(1)} collective-permute-done((f32[8,128]{1,0:T(8,128)S(1)}, f32[8,128]{1,0:T(8,128)S(1)}, u32[]{:S(2)}, u32[]{:S(2)}) %collective-permute-start.3) | collective-permute-done | bytes 4128 | tf_op jit(solution)/shard_map/ppermute | solution.py:227
  84.1 1.6 collective-permute-start.1
  85.8 1.8 %collective-permute-done.2 = f32[8,128]{1,0:T(8,128)S(1)} collective-permute-done((f32[8,128]{1,0:T(8,128)S(1)}, f32[8,128]{1,0:T(8,128)S(1)}, u32[]{:S(2)}, u32[]{:S(2)}) %collective-permute-start.2) | collective-permute-done | bytes 4128 | tf_op jit(solution)/shard_map/ppermute | solution.py:227
  87.6 1.7 collective-permute-done.1
  89.2 1.2 collective-permute-done.4.other_ref
  90.4 0.5 collective-permute-start.7
  90.9 1.6 collective-permute-start.6
  92.4 1.6 collective-permute-done.7.mean_3
  94.1 2.7 %collective-permute-start.5 = (f32[16,128]{1,0:T(8,128)S(1)}, f32[16,128]{1,0:T(8,128)S(1)}, u32[]{:S(2)}, u32[]{:S(2)}) collective-permute-start(f32[16,128]{1,0:T(8,128)S(1)} %shard_map.53.mean_0), channel_id=1, source_target_pairs={{0,128},{64,192},{128,0},{192,64},{1,129},{65,193},{129,1},{193,65... | collective-permute-start | bytes 24584 | tf_op jit(solution)/shard_map/ppermute | solution.py:227
  96.8 2.4 %collective-permute-done.5.mean_1 = f32[16,128]{1,0:T(8,128)S(1)} collective-permute-done((f32[16,128]{1,0:T(8,128)S(1)}, f32[16,128]{1,0:T(8,128)S(1)}, u32[]{:S(2)}, u32[]{:S(2)}) %collective-permute-start.5) | collective-permute-done | bytes 8224 | tf_op jit(solution)/shard_map/ppermute | solution.py:227
  99.7 0.5 collective-permute-start.13
  100.4 2.1 %shard_map.55.refs_1_ = bf16[1,256,2048]{2,1,0:T(8,128)(2,1)S(1)} custom-call(bf16[16,160,128]{2,1,0:T(8,128)(2,1)S(1)} %all_to_all.20.parts_ref.columns_ref, f32[4,16,128]{2,1,0:T(8,128)S(1)} %get-tuple-element.32.scale_ref, f32[4,16,128]{2,1,0:T(8,128)S(1)} %get-tuple-element.33.inverse_ref), custom_call_target="tpu_custom_call" | custom-call | flops 2415919104 | tf_op jit(solution)/shard_map/pallas_call | solution.py:276
  102.5 4.2 %shard_map.56.refs_2_ = bf16[2,256,2048]{2,1,0:T(8,128)(2,1)S(1)} custom-call(bf16[16,128,128]{2,1,0:T(8,128)(2,1)S(1)} %all_to_all.21.columns_ref, f32[4,16,128]{2,1,0:T(8,128)S(1)} %get-tuple-element.32.scale_ref, f32[4,16,128]{2,1,0:T(8,128)S(1)} %get-tuple-element.33.inverse_ref), custom_call_target="tpu_custom_call" | custom-call | flops 2415919104 | tf_op jit(solution)/shard_map/pallas_call | solution.py:276
  106.8 5.0 %shard_map.57 = (bf16[3,4,16,768]{3,2,1,0:T(8,128)(2,1)S(1)}, bf16[3,4,16,768]{3,2,1,0:T(8,128)(2,1)}, bf16[3,4,16,768]{3,2,1,0:T(8,128)(2,1)}, bf16[3,4,16,768]{3,2,1,0:T(8,128)(2,1)}, bf16[768,2048]{1,0:T(8,128)(2,1)}) custom-call(s32[1]{0:T(128)} %bitcast.core_ref.refs_0_, bf16[1,256,2048]{2,1,0:T(8,128)(2,1)S(1)} %shard_map.55.refs_1_, ...), custom_call_target="tpu_custom_call" | custom-call | flops 1207959552 | tf_op jit(solution)/shard_map/pallas_call | solution.py:277
  111.8 2.8 %collective-permute-start.15 = (bf16[3,4,16,768]{3,2,1,0:T(8,128)(2,1)}, bf16[3,4,16,768]{3,2,1,0:T(8,128)(2,1)S(1)}, u32[]{:S(2)}, u32[]{:S(2)}) collective-permute-start(bf16[3,4,16,768]{3,2,1,0:T(8,128)(2,1)} %get-tuple-element.38), channel_id=1, source_target_pairs={{0,128},{64,192},{128,0},{192,64},{1,129},{65,193},{129,1},{193,65... | collective-permute-start | bytes 884744 | tf_op jit(solution)/shard_map/ppermute | solution.py:227
  114.6 2.0 %collective-permute-start.17 = (bf16[3,4,16,768]{3,2,1,0:T(8,128)(2,1)}, bf16[3,4,16,768]{3,2,1,0:T(8,128)(2,1)S(1)}, u32[]{:S(2)}, u32[]{:S(2)}) collective-permute-start(bf16[3,4,16,768]{3,2,1,0:T(8,128)(2,1)} %get-tuple-element.40), channel_id=1, source_target_pairs={{0,192},{64,0},{128,64},{192,128},{1,193},{65,1},{129,65},{193,129... | collective-permute-start | bytes 884744 | tf_op jit(solution)/shard_map/ppermute | solution.py:227
  116.7 5.8 %shard_map.58 = (bf16[2,4,16,768]{3,2,1,0:T(8,128)(2,1)S(1)}, bf16[2,4,16,768]{3,2,1,0:T(8,128)(2,1)S(1)}, bf16[2,4,16,768]{3,2,1,0:T(8,128)(2,1)}, bf16[2,4,16,768]{3,2,1,0:T(8,128)(2,1)S(1)}) custom-call(bf16[16,256,128]{2,1,0:T(8,128)(2,1)S(1)} %all-to-all-done.2.columns_ref, f32[4,16,128]{2,1,0:T(8,128)S(1)} %get-tuple-element.32.scale_ref, ...), custom_call_target="tpu_custom_call" | custom-call | flops 2415919104 | tf_op jit(solution)/shard_map/pallas_call | solution.py:284
  122.5 5.9 %shard_map.59 = (bf16[2,4,16,768]{3,2,1,0:T(8,128)(2,1)S(1)}, bf16[2,4,16,768]{3,2,1,0:T(8,128)(2,1)}, bf16[2,4,16,768]{3,2,1,0:T(8,128)(2,1)S(1)}, bf16[2,4,16,768]{3,2,1,0:T(8,128)(2,1)}) custom-call(bf16[16,256,128]{2,1,0:T(8,128)(2,1)S(1)} %all-to-all-done.2.columns_ref, f32[4,16,128]{2,1,0:T(8,128)S(1)} %get-tuple-element.32.scale_ref, ...), custom_call_target="tpu_custom_call" | custom-call | flops 2415919104 | tf_op jit(solution)/shard_map/pallas_call | solution.py:284
  128.4 0.9 collective-permute-start.21
  129.2 2.2 %collective-permute-start.22 = (bf16[2,4,16,768]{3,2,1,0:T(8,128)(2,1)}, bf16[2,4,16,768]{3,2,1,0:T(8,128)(2,1)S(1)}, u32[]{:S(2)}, u32[]{:S(2)}) collective-permute-start(bf16[2,4,16,768]{3,2,1,0:T(8,128)(2,1)} %get-tuple-element.52), channel_id=1, source_target_pairs={{0,64},{64,128},{128,192},{192,0},{1,65},{65,129},{129,193},{193,1... | collective-permute-start | bytes 589832 | tf_op jit(solution)/shard_map/ppermute | solution.py:227
  131.4 2.6 %collective-permute-start.18 = (bf16[2,4,16,768]{3,2,1,0:T(8,128)(2,1)}, bf16[2,4,16,768]{3,2,1,0:T(8,128)(2,1)S(1)}, u32[]{:S(2)}, u32[]{:S(2)}) collective-permute-start(bf16[2,4,16,768]{3,2,1,0:T(8,128)(2,1)} %get-tuple-element.46), channel_id=1, source_target_pairs={{0,128},{64,192},{128,0},{192,64},{1,129},{65,193},{129,1},{193,65... | collective-permute-start | bytes 589832 | tf_op jit(solution)/shard_map/ppermute | solution.py:227
  134.0 1.2 collective-permute-start.19
  135.2 2.5 %collective-permute-done.21.refs_9_ = bf16[2,4,16,768]{3,2,1,0:T(8,128)(2,1)S(1)} collective-permute-done((bf16[2,4,16,768]{3,2,1,0:T(8,128)(2,1)S(1)}, bf16[2,4,16,768]{3,2,1,0:T(8,128)(2,1)S(1)}, u32[]{:S(2)}, u32[]{:S(2)}) %collective-permute-start.21) | collective-permute-done | bytes 196640 | tf_op jit(solution)/shard_map/ppermute | solution.py:227
  137.7 1.5 collective-permute-start.20
  139.3 1.2 collective-permute-done.22.refs_10_
  140.5 3.1 %collective-permute-done.23.refs_11_ = bf16[2,4,16,768]{3,2,1,0:T(8,128)(2,1)S(1)} collective-permute-done((bf16[2,4,16,768]{3,2,1,0:T(8,128)(2,1)}, bf16[2,4,16,768]{3,2,1,0:T(8,128)(2,1)S(1)}, u32[]{:S(2)}, u32[]{:S(2)}) %collective-permute-start.23) | collective-permute-done | bytes 196640 | tf_op jit(solution)/shard_map/ppermute | solution.py:227
  143.6 2.6 %collective-permute-done.18.refs_5_ = bf16[2,4,16,768]{3,2,1,0:T(8,128)(2,1)S(1)} collective-permute-done((bf16[2,4,16,768]{3,2,1,0:T(8,128)(2,1)}, bf16[2,4,16,768]{3,2,1,0:T(8,128)(2,1)S(1)}, u32[]{:S(2)}, u32[]{:S(2)}) %collective-permute-start.18) | collective-permute-done | bytes 196640 | tf_op jit(solution)/shard_map/ppermute | solution.py:227
  146.2 1.5 collective-permute-done.19.refs_6_
  147.7 1.1 collective-permute-done.20.refs_7_
  148.8 0.6 shard_map.60
  149.4 0.7 broadcast_in_dim.9
  150.1 11.3 %all-to-all-start.3 = ((f32[256,1,4]{2,1,0:T(1,128)}), f32[256,1,4]{2,1,0:T(1,128)S(1)}, u32[]{:S(2)}, u32[]{:S(2)}) async-start(f32[256,1,4]{2,1,0:T(1,128)} %broadcast_in_dim.9), calls=%async_computation.3 | async-start | bytes 262144 | tf_op jit(solution)/shard_map/all_to_all | solution.py:222
  161.5 0.6 broadcast_multiply_fusion
  162.0 0.6 dynamic_slice.3
  162.6 11.1 %all-to-all-done.3 = f32[256,1,4]{2,1,0:T(1,128)S(1)} async-done(((f32[256,1,4]{2,1,0:T(1,128)}), f32[256,1,4]{2,1,0:T(1,128)S(1)}, u32[]{:S(2)}, u32[]{:S(2)}) %all-to-all-start.3) | async-done | bytes 4128 | tf_op jit(solution)/shard_map/all_to_all | solution.py:222
  174.0 0.5 broadcast_multiply_fusion.1
  (28 shorter events, 1.3 us)
Async XLA Ops:
  0.6 0.8 copy-start.1
  1.5 6.9 %collective-permute-start = (bf16[24,1024]{1,0:T(8,128)(2,1)S(1)}, bf16[24,1024]{1,0:T(8,128)(2,1)S(1)}, u32[]{:S(2)}, u32[]{:S(2)}) collective-permute-start(bf16[24,1024]{1,0:T(8,128)(2,1)S(1)} %shard_map.49), channel_id=1, source_target_pairs={{0,0},{1,64},{2,128},{3,192},{64,1},{65,65},{66,129},{67,193},{128... | collective-permute-start | bytes 147464 | tf_op jit(solution)/shard_map/ppermute | solution.py:241
  5.0 1.5 copy-start
  55.8 60.9 %all-to-all-start.2 = ((bf16[16,256,128]{2,1,0:T(8,128)(2,1)}), bf16[16,256,128]{2,1,0:T(8,128)(2,1)S(1)}, u32[]{:S(2)}, u32[]{:S(2)}) async-start(bf16[16,256,128]{2,1,0:T(8,128)(2,1)} %get-tuple-element.42), calls=%async_computation.2 | async-start | bytes 2097152 | tf_op jit(solution)/shard_map/all_to_all | solution.py:252
  60.0 39.5 %collective-permute-start.10 = (bf16[192,1024]{1,0:T(8,128)(2,1)S(1)}, bf16[192,1024]{1,0:T(8,128)(2,1)S(1)}, u32[]{:S(2)}, u32[]{:S(2)}) collective-permute-start(bf16[192,1024]{1,0:T(8,128)(2,1)S(1)} %get-tuple-element.35.refs_3_), channel_id=1, source_target_pairs={{0,3},{1,0},{2,1},{3,2},{4,7},{5,4},{6,5},{7,6},{8,11},{9,8},{10,9... | collective-permute-start | bytes 1179656 | tf_op jit(solution)/shard_map/ppermute | solution.py:227
  66.1 33.5 %collective-permute-start.9 = (bf16[192,1024]{1,0:T(8,128)(2,1)S(1)}, bf16[192,1024]{1,0:T(8,128)(2,1)S(1)}, u32[]{:S(2)}, u32[]{:S(2)}) collective-permute-start(bf16[192,1024]{1,0:T(8,128)(2,1)S(1)} %get-tuple-element.35.refs_3_), channel_id=1, source_target_pairs={{0,1},{1,2},{2,3},{3,0},{4,5},{5,6},{6,7},{7,4},{8,9},{9,10},{10,1... | collective-permute-start | bytes 1179656 | tf_op jit(solution)/shard_map/ppermute | solution.py:227
  66.1 34.0 %collective-permute-start.8 = (bf16[192,1024]{1,0:T(8,128)(2,1)S(1)}, bf16[192,1024]{1,0:T(8,128)(2,1)}, u32[]{:S(2)}, u32[]{:S(2)}) collective-permute-start(bf16[192,1024]{1,0:T(8,128)(2,1)S(1)} %get-tuple-element.35.refs_3_), channel_id=1, source_target_pairs={{0,2},{1,3},{2,0},{3,1},{4,6},{5,7},{6,4},{7,5},{8,10},{9,11},{10,... | collective-permute-start | bytes 1179656 | tf_op jit(solution)/shard_map/ppermute | solution.py:227
  67.7 16.5 %collective-permute-start.3 = (f32[8,128]{1,0:T(8,128)S(1)}, f32[8,128]{1,0:T(8,128)S(1)}, u32[]{:S(2)}, u32[]{:S(2)}) collective-permute-start(f32[8,128]{1,0:T(8,128)S(1)} %get-tuple-element.31), channel_id=1, source_target_pairs={{0,3},{1,0},{2,1},{3,2},{4,7},{5,4},{6,5},{7,6},{8,11},{9,8},{10,9... | collective-permute-start | bytes 12296 | tf_op jit(solution)/shard_map/ppermute | solution.py:227
  69.4 18.2 %collective-permute-start.2 = (f32[8,128]{1,0:T(8,128)S(1)}, f32[8,128]{1,0:T(8,128)S(1)}, u32[]{:S(2)}, u32[]{:S(2)}) collective-permute-start(f32[8,128]{1,0:T(8,128)S(1)} %get-tuple-element.31), channel_id=1, source_target_pairs={{0,1},{1,2},{2,3},{3,0},{4,5},{5,6},{6,7},{7,4},{8,9},{9,10},{10,1... | collective-permute-start | bytes 12296 | tf_op jit(solution)/shard_map/ppermute | solution.py:227
  84.1 5.1 %collective-permute-start.1 = (f32[8,128]{1,0:T(8,128)S(1)}, f32[8,128]{1,0:T(8,128)S(1)}, u32[]{:S(2)}, u32[]{:S(2)}) collective-permute-start(f32[8,128]{1,0:T(8,128)S(1)} %get-tuple-element.31), channel_id=1, source_target_pairs={{0,2},{1,3},{2,0},{3,1},{4,6},{5,7},{6,4},{7,5},{8,10},{9,11},{10,... | collective-permute-start | bytes 12296 | tf_op jit(solution)/shard_map/ppermute | solution.py:227
  89.2 1.2 collective-permute-start.4
  90.4 3.7 %collective-permute-start.7 = (f32[16,128]{1,0:T(8,128)S(1)}, f32[16,128]{1,0:T(8,128)S(1)}, u32[]{:S(2)}, u32[]{:S(2)}) collective-permute-start(f32[16,128]{1,0:T(8,128)S(1)} %shard_map.53.mean_0), channel_id=1, source_target_pairs={{0,192},{64,0},{128,64},{192,128},{1,193},{65,1},{129,65},{193,129... | collective-permute-start | bytes 24584 | tf_op jit(solution)/shard_map/ppermute | solution.py:227
  90.9 5.9 %collective-permute-start.6 = (f32[16,128]{1,0:T(8,128)S(1)}, f32[16,128]{1,0:T(8,128)S(1)}, u32[]{:S(2)}, u32[]{:S(2)}) collective-permute-start(f32[16,128]{1,0:T(8,128)S(1)} %shard_map.53.mean_0), channel_id=1, source_target_pairs={{0,64},{64,128},{128,192},{192,0},{1,65},{65,129},{129,193},{193,1... | collective-permute-start | bytes 24584 | tf_op jit(solution)/shard_map/ppermute | solution.py:227
  94.1 5.2 %collective-permute-start.5 = (f32[16,128]{1,0:T(8,128)S(1)}, f32[16,128]{1,0:T(8,128)S(1)}, u32[]{:S(2)}, u32[]{:S(2)}) collective-permute-start(f32[16,128]{1,0:T(8,128)S(1)} %shard_map.53.mean_0), channel_id=1, source_target_pairs={{0,128},{64,192},{128,0},{192,64},{1,129},{65,193},{129,1},{193,65... | collective-permute-start | bytes 24584 | tf_op jit(solution)/shard_map/ppermute | solution.py:227
  96.8 10.0 %collective-permute-start.11 = (bf16[192,1024]{1,0:T(8,128)(2,1)S(1)}, bf16[192,1024]{1,0:T(8,128)(2,1)S(1)}, u32[]{:S(2)}, u32[]{:S(2)}) collective-permute-start(bf16[192,1024]{1,0:T(8,128)(2,1)S(1)} %get-tuple-element.35.refs_3_), channel_id=1, source_target_pairs={{0,4},{4,0},{1,5},{5,1},{2,6},{6,2},{3,7},{7,3},{8,12},{12,8},{9,1... | collective-permute-start | bytes 1179656 | tf_op jit(solution)/shard_map/ppermute | solution.py:227
  99.6 7.2 %collective-permute-start.14 = (bf16[192,1024]{1,0:T(8,128)(2,1)S(1)}, bf16[192,1024]{1,0:T(8,128)(2,1)S(1)}, u32[]{:S(2)}, u32[]{:S(2)}) collective-permute-start(bf16[192,1024]{1,0:T(8,128)(2,1)S(1)} %collective-permute-done.10.refs_6_), channel_id=1, source_target_pairs={{0,4},{4,0},{1,5},{5,1},{2,6},{6,2},{3,7},{7,3},{8,12},{12,8},{9,1... | collective-permute-start | bytes 1179656 | tf_op jit(solution)/shard_map/ppermute | solution.py:227
  99.7 7.1 %collective-permute-start.13 = (bf16[192,1024]{1,0:T(8,128)(2,1)S(1)}, bf16[192,1024]{1,0:T(8,128)(2,1)S(1)}, u32[]{:S(2)}, u32[]{:S(2)}) collective-permute-start(bf16[192,1024]{1,0:T(8,128)(2,1)S(1)} %collective-permute-done.9.refs_5_), channel_id=1, source_target_pairs={{0,4},{4,0},{1,5},{5,1},{2,6},{6,2},{3,7},{7,3},{8,12},{12,8},{9,1... | collective-permute-start | bytes 1179656 | tf_op jit(solution)/shard_map/ppermute | solution.py:227
  100.2 6.7 %collective-permute-start.12 = (bf16[192,1024]{1,0:T(8,128)(2,1)}, bf16[192,1024]{1,0:T(8,128)(2,1)S(1)}, u32[]{:S(2)}, u32[]{:S(2)}) collective-permute-start(bf16[192,1024]{1,0:T(8,128)(2,1)} %collective-permute-done.8.refs_4_), channel_id=1, source_target_pairs={{0,4},{4,0},{1,5},{5,1},{2,6},{6,2},{3,7},{7,3},{8,12},{12,8},{9,1... | collective-permute-start | bytes 1179656 | tf_op jit(solution)/shard_map/ppermute | solution.py:227
  111.8 19.6 %collective-permute-start.15 = (bf16[3,4,16,768]{3,2,1,0:T(8,128)(2,1)}, bf16[3,4,16,768]{3,2,1,0:T(8,128)(2,1)S(1)}, u32[]{:S(2)}, u32[]{:S(2)}) collective-permute-start(bf16[3,4,16,768]{3,2,1,0:T(8,128)(2,1)} %get-tuple-element.38), channel_id=1, source_target_pairs={{0,128},{64,192},{128,0},{192,64},{1,129},{65,193},{129,1},{193,65... | collective-permute-start | bytes 884744 | tf_op jit(solution)/shard_map/ppermute | solution.py:227
  114.6 16.8 %collective-permute-start.16 = (bf16[3,4,16,768]{3,2,1,0:T(8,128)(2,1)}, bf16[3,4,16,768]{3,2,1,0:T(8,128)(2,1)S(1)}, u32[]{:S(2)}, u32[]{:S(2)}) collective-permute-start(bf16[3,4,16,768]{3,2,1,0:T(8,128)(2,1)} %get-tuple-element.39), channel_id=1, source_target_pairs={{0,64},{64,128},{128,192},{192,0},{1,65},{65,129},{129,193},{193,1... | collective-permute-start | bytes 884744 | tf_op jit(solution)/shard_map/ppermute | solution.py:227
  114.6 19.4 %collective-permute-start.17 = (bf16[3,4,16,768]{3,2,1,0:T(8,128)(2,1)}, bf16[3,4,16,768]{3,2,1,0:T(8,128)(2,1)S(1)}, u32[]{:S(2)}, u32[]{:S(2)}) collective-permute-start(bf16[3,4,16,768]{3,2,1,0:T(8,128)(2,1)} %get-tuple-element.40), channel_id=1, source_target_pairs={{0,192},{64,0},{128,64},{192,128},{1,193},{65,1},{129,65},{193,129... | collective-permute-start | bytes 884744 | tf_op jit(solution)/shard_map/ppermute | solution.py:227
  128.4 9.4 %collective-permute-start.21 = (bf16[2,4,16,768]{3,2,1,0:T(8,128)(2,1)S(1)}, bf16[2,4,16,768]{3,2,1,0:T(8,128)(2,1)S(1)}, u32[]{:S(2)}, u32[]{:S(2)}) collective-permute-start(bf16[2,4,16,768]{3,2,1,0:T(8,128)(2,1)S(1)} %get-tuple-element.51), channel_id=1, source_target_pairs={{0,128},{64,192},{128,0},{192,64},{1,129},{65,193},{129,1},{193,65... | collective-permute-start | bytes 589832 | tf_op jit(solution)/shard_map/ppermute | solution.py:227
  129.2 11.3 %collective-permute-start.22 = (bf16[2,4,16,768]{3,2,1,0:T(8,128)(2,1)}, bf16[2,4,16,768]{3,2,1,0:T(8,128)(2,1)S(1)}, u32[]{:S(2)}, u32[]{:S(2)}) collective-permute-start(bf16[2,4,16,768]{3,2,1,0:T(8,128)(2,1)} %get-tuple-element.52), channel_id=1, source_target_pairs={{0,64},{64,128},{128,192},{192,0},{1,65},{65,129},{129,193},{193,1... | collective-permute-start | bytes 589832 | tf_op jit(solution)/shard_map/ppermute | solution.py:227
  131.4 12.1 %collective-permute-start.23 = (bf16[2,4,16,768]{3,2,1,0:T(8,128)(2,1)}, bf16[2,4,16,768]{3,2,1,0:T(8,128)(2,1)S(1)}, u32[]{:S(2)}, u32[]{:S(2)}) collective-permute-start(bf16[2,4,16,768]{3,2,1,0:T(8,128)(2,1)} %get-tuple-element.53), channel_id=1, source_target_pairs={{0,192},{64,0},{128,64},{192,128},{1,193},{65,1},{129,65},{193,129... | collective-permute-start | bytes 589832 | tf_op jit(solution)/shard_map/ppermute | solution.py:227
  131.4 14.8 %collective-permute-start.18 = (bf16[2,4,16,768]{3,2,1,0:T(8,128)(2,1)}, bf16[2,4,16,768]{3,2,1,0:T(8,128)(2,1)S(1)}, u32[]{:S(2)}, u32[]{:S(2)}) collective-permute-start(bf16[2,4,16,768]{3,2,1,0:T(8,128)(2,1)} %get-tuple-element.46), channel_id=1, source_target_pairs={{0,128},{64,192},{128,0},{192,64},{1,129},{65,193},{129,1},{193,65... | collective-permute-start | bytes 589832 | tf_op jit(solution)/shard_map/ppermute | solution.py:227
  134.0 13.7 %collective-permute-start.19 = (bf16[2,4,16,768]{3,2,1,0:T(8,128)(2,1)S(1)}, bf16[2,4,16,768]{3,2,1,0:T(8,128)(2,1)S(1)}, u32[]{:S(2)}, u32[]{:S(2)}) collective-permute-start(bf16[2,4,16,768]{3,2,1,0:T(8,128)(2,1)S(1)} %get-tuple-element.47), channel_id=1, source_target_pairs={{0,64},{64,128},{128,192},{192,0},{1,65},{65,129},{129,193},{193,1... | collective-permute-start | bytes 589832 | tf_op jit(solution)/shard_map/ppermute | solution.py:227
  137.7 11.1 %collective-permute-start.20 = (bf16[2,4,16,768]{3,2,1,0:T(8,128)(2,1)S(1)}, bf16[2,4,16,768]{3,2,1,0:T(8,128)(2,1)S(1)}, u32[]{:S(2)}, u32[]{:S(2)}) collective-permute-start(bf16[2,4,16,768]{3,2,1,0:T(8,128)(2,1)S(1)} %get-tuple-element.48), channel_id=1, source_target_pairs={{0,192},{64,0},{128,64},{192,128},{1,193},{65,1},{129,65},{193,129... | collective-permute-start | bytes 589832 | tf_op jit(solution)/shard_map/ppermute | solution.py:227
  150.1 23.6 %all-to-all-start.3 = ((f32[256,1,4]{2,1,0:T(1,128)}), f32[256,1,4]{2,1,0:T(1,128)S(1)}, u32[]{:S(2)}, u32[]{:S(2)}) async-start(f32[256,1,4]{2,1,0:T(1,128)} %broadcast_in_dim.9), calls=%async_computation.3 | async-start | bytes 262144 | tf_op jit(solution)/shard_map/all_to_all | solution.py:222

commit v8 on v7

--- a/solution.py
+++ b/solution.py
@@ -20,20 +20,23 @@
 UNIT = NX * ROWS
 BLOCK = D // NX
 GROUPS = BLOCK // GROUP
-SENDS = (1, 2, 4)
-PIECES = ((None, 0, 3), (2, 0, 2), (2, 2, 2))
+SENDS = (1, 3, 3)
+PIECES = ((None, 0, 4), (2, 0, 3))
 MIB = 1 << 20
 HALF = BLOCK // 2
 OWN = TOKENS // (NX * NZ * NC)
 LEAD = OWN * HALF // GROUP
 
-SINE = (
-    0.9999996039230294,
-    -6.579691569847717,
-    12.98643599053418,
-    -12.188101430391939,
-    6.558041838366218,
-    -1.9530314806292366,
+SINE = tuple(
+    c / 7.0
+    for c in (
+        0.9999996039230294,
+        -6.579691569847717,
+        12.98643599053418,
+        -12.188101430391939,
+        6.558041838366218,
+        -1.9530314806292366,
+    )
 )
 
 
@@ -116,7 +119,7 @@
         poly = jnp.full_like(square, SINE[-1])
         for coefficient in SINE[-2::-1]:
             poly = poly * square + coefficient
-        shift = (r * poly) * (top * (1.0 / 7.0))
+        shift = (r * poly) * top
         if k:
             shift = shift * inverse_ref[k, pl.ds(group, 1), :]
         dequant = (wide - shift).astype(jnp.bfloat16)

time: 177 us -> 183 us (1.034)
  blocking collectives: 47.1 us -> 53.5 us
  waiting for transfers between devices: 46.1 us -> 51.3 us
  starting transfers between devices: 49.7 us -> 45 us
    all_to_all x1, blocking collectives: 18.8 us -> 25.2 us  [search(): received.append(lax.all_to_all(part, ZC, 0, 0, tiled=True))]
    ppermute x23 -> x20, waiting for transfers between devices: 34.6 us -> 39.6 us  [shifted(): lax.ppermute(value, axis, [(i, (i + hops) % size) for i in range(size)])]
    ppermute x23 -> x20, starting transfers between devices: 30.7 us -> 25.8 us  [shifted(): lax.ppermute(value, axis, [(i, (i + hops) % size) for i in range(size)])]
    pallas_call x2 -> x1, Pallas kernels: 11.7 us -> 8.58 us  [search(): kernel(piece_kernel(first, units), out_shape, flops=3 * work, in_specs=[l...]
    pallas_call x2, Pallas kernels: 6.34 us -> 8.32 us  [search(): deltas.append(step(received[send], scale, inverse))]
  transfers between devices with their start and end apart: 26 -> 23, of which waited for: 14 -> 13; matrix products, arithmetic and copies ran while one was open for 1% -> 1% of each run, Pallas kernels for 14% -> 14%
where the time goes in v8:
time: 183 us; the launch traced here: 181 us
  blocking collectives  53.5 us (29%)
  waiting for transfers between devices  51.3 us (28%)
  starting transfers between devices  45 us (25%)
  Pallas kernels  25.4 us (14%)
  local copies, waits for them, and re-layouts  3.65 us (2%)
    ppermute x20, waiting for transfers between devices, shifted(): lax.ppermute(value, axis, [(i, (i + hops) % size) for i in range(size)])  39.6 us
    all_to_all x1, blocking collectives, search(): received = [lax.all_to_all(merged, ZC, 0, 0, tiled=True)]  28.3 us
    ppermute x20, starting transfers between devices, shifted(): lax.ppermute(value, axis, [(i, (i + hops) % size) for i in range(size)])  25.8 us
    all_to_all x1, blocking collectives, search(): received.append(lax.all_to_all(part, ZC, 0, 0, tiled=True))  25.2 us
    all_to_all x1, starting transfers between devices, spread(): return lax.all_to_all(wide, axes, 0, 0, tiled=True)  12.2 us
    all_to_all x1, waiting for transfers between devices, spread(): return lax.all_to_all(wide, axes, 0, 0, tiled=True)  11.1 us
    pallas_call x1, Pallas kernels, search(): kernel(piece_kernel(first, units), out_shape, flops=3 * work, in_specs=[l...  8.58 us
    pallas_call x2, Pallas kernels, search(): deltas.append(step(received[send], scale, inverse))  8.32 us
  transfers between devices with their start and end apart: 23, of which 13 were waited for; matrix products, arithmetic and copies ran while one was open for 1% of the time, Pallas kernels for 14%

profile of v8, /device:TPU:2, one launch (start us, length us, event | category | flops | bytes accessed | tf_op | source)
XLA Modules:
  0.0 181.0 jit_solution(14224207625077279462)
XLA Ops:
  0.6 0.8 copy-done.1
  1.5 3.5 %collective-permute-start = (bf16[24,1024]{1,0:T(8,128)(2,1)S(1)}, bf16[24,1024]{1,0:T(8,128)(2,1)S(1)}, u32[]{:S(2)}, u32[]{:S(2)}) collective-permute-start(bf16[24,1024]{1,0:T(8,128)(2,1)S(1)} %shard_map.49), channel_id=1, source_target_pairs={{0,0},{1,64},{2,128},{3,192},{64,1},{65,65},{66,129},{67,193},{128... | collective-permute-start | bytes 147464 | tf_op jit(solution)/shard_map/ppermute | solution.py:244
  5.0 1.5 copy-done
  6.5 1.4 shard_map.50
  7.9 0.5 collective-permute-done.tokens_ref
  8.4 0.1 shard_map.51
  8.5 28.3 %all_to_all.20.parts_ref.columns_ref = bf16[16,160,128]{2,1,0:T(8,128)(2,1)S(1)} all-to-all(bf16[16,160,128]{2,1,0:T(8,128)(2,1)S(1)} %shard_map.51), channel_id=1, replica_groups=mesh['dp_0'=4,'dp_1'=8,'dp_2'=2,'tensor'=4] {'dp_1','dp_2'}, dimensions={0} | all-to-all | bytes 1310720 | tf_op jit(solution)/shard_map/all_to_all | solution.py:250
  36.8 0.2 shard_map.52
  37.0 25.2 %all_to_all.21.columns_ref = bf16[16,192,128]{2,1,0:T(8,128)(2,1)S(1)} all-to-all(bf16[16,192,128]{2,1,0:T(8,128)(2,1)S(1)} %get-tuple-element.31), channel_id=1, replica_groups=mesh['dp_0'=4,'dp_1'=8,'dp_2'=2,'tensor'=4] {'dp_1','dp_2'}, dimensions={0} | all-to-all | bytes 1572864 | tf_op jit(solution)/shard_map/all_to_all | solution.py:255
  62.2 3.6 %all-to-all-start.2 = ((bf16[16,192,128]{2,1,0:T(8,128)(2,1)}), bf16[16,192,128]{2,1,0:T(8,128)(2,1)S(1)}, u32[]{:S(2)}, u32[]{:S(2)}) async-start(bf16[16,192,128]{2,1,0:T(8,128)(2,1)} %get-tuple-element.37), calls=%async_computation.2 | async-start | bytes 1572864 | tf_op jit(solution)/shard_map/all_to_all | solution.py:255
  65.8 6.1 %collective-permute-start.10 = (bf16[192,1024]{1,0:T(8,128)(2,1)S(1)}, bf16[192,1024]{1,0:T(8,128)(2,1)S(1)}, u32[]{:S(2)}, u32[]{:S(2)}) collective-permute-start(bf16[192,1024]{1,0:T(8,128)(2,1)S(1)} %get-tuple-element.30.refs_3_), channel_id=1, source_target_pairs={{0,3},{1,0},{2,1},{3,2},{4,7},{5,4},{6,5},{7,6},{8,11},{9,8},{10,9... | collective-permute-start | bytes 1179656 | tf_op jit(solution)/shard_map/ppermute | solution.py:230
  71.9 1.6 collective-permute-start.8
  73.4 1.7 collective-permute-start.3
  75.1 0.9 collective-permute-start.2
  76.0 13.7 %collective-permute-done.3 = f32[8,128]{1,0:T(8,128)S(1)} collective-permute-done((f32[8,128]{1,0:T(8,128)S(1)}, f32[8,128]{1,0:T(8,128)S(1)}, u32[]{:S(2)}, u32[]{:S(2)}) %collective-permute-start.3) | collective-permute-done | bytes 4128 | tf_op jit(solution)/shard_map/ppermute | solution.py:230
  89.7 2.0 %collective-permute-start.1 = (f32[8,128]{1,0:T(8,128)S(1)}, f32[8,128]{1,0:T(8,128)S(1)}, u32[]{:S(2)}, u32[]{:S(2)}) collective-permute-start(f32[8,128]{1,0:T(8,128)S(1)} %get-tuple-element.26), channel_id=1, source_target_pairs={{0,2},{1,3},{2,0},{3,1},{4,6},{5,7},{6,4},{7,5},{8,10},{9,11},{10,... | collective-permute-start | bytes 12296 | tf_op jit(solution)/shard_map/ppermute | solution.py:230
  91.7 1.4 collective-permute-done.2
  93.1 1.7 collective-permute-done.1
  94.9 1.2 collective-permute-done.4.other_ref
  96.0 0.5 collective-permute-start.7
  96.5 1.6 collective-permute-start.6
  98.0 1.6 collective-permute-done.7.mean_3
  99.7 2.7 %collective-permute-start.5 = (f32[16,128]{1,0:T(8,128)S(1)}, f32[16,128]{1,0:T(8,128)S(1)}, u32[]{:S(2)}, u32[]{:S(2)}) collective-permute-start(f32[16,128]{1,0:T(8,128)S(1)} %shard_map.53.mean_0), channel_id=1, source_target_pairs={{0,128},{64,192},{128,0},{192,64},{1,129},{65,193},{129,1},{193,65... | collective-permute-start | bytes 24584 | tf_op jit(solution)/shard_map/ppermute | solution.py:230
  102.4 2.4 %collective-permute-done.5.mean_1 = f32[16,128]{1,0:T(8,128)S(1)} collective-permute-done((f32[16,128]{1,0:T(8,128)S(1)}, f32[16,128]{1,0:T(8,128)S(1)}, u32[]{:S(2)}, u32[]{:S(2)}) %collective-permute-start.5) | collective-permute-done | bytes 8224 | tf_op jit(solution)/shard_map/ppermute | solution.py:230
  104.8 0.3 shard_map.54
  105.3 0.5 collective-permute-start.13
  105.8 0.3 collective-permute-start.12
  106.0 2.1 %shard_map.55.refs_1_ = bf16[1,256,2048]{2,1,0:T(8,128)(2,1)S(1)} custom-call(bf16[16,160,128]{2,1,0:T(8,128)(2,1)S(1)} %all_to_all.20.parts_ref.columns_ref, f32[4,16,128]{2,1,0:T(8,128)S(1)} %get-tuple-element.27.scale_ref, f32[4,16,128]{2,1,0:T(8,128)S(1)} %get-tuple-element.28.inverse_ref), custom_call_target="tpu_custom_call" | custom-call | flops 3221225472 | tf_op jit(solution)/shard_map/pallas_call | solution.py:279
  108.1 6.2 %shard_map.56.refs_2_ = bf16[3,256,2048]{2,1,0:T(8,128)(2,1)S(1)} custom-call(bf16[16,192,128]{2,1,0:T(8,128)(2,1)S(1)} %all_to_all.21.columns_ref, f32[4,16,128]{2,1,0:T(8,128)S(1)} %get-tuple-element.27.scale_ref, f32[4,16,128]{2,1,0:T(8,128)S(1)} %get-tuple-element.28.inverse_ref), custom_call_target="tpu_custom_call" | custom-call | flops 3221225472 | tf_op jit(solution)/shard_map/pallas_call | solution.py:279
  114.4 5.8 %shard_map.57 = (bf16[4,4,16,768]{3,2,1,0:T(8,128)(2,1)S(1)}, bf16[4,4,16,768]{3,2,1,0:T(8,128)(2,1)}, bf16[4,4,16,768]{3,2,1,0:T(8,128)(2,1)}, bf16[4,4,16,768]{3,2,1,0:T(8,128)(2,1)}, bf16[768,2048]{1,0:T(8,128)(2,1)}) custom-call(s32[1]{0:T(128)} %bitcast.core_ref.refs_0_, bf16[1,256,2048]{2,1,0:T(8,128)(2,1)S(1)} %shard_map.55.refs_1_, ...), custom_call_target="tpu_custom_call" | custom-call | flops 1610612736 | tf_op jit(solution)/shard_map/pallas_call | solution.py:280
  120.3 2.8 %collective-permute-start.15 = (bf16[4,4,16,768]{3,2,1,0:T(8,128)(2,1)}, bf16[4,4,16,768]{3,2,1,0:T(8,128)(2,1)S(1)}, u32[]{:S(2)}, u32[]{:S(2)}) collective-permute-start(bf16[4,4,16,768]{3,2,1,0:T(8,128)(2,1)} %get-tuple-element.33), channel_id=1, source_target_pairs={{0,128},{64,192},{128,0},{192,64},{1,129},{65,193},{129,1},{193,65... | collective-permute-start | bytes 1179656 | tf_op jit(solution)/shard_map/ppermute | solution.py:230
  123.1 2.0 %collective-permute-start.17 = (bf16[4,4,16,768]{3,2,1,0:T(8,128)(2,1)}, bf16[4,4,16,768]{3,2,1,0:T(8,128)(2,1)S(1)}, u32[]{:S(2)}, u32[]{:S(2)}) collective-permute-start(bf16[4,4,16,768]{3,2,1,0:T(8,128)(2,1)} %get-tuple-element.35), channel_id=1, source_target_pairs={{0,192},{64,0},{128,64},{192,128},{1,193},{65,1},{129,65},{193,129... | collective-permute-start | bytes 1179656 | tf_op jit(solution)/shard_map/ppermute | solution.py:230
  125.1 8.6 %shard_map.58 = (bf16[3,4,16,768]{3,2,1,0:T(8,128)(2,1)S(1)}, bf16[3,4,16,768]{3,2,1,0:T(8,128)(2,1)}, bf16[3,4,16,768]{3,2,1,0:T(8,128)(2,1)}, bf16[3,4,16,768]{3,2,1,0:T(8,128)(2,1)S(1)}) custom-call(bf16[16,192,128]{2,1,0:T(8,128)(2,1)S(1)} %all-to-all-done.2.columns_ref, f32[4,16,128]{2,1,0:T(8,128)S(1)} %get-tuple-element.27.scale_ref, ...), custom_call_target="tpu_custom_call" | custom-call | flops 3623878656 | tf_op jit(solution)/shard_map/pallas_call | solution.py:287
  133.7 0.9 collective-permute-start.18
  134.6 2.2 %collective-permute-start.19 = (bf16[3,4,16,768]{3,2,1,0:T(8,128)(2,1)}, bf16[3,4,16,768]{3,2,1,0:T(8,128)(2,1)S(1)}, u32[]{:S(2)}, u32[]{:S(2)}) collective-permute-start(bf16[3,4,16,768]{3,2,1,0:T(8,128)(2,1)} %get-tuple-element.42), channel_id=1, source_target_pairs={{0,64},{64,128},{128,192},{192,0},{1,65},{65,129},{129,193},{193,1... | collective-permute-start | bytes 884744 | tf_op jit(solution)/shard_map/ppermute | solution.py:230
  136.8 5.3 %collective-permute-done.16.refs_2_ = bf16[4,4,16,768]{3,2,1,0:T(8,128)(2,1)S(1)} collective-permute-done((bf16[4,4,16,768]{3,2,1,0:T(8,128)(2,1)}, bf16[4,4,16,768]{3,2,1,0:T(8,128)(2,1)S(1)}, u32[]{:S(2)}, u32[]{:S(2)}) %collective-permute-start.16) | collective-permute-done | bytes 393248 | tf_op jit(solution)/shard_map/ppermute | solution.py:230
  142.0 0.5 collective-permute-done.17.refs_3_
  142.6 6.3 %collective-permute-done.18.refs_5_ = bf16[3,4,16,768]{3,2,1,0:T(8,128)(2,1)S(1)} collective-permute-done((bf16[3,4,16,768]{3,2,1,0:T(8,128)(2,1)}, bf16[3,4,16,768]{3,2,1,0:T(8,128)(2,1)S(1)}, u32[]{:S(2)}, u32[]{:S(2)}) %collective-permute-start.18) | collective-permute-done | bytes 294944 | tf_op jit(solution)/shard_map/ppermute | solution.py:230
  148.9 5.1 %collective-permute-done.19.refs_6_ = bf16[3,4,16,768]{3,2,1,0:T(8,128)(2,1)S(1)} collective-permute-done((bf16[3,4,16,768]{3,2,1,0:T(8,128)(2,1)}, bf16[3,4,16,768]{3,2,1,0:T(8,128)(2,1)S(1)}, u32[]{:S(2)}, u32[]{:S(2)}) %collective-permute-start.19) | collective-permute-done | bytes 294944 | tf_op jit(solution)/shard_map/ppermute | solution.py:230
  154.0 0.4 collective-permute-done.20.refs_7_
  154.4 0.6 shard_map.59
  155.0 0.7 broadcast_in_dim.9
  155.7 12.2 %all-to-all-start.3 = ((f32[256,1,4]{2,1,0:T(1,128)}), f32[256,1,4]{2,1,0:T(1,128)S(1)}, u32[]{:S(2)}, u32[]{:S(2)}) async-start(f32[256,1,4]{2,1,0:T(1,128)} %broadcast_in_dim.9), calls=%async_computation.3 | async-start | bytes 262144 | tf_op jit(solution)/shard_map/all_to_all | solution.py:225
  167.9 0.6 broadcast_multiply_fusion
  168.5 0.6 dynamic_slice.3
  169.1 11.1 %all-to-all-done.3 = f32[256,1,4]{2,1,0:T(1,128)S(1)} async-done(((f32[256,1,4]{2,1,0:T(1,128)}), f32[256,1,4]{2,1,0:T(1,128)S(1)}, u32[]{:S(2)}, u32[]{:S(2)}) %all-to-all-start.3) | async-done | bytes 4128 | tf_op jit(solution)/shard_map/all_to_all | solution.py:225
  180.2 0.3 reduce_sum.9
  180.5 0.5 broadcast_multiply_fusion.1
  (21 shorter events, 0.2 us)
Async XLA Ops:
  0.6 0.8 copy-start.1
  1.5 6.9 %collective-permute-start = (bf16[24,1024]{1,0:T(8,128)(2,1)S(1)}, bf16[24,1024]{1,0:T(8,128)(2,1)S(1)}, u32[]{:S(2)}, u32[]{:S(2)}) collective-permute-start(bf16[24,1024]{1,0:T(8,128)(2,1)S(1)} %shard_map.49), channel_id=1, source_target_pairs={{0,0},{1,64},{2,128},{3,192},{64,1},{65,65},{66,129},{67,193},{128... | collective-permute-start | bytes 147464 | tf_op jit(solution)/shard_map/ppermute | solution.py:244
  5.0 1.5 copy-start
  62.2 62.9 %all-to-all-start.2 = ((bf16[16,192,128]{2,1,0:T(8,128)(2,1)}), bf16[16,192,128]{2,1,0:T(8,128)(2,1)S(1)}, u32[]{:S(2)}, u32[]{:S(2)}) async-start(bf16[16,192,128]{2,1,0:T(8,128)(2,1)} %get-tuple-element.37), calls=%async_computation.2 | async-start | bytes 1572864 | tf_op jit(solution)/shard_map/all_to_all | solution.py:255
  65.8 39.4 %collective-permute-start.10 = (bf16[192,1024]{1,0:T(8,128)(2,1)S(1)}, bf16[192,1024]{1,0:T(8,128)(2,1)S(1)}, u32[]{:S(2)}, u32[]{:S(2)}) collective-permute-start(bf16[192,1024]{1,0:T(8,128)(2,1)S(1)} %get-tuple-element.30.refs_3_), channel_id=1, source_target_pairs={{0,3},{1,0},{2,1},{3,2},{4,7},{5,4},{6,5},{7,6},{8,11},{9,8},{10,9... | collective-permute-start | bytes 1179656 | tf_op jit(solution)/shard_map/ppermute | solution.py:230
  71.9 33.4 %collective-permute-start.9 = (bf16[192,1024]{1,0:T(8,128)(2,1)S(1)}, bf16[192,1024]{1,0:T(8,128)(2,1)S(1)}, u32[]{:S(2)}, u32[]{:S(2)}) collective-permute-start(bf16[192,1024]{1,0:T(8,128)(2,1)S(1)} %get-tuple-element.30.refs_3_), channel_id=1, source_target_pairs={{0,1},{1,2},{2,3},{3,0},{4,5},{5,6},{6,7},{7,4},{8,9},{9,10},{10,1... | collective-permute-start | bytes 1179656 | tf_op jit(solution)/shard_map/ppermute | solution.py:230
  71.9 33.9 %collective-permute-start.8 = (bf16[192,1024]{1,0:T(8,128)(2,1)S(1)}, bf16[192,1024]{1,0:T(8,128)(2,1)}, u32[]{:S(2)}, u32[]{:S(2)}) collective-permute-start(bf16[192,1024]{1,0:T(8,128)(2,1)S(1)} %get-tuple-element.30.refs_3_), channel_id=1, source_target_pairs={{0,2},{1,3},{2,0},{3,1},{4,6},{5,7},{6,4},{7,5},{8,10},{9,11},{10,... | collective-permute-start | bytes 1179656 | tf_op jit(solution)/shard_map/ppermute | solution.py:230
  73.4 16.3 %collective-permute-start.3 = (f32[8,128]{1,0:T(8,128)S(1)}, f32[8,128]{1,0:T(8,128)S(1)}, u32[]{:S(2)}, u32[]{:S(2)}) collective-permute-start(f32[8,128]{1,0:T(8,128)S(1)} %get-tuple-element.26), channel_id=1, source_target_pairs={{0,3},{1,0},{2,1},{3,2},{4,7},{5,4},{6,5},{7,6},{8,11},{9,8},{10,9... | collective-permute-start | bytes 12296 | tf_op jit(solution)/shard_map/ppermute | solution.py:230
  75.1 18.0 %collective-permute-start.2 = (f32[8,128]{1,0:T(8,128)S(1)}, f32[8,128]{1,0:T(8,128)S(1)}, u32[]{:S(2)}, u32[]{:S(2)}) collective-permute-start(f32[8,128]{1,0:T(8,128)S(1)} %get-tuple-element.26), channel_id=1, source_target_pairs={{0,1},{1,2},{2,3},{3,0},{4,5},{5,6},{6,7},{7,4},{8,9},{9,10},{10,1... | collective-permute-start | bytes 12296 | tf_op jit(solution)/shard_map/ppermute | solution.py:230
  89.7 5.1 %collective-permute-start.1 = (f32[8,128]{1,0:T(8,128)S(1)}, f32[8,128]{1,0:T(8,128)S(1)}, u32[]{:S(2)}, u32[]{:S(2)}) collective-permute-start(f32[8,128]{1,0:T(8,128)S(1)} %get-tuple-element.26), channel_id=1, source_target_pairs={{0,2},{1,3},{2,0},{3,1},{4,6},{5,7},{6,4},{7,5},{8,10},{9,11},{10,... | collective-permute-start | bytes 12296 | tf_op jit(solution)/shard_map/ppermute | solution.py:230
  94.8 1.2 collective-permute-start.4
  96.0 3.7 %collective-permute-start.7 = (f32[16,128]{1,0:T(8,128)S(1)}, f32[16,128]{1,0:T(8,128)S(1)}, u32[]{:S(2)}, u32[]{:S(2)}) collective-permute-start(f32[16,128]{1,0:T(8,128)S(1)} %shard_map.53.mean_0), channel_id=1, source_target_pairs={{0,192},{64,0},{128,64},{192,128},{1,193},{65,1},{129,65},{193,129... | collective-permute-start | bytes 24584 | tf_op jit(solution)/shard_map/ppermute | solution.py:230
  96.5 5.9 %collective-permute-start.6 = (f32[16,128]{1,0:T(8,128)S(1)}, f32[16,128]{1,0:T(8,128)S(1)}, u32[]{:S(2)}, u32[]{:S(2)}) collective-permute-start(f32[16,128]{1,0:T(8,128)S(1)} %shard_map.53.mean_0), channel_id=1, source_target_pairs={{0,64},{64,128},{128,192},{192,0},{1,65},{65,129},{129,193},{193,1... | collective-permute-start | bytes 24584 | tf_op jit(solution)/shard_map/ppermute | solution.py:230
  99.7 5.2 %collective-permute-start.5 = (f32[16,128]{1,0:T(8,128)S(1)}, f32[16,128]{1,0:T(8,128)S(1)}, u32[]{:S(2)}, u32[]{:S(2)}) collective-permute-start(f32[16,128]{1,0:T(8,128)S(1)} %shard_map.53.mean_0), channel_id=1, source_target_pairs={{0,128},{64,192},{128,0},{192,64},{1,129},{65,193},{129,1},{193,65... | collective-permute-start | bytes 24584 | tf_op jit(solution)/shard_map/ppermute | solution.py:230
  102.4 12.0 %collective-permute-start.11 = (bf16[192,1024]{1,0:T(8,128)(2,1)S(1)}, bf16[192,1024]{1,0:T(8,128)(2,1)S(1)}, u32[]{:S(2)}, u32[]{:S(2)}) collective-permute-start(bf16[192,1024]{1,0:T(8,128)(2,1)S(1)} %get-tuple-element.30.refs_3_), channel_id=1, source_target_pairs={{0,4},{4,0},{1,5},{5,1},{2,6},{6,2},{3,7},{7,3},{8,12},{12,8},{9,1... | collective-permute-start | bytes 1179656 | tf_op jit(solution)/shard_map/ppermute | solution.py:230
  105.2 9.2 %collective-permute-start.14 = (bf16[192,1024]{1,0:T(8,128)(2,1)S(1)}, bf16[192,1024]{1,0:T(8,128)(2,1)S(1)}, u32[]{:S(2)}, u32[]{:S(2)}) collective-permute-start(bf16[192,1024]{1,0:T(8,128)(2,1)S(1)} %collective-permute-done.10.refs_6_), channel_id=1, source_target_pairs={{0,4},{4,0},{1,5},{5,1},{2,6},{6,2},{3,7},{7,3},{8,12},{12,8},{9,1... | collective-permute-start | bytes 1179656 | tf_op jit(solution)/shard_map/ppermute | solution.py:230
  105.3 9.1 %collective-permute-start.13 = (bf16[192,1024]{1,0:T(8,128)(2,1)S(1)}, bf16[192,1024]{1,0:T(8,128)(2,1)S(1)}, u32[]{:S(2)}, u32[]{:S(2)}) collective-permute-start(bf16[192,1024]{1,0:T(8,128)(2,1)S(1)} %collective-permute-done.9.refs_5_), channel_id=1, source_target_pairs={{0,4},{4,0},{1,5},{5,1},{2,6},{6,2},{3,7},{7,3},{8,12},{12,8},{9,1... | collective-permute-start | bytes 1179656 | tf_op jit(solution)/shard_map/ppermute | solution.py:230
  105.8 8.6 %collective-permute-start.12 = (bf16[192,1024]{1,0:T(8,128)(2,1)}, bf16[192,1024]{1,0:T(8,128)(2,1)S(1)}, u32[]{:S(2)}, u32[]{:S(2)}) collective-permute-start(bf16[192,1024]{1,0:T(8,128)(2,1)} %collective-permute-done.8.refs_4_), channel_id=1, source_target_pairs={{0,4},{4,0},{1,5},{5,1},{2,6},{6,2},{3,7},{7,3},{8,12},{12,8},{9,1... | collective-permute-start | bytes 1179656 | tf_op jit(solution)/shard_map/ppermute | solution.py:230
  120.3 16.5 %collective-permute-start.15 = (bf16[4,4,16,768]{3,2,1,0:T(8,128)(2,1)}, bf16[4,4,16,768]{3,2,1,0:T(8,128)(2,1)S(1)}, u32[]{:S(2)}, u32[]{:S(2)}) collective-permute-start(bf16[4,4,16,768]{3,2,1,0:T(8,128)(2,1)} %get-tuple-element.33), channel_id=1, source_target_pairs={{0,128},{64,192},{128,0},{192,64},{1,129},{65,193},{129,1},{193,65... | collective-permute-start | bytes 1179656 | tf_op jit(solution)/shard_map/ppermute | solution.py:230
  123.1 18.9 %collective-permute-start.16 = (bf16[4,4,16,768]{3,2,1,0:T(8,128)(2,1)}, bf16[4,4,16,768]{3,2,1,0:T(8,128)(2,1)S(1)}, u32[]{:S(2)}, u32[]{:S(2)}) collective-permute-start(bf16[4,4,16,768]{3,2,1,0:T(8,128)(2,1)} %get-tuple-element.34), channel_id=1, source_target_pairs={{0,64},{64,128},{128,192},{192,0},{1,65},{65,129},{129,193},{193,1... | collective-permute-start | bytes 1179656 | tf_op jit(solution)/shard_map/ppermute | solution.py:230
  123.1 19.5 %collective-permute-start.17 = (bf16[4,4,16,768]{3,2,1,0:T(8,128)(2,1)}, bf16[4,4,16,768]{3,2,1,0:T(8,128)(2,1)S(1)}, u32[]{:S(2)}, u32[]{:S(2)}) collective-permute-start(bf16[4,4,16,768]{3,2,1,0:T(8,128)(2,1)} %get-tuple-element.35), channel_id=1, source_target_pairs={{0,192},{64,0},{128,64},{192,128},{1,193},{65,1},{129,65},{193,129... | collective-permute-start | bytes 1179656 | tf_op jit(solution)/shard_map/ppermute | solution.py:230
  133.7 15.2 %collective-permute-start.18 = (bf16[3,4,16,768]{3,2,1,0:T(8,128)(2,1)}, bf16[3,4,16,768]{3,2,1,0:T(8,128)(2,1)S(1)}, u32[]{:S(2)}, u32[]{:S(2)}) collective-permute-start(bf16[3,4,16,768]{3,2,1,0:T(8,128)(2,1)} %get-tuple-element.41), channel_id=1, source_target_pairs={{0,128},{64,192},{128,0},{192,64},{1,129},{65,193},{129,1},{193,65... | collective-permute-start | bytes 884744 | tf_op jit(solution)/shard_map/ppermute | solution.py:230
  134.6 19.4 %collective-permute-start.19 = (bf16[3,4,16,768]{3,2,1,0:T(8,128)(2,1)}, bf16[3,4,16,768]{3,2,1,0:T(8,128)(2,1)S(1)}, u32[]{:S(2)}, u32[]{:S(2)}) collective-permute-start(bf16[3,4,16,768]{3,2,1,0:T(8,128)(2,1)} %get-tuple-element.42), channel_id=1, source_target_pairs={{0,64},{64,128},{128,192},{192,0},{1,65},{65,129},{129,193},{193,1... | collective-permute-start | bytes 884744 | tf_op jit(solution)/shard_map/ppermute | solution.py:230
  136.8 17.6 %collective-permute-start.20 = (bf16[3,4,16,768]{3,2,1,0:T(8,128)(2,1)S(1)}, bf16[3,4,16,768]{3,2,1,0:T(8,128)(2,1)S(1)}, u32[]{:S(2)}, u32[]{:S(2)}) collective-permute-start(bf16[3,4,16,768]{3,2,1,0:T(8,128)(2,1)S(1)} %get-tuple-element.43), channel_id=1, source_target_pairs={{0,192},{64,0},{128,64},{192,128},{1,193},{65,1},{129,65},{193,129... | collective-permute-start | bytes 884744 | tf_op jit(solution)/shard_map/ppermute | solution.py:230
  155.7 24.5 %all-to-all-start.3 = ((f32[256,1,4]{2,1,0:T(1,128)}), f32[256,1,4]{2,1,0:T(1,128)S(1)}, u32[]{:S(2)}, u32[]{:S(2)}) async-start(f32[256,1,4]{2,1,0:T(1,128)} %broadcast_in_dim.9), calls=%async_computation.3 | async-start | bytes 262144 | tf_op jit(solution)/shard_map/all_to_all | solution.py:225

commit v9 on v8

--- a/solution.py
+++ b/solution.py
@@ -20,8 +20,8 @@
 UNIT = NX * ROWS
 BLOCK = D // NX
 GROUPS = BLOCK // GROUP
-SENDS = (1, 3, 3)
-PIECES = ((None, 0, 4), (2, 0, 3))
+SENDS = (1, 2, 4)
+PIECES = ((None, 0, 3), (2, 0, 2), (2, 2, 2))
 MIB = 1 << 20
 HALF = BLOCK // 2
 OWN = TOKENS // (NX * NZ * NC)
@@ -293,9 +293,12 @@
             )(after(received[source], shares[-NX]), scale, inverse, pltpu.with_memory_space_constraint(tokens, pltpu.HBM))
         shares += [partial[0]] + [shifted(partial[hops], "dp_0", hops) for hops in (2, 1, 3)]
     sums, totals = kernel(error_kernel, [array((GRID, UNITS * ROWS), f32), array((1, GRID), f32)])(*shares)
+    totals = totals + shifted(totals, "dp_2", 1)
+    around = [shifted(totals, "dp_0", hops) for hops in (2, 1, 3)]
+    totals = (totals + around[0]) + (around[1] + around[2])
     own_mean = lax.dynamic_slice_in_dim(after(mean, sums).reshape(-1), lax.axis_index(ZC) * GROUP, GROUP)
-    errors = jnp.sum(spread(totals, ("dp_0", "dp_1", "dp_2", "tensor"), NX * NZ * NC * NY), axis=0).reshape(GRID) / (TOKENS * F)
-    column_errors = sums / TOKENS
+    errors = jnp.sum(spread(totals, ("dp_1", "tensor"), NZ * NY), axis=0).reshape(GRID) / (TOKENS * F)
+    column_errors = after(sums, totals) / TOKENS
     return (own_mean, column_errors, errors)
 
 

time: 183 us -> 179 us (0.978)
  blocking collectives: 53.5 us -> 47.1 us
  starting transfers between devices: 45 us -> 50.9 us
  waiting for transfers between devices: 51.3 us -> 47.6 us
    ppermute x20 -> x27, starting transfers between devices: 25.8 us -> 35 us  [shifted(): lax.ppermute(value, axis, [(i, (i + hops) % size) for i in range(size)])]
    all_to_all x1, blocking collectives: 25.2 us -> 18.8 us  [search(): received.append(lax.all_to_all(part, ZC, 0, 0, tiled=True))]
    all_to_all x1, starting transfers between devices: 12.2 us -> 8.19 us  [spread(): return lax.all_to_all(wide, axes, 0, 0, tiled=True)]
    pallas_call x1 -> x2, Pallas kernels: 8.58 us -> 11.6 us  [search(): kernel(piece_kernel(first, units), out_shape, flops=3 * work, in_specs=[l...]
    pallas_call x2, Pallas kernels: 8.32 us -> 6.23 us  [search(): deltas.append(step(received[send], scale, inverse))]
    all_to_all x1, waiting for transfers between devices: 11.1 us -> 9.19 us  [spread(): return lax.all_to_all(wide, axes, 0, 0, tiled=True)]
    ppermute x20 -> x27, waiting for transfers between devices: 39.6 us -> 38 us  [shifted(): lax.ppermute(value, axis, [(i, (i + hops) % size) for i in range(size)])]
  transfers between devices with their start and end apart: 23 -> 30, of which waited for: 13 -> 17; matrix products, arithmetic and copies ran while one was open for 1% -> 1% of each run, Pallas kernels for 14% -> 14%
where the time goes in v9:
time: 179 us; the launch traced here: 177 us
  starting transfers between devices  50.9 us (28%)
  waiting for transfers between devices  47.6 us (27%)
  blocking collectives  47.1 us (26%)
  Pallas kernels  25.5 us (14%)
  local copies, waits for them, and re-layouts  3.52 us (2%)
    ppermute x27, waiting for transfers between devices, shifted(): lax.ppermute(value, axis, [(i, (i + hops) % size) for i in range(size)])  38 us
    ppermute x27, starting transfers between devices, shifted(): lax.ppermute(value, axis, [(i, (i + hops) % size) for i in range(size)])  35 us
    all_to_all x1, blocking collectives, search(): received = [lax.all_to_all(merged, ZC, 0, 0, tiled=True)]  28.3 us
    all_to_all x1, blocking collectives, search(): received.append(lax.all_to_all(part, ZC, 0, 0, tiled=True))  18.8 us
    pallas_call x2, Pallas kernels, search(): kernel(piece_kernel(first, units), out_shape, flops=3 * work, in_specs=[l...  11.6 us
    all_to_all x1, waiting for transfers between devices, spread(): return lax.all_to_all(wide, axes, 0, 0, tiled=True)  9.19 us
    all_to_all x1, starting transfers between devices, spread(): return lax.all_to_all(wide, axes, 0, 0, tiled=True)  8.19 us
    pallas_call x2, Pallas kernels, search(): deltas.append(step(received[send], scale, inverse))  6.23 us
  transfers between devices with their start and end apart: 30, of which 17 were waited for; matrix products, arithmetic and copies ran while one was open for 1% of the time, Pallas kernels for 14%

profile of v9, /device:TPU:2, one launch (start us, length us, event | category | flops | bytes accessed | tf_op | source)
XLA Modules:
  0.0 176.7 jit_solution(4016411910639716542)
XLA Ops:
  0.6 0.8 copy-done.1
  1.5 3.5 %collective-permute-start = (bf16[24,1024]{1,0:T(8,128)(2,1)S(1)}, bf16[24,1024]{1,0:T(8,128)(2,1)S(1)}, u32[]{:S(2)}, u32[]{:S(2)}) collective-permute-start(bf16[24,1024]{1,0:T(8,128)(2,1)S(1)} %shard_map.49), channel_id=1, source_target_pairs={{0,0},{1,64},{2,128},{3,192},{64,1},{65,65},{66,129},{67,193},{128... | collective-permute-start | bytes 147464 | tf_op jit(solution)/shard_map/ppermute | solution.py:244
  5.0 1.5 copy-done
  6.5 1.5 shard_map.50
  8.5 28.3 %all_to_all.20.parts_ref.columns_ref = bf16[16,160,128]{2,1,0:T(8,128)(2,1)S(1)} all-to-all(bf16[16,160,128]{2,1,0:T(8,128)(2,1)S(1)} %shard_map.51), channel_id=1, replica_groups=mesh['dp_0'=4,'dp_1'=8,'dp_2'=2,'tensor'=4] {'dp_1','dp_2'}, dimensions={0} | all-to-all | bytes 1310720 | tf_op jit(solution)/shard_map/all_to_all | solution.py:250
  37.0 18.8 %all_to_all.21.columns_ref = bf16[16,128,128]{2,1,0:T(8,128)(2,1)S(1)} all-to-all(bf16[16,128,128]{2,1,0:T(8,128)(2,1)S(1)} %get-tuple-element.37), channel_id=1, replica_groups=mesh['dp_0'=4,'dp_1'=8,'dp_2'=2,'tensor'=4] {'dp_1','dp_2'}, dimensions={0} | all-to-all | bytes 1048576 | tf_op jit(solution)/shard_map/all_to_all | solution.py:255
  55.8 4.2 %all-to-all-start.2 = ((bf16[16,256,128]{2,1,0:T(8,128)(2,1)}), bf16[16,256,128]{2,1,0:T(8,128)(2,1)S(1)}, u32[]{:S(2)}, u32[]{:S(2)}) async-start(bf16[16,256,128]{2,1,0:T(8,128)(2,1)} %get-tuple-element.43), calls=%async_computation.2 | async-start | bytes 2097152 | tf_op jit(solution)/shard_map/all_to_all | solution.py:255
  60.0 6.1 %collective-permute-start.10 = (bf16[192,1024]{1,0:T(8,128)(2,1)S(1)}, bf16[192,1024]{1,0:T(8,128)(2,1)S(1)}, u32[]{:S(2)}, u32[]{:S(2)}) collective-permute-start(bf16[192,1024]{1,0:T(8,128)(2,1)S(1)} %get-tuple-element.36.refs_3_), channel_id=1, source_target_pairs={{0,3},{1,0},{2,1},{3,2},{4,7},{5,4},{6,5},{7,6},{8,11},{9,8},{10,9... | collective-permute-start | bytes 1179656 | tf_op jit(solution)/shard_map/ppermute | solution.py:230
  66.1 1.6 collective-permute-start.8
  67.7 1.7 collective-permute-start.3
  69.4 0.9 collective-permute-start.2
  70.2 13.9 %collective-permute-done.3 = f32[8,128]{1,0:T(8,128)S(1)} collective-permute-done((f32[8,128]{1,0:T(8,128)S(1)}, f32[8,128]{1,0:T(8,128)S(1)}, u32[]{:S(2)}, u32[]{:S(2)}) %collective-permute-start.3) | collective-permute-done | bytes 4128 | tf_op jit(solution)/shard_map/ppermute | solution.py:230
  84.1 1.6 collective-permute-start.1
  85.8 1.8 %collective-permute-done.2 = f32[8,128]{1,0:T(8,128)S(1)} collective-permute-done((f32[8,128]{1,0:T(8,128)S(1)}, f32[8,128]{1,0:T(8,128)S(1)}, u32[]{:S(2)}, u32[]{:S(2)}) %collective-permute-start.2) | collective-permute-done | bytes 4128 | tf_op jit(solution)/shard_map/ppermute | solution.py:230
  87.6 1.7 collective-permute-done.1
  89.2 1.2 collective-permute-done.4.other_ref
  90.9 1.6 collective-permute-start.6
  92.4 1.6 collective-permute-done.7.mean_3
  94.1 2.7 %collective-permute-start.5 = (f32[16,128]{1,0:T(8,128)S(1)}, f32[16,128]{1,0:T(8,128)S(1)}, u32[]{:S(2)}, u32[]{:S(2)}) collective-permute-start(f32[16,128]{1,0:T(8,128)S(1)} %shard_map.53.mean_0), channel_id=1, source_target_pairs={{0,128},{64,192},{128,0},{192,64},{1,129},{65,193},{129,1},{193,65... | collective-permute-start | bytes 24584 | tf_op jit(solution)/shard_map/ppermute | solution.py:230
  96.8 2.4 %collective-permute-done.5.mean_1 = f32[16,128]{1,0:T(8,128)S(1)} collective-permute-done((f32[16,128]{1,0:T(8,128)S(1)}, f32[16,128]{1,0:T(8,128)S(1)}, u32[]{:S(2)}, u32[]{:S(2)}) %collective-permute-start.5) | collective-permute-done | bytes 8224 | tf_op jit(solution)/shard_map/ppermute | solution.py:230
  100.4 2.1 %shard_map.55.refs_1_ = bf16[1,256,2048]{2,1,0:T(8,128)(2,1)S(1)} custom-call(bf16[16,160,128]{2,1,0:T(8,128)(2,1)S(1)} %all_to_all.20.parts_ref.columns_ref, f32[4,16,128]{2,1,0:T(8,128)S(1)} %get-tuple-element.33.scale_ref, f32[4,16,128]{2,1,0:T(8,128)S(1)} %get-tuple-element.34.inverse_ref), custom_call_target="tpu_custom_call" | custom-call | flops 2415919104 | tf_op jit(solution)/shard_map/pallas_call | solution.py:279
  102.5 4.2 %shard_map.56.refs_2_ = bf16[2,256,2048]{2,1,0:T(8,128)(2,1)S(1)} custom-call(bf16[16,128,128]{2,1,0:T(8,128)(2,1)S(1)} %all_to_all.21.columns_ref, f32[4,16,128]{2,1,0:T(8,128)S(1)} %get-tuple-element.33.scale_ref, f32[4,16,128]{2,1,0:T(8,128)S(1)} %get-tuple-element.34.inverse_ref), custom_call_target="tpu_custom_call" | custom-call | flops 2415919104 | tf_op jit(solution)/shard_map/pallas_call | solution.py:279
  106.7 4.9 %shard_map.57 = (bf16[3,4,16,768]{3,2,1,0:T(8,128)(2,1)S(1)}, bf16[3,4,16,768]{3,2,1,0:T(8,128)(2,1)}, bf16[3,4,16,768]{3,2,1,0:T(8,128)(2,1)}, bf16[3,4,16,768]{3,2,1,0:T(8,128)(2,1)}, bf16[768,2048]{1,0:T(8,128)(2,1)}) custom-call(s32[1]{0:T(128)} %bitcast.core_ref.refs_0_, bf16[1,256,2048]{2,1,0:T(8,128)(2,1)S(1)} %shard_map.55.refs_1_, ...), custom_call_target="tpu_custom_call" | custom-call | flops 1207959552 | tf_op jit(solution)/shard_map/pallas_call | solution.py:280
  111.7 2.8 %collective-permute-start.15 = (bf16[3,4,16,768]{3,2,1,0:T(8,128)(2,1)}, bf16[3,4,16,768]{3,2,1,0:T(8,128)(2,1)S(1)}, u32[]{:S(2)}, u32[]{:S(2)}) collective-permute-start(bf16[3,4,16,768]{3,2,1,0:T(8,128)(2,1)} %get-tuple-element.39), channel_id=1, source_target_pairs={{0,128},{64,192},{128,0},{192,64},{1,129},{65,193},{129,1},{193,65... | collective-permute-start | bytes 884744 | tf_op jit(solution)/shard_map/ppermute | solution.py:230
  114.5 2.0 %collective-permute-start.17 = (bf16[3,4,16,768]{3,2,1,0:T(8,128)(2,1)}, bf16[3,4,16,768]{3,2,1,0:T(8,128)(2,1)S(1)}, u32[]{:S(2)}, u32[]{:S(2)}) collective-permute-start(bf16[3,4,16,768]{3,2,1,0:T(8,128)(2,1)} %get-tuple-element.41), channel_id=1, source_target_pairs={{0,192},{64,0},{128,64},{192,128},{1,193},{65,1},{129,65},{193,129... | collective-permute-start | bytes 884744 | tf_op jit(solution)/shard_map/ppermute | solution.py:230
  116.5 5.8 %shard_map.58 = (bf16[2,4,16,768]{3,2,1,0:T(8,128)(2,1)S(1)}, bf16[2,4,16,768]{3,2,1,0:T(8,128)(2,1)S(1)}, bf16[2,4,16,768]{3,2,1,0:T(8,128)(2,1)}, bf16[2,4,16,768]{3,2,1,0:T(8,128)(2,1)S(1)}) custom-call(bf16[16,256,128]{2,1,0:T(8,128)(2,1)S(1)} %all-to-all-done.2.columns_ref, f32[4,16,128]{2,1,0:T(8,128)S(1)} %get-tuple-element.33.scale_ref, ...), custom_call_target="tpu_custom_call" | custom-call | flops 2415919104 | tf_op jit(solution)/shard_map/pallas_call | solution.py:287
  122.3 5.8 %shard_map.59 = (bf16[2,4,16,768]{3,2,1,0:T(8,128)(2,1)S(1)}, bf16[2,4,16,768]{3,2,1,0:T(8,128)(2,1)}, bf16[2,4,16,768]{3,2,1,0:T(8,128)(2,1)S(1)}, bf16[2,4,16,768]{3,2,1,0:T(8,128)(2,1)}) custom-call(bf16[16,256,128]{2,1,0:T(8,128)(2,1)S(1)} %all-to-all-done.2.columns_ref, f32[4,16,128]{2,1,0:T(8,128)S(1)} %get-tuple-element.33.scale_ref, ...), custom_call_target="tpu_custom_call" | custom-call | flops 2415919104 | tf_op jit(solution)/shard_map/pallas_call | solution.py:287
  128.2 0.9 collective-permute-start.21
  129.1 2.2 %collective-permute-start.22 = (bf16[2,4,16,768]{3,2,1,0:T(8,128)(2,1)}, bf16[2,4,16,768]{3,2,1,0:T(8,128)(2,1)S(1)}, u32[]{:S(2)}, u32[]{:S(2)}) collective-permute-start(bf16[2,4,16,768]{3,2,1,0:T(8,128)(2,1)} %get-tuple-element.53), channel_id=1, source_target_pairs={{0,64},{64,128},{128,192},{192,0},{1,65},{65,129},{129,193},{193,1... | collective-permute-start | bytes 589832 | tf_op jit(solution)/shard_map/ppermute | solution.py:230
  131.3 2.6 %collective-permute-start.18 = (bf16[2,4,16,768]{3,2,1,0:T(8,128)(2,1)}, bf16[2,4,16,768]{3,2,1,0:T(8,128)(2,1)S(1)}, u32[]{:S(2)}, u32[]{:S(2)}) collective-permute-start(bf16[2,4,16,768]{3,2,1,0:T(8,128)(2,1)} %get-tuple-element.47), channel_id=1, source_target_pairs={{0,128},{64,192},{128,0},{192,64},{1,129},{65,193},{129,1},{193,65... | collective-permute-start | bytes 589832 | tf_op jit(solution)/shard_map/ppermute | solution.py:230
  133.8 1.2 collective-permute-start.19
  135.1 2.5 %collective-permute-done.21.refs_9_ = bf16[2,4,16,768]{3,2,1,0:T(8,128)(2,1)S(1)} collective-permute-done((bf16[2,4,16,768]{3,2,1,0:T(8,128)(2,1)S(1)}, bf16[2,4,16,768]{3,2,1,0:T(8,128)(2,1)S(1)}, u32[]{:S(2)}, u32[]{:S(2)}) %collective-permute-start.21) | collective-permute-done | bytes 196640 | tf_op jit(solution)/shard_map/ppermute | solution.py:230
  137.6 1.6 collective-permute-start.20
  139.1 1.2 collective-permute-done.22.refs_10_
  140.3 3.1 %collective-permute-done.23.refs_11_ = bf16[2,4,16,768]{3,2,1,0:T(8,128)(2,1)S(1)} collective-permute-done((bf16[2,4,16,768]{3,2,1,0:T(8,128)(2,1)}, bf16[2,4,16,768]{3,2,1,0:T(8,128)(2,1)S(1)}, u32[]{:S(2)}, u32[]{:S(2)}) %collective-permute-start.23) | collective-permute-done | bytes 196640 | tf_op jit(solution)/shard_map/ppermute | solution.py:230
  143.4 2.6 %collective-permute-done.18.refs_5_ = bf16[2,4,16,768]{3,2,1,0:T(8,128)(2,1)S(1)} collective-permute-done((bf16[2,4,16,768]{3,2,1,0:T(8,128)(2,1)}, bf16[2,4,16,768]{3,2,1,0:T(8,128)(2,1)S(1)}, u32[]{:S(2)}, u32[]{:S(2)}) %collective-permute-start.18) | collective-permute-done | bytes 196640 | tf_op jit(solution)/shard_map/ppermute | solution.py:230
  146.0 1.5 collective-permute-done.19.refs_6_
  147.5 1.1 collective-permute-done.20.refs_7_
  148.6 0.6 shard_map.60
  149.2 0.6 dynamic_slice.3
  150.4 1.5 collective-permute-start.27
  152.4 2.2 %collective-permute-start.25 = (f32[1,4]{1,0:T(1,128)S(1)}, f32[1,4]{1,0:T(1,128)S(1)}, u32[]{:S(2)}, u32[]{:S(2)}) collective-permute-start(f32[1,4]{1,0:T(1,128)S(1)} %add.32), channel_id=1, source_target_pairs={{0,128},{64,192},{128,0},{192,64},{1,129},{65,193},{129,1},{193,65... | collective-permute-start | bytes 56 | tf_op jit(solution)/shard_map/ppermute | solution.py:230
  154.7 0.8 collective-permute-done.26
  155.5 2.0 %collective-permute-done.25 = f32[1,4]{1,0:T(1,128)S(1)} collective-permute-done((f32[1,4]{1,0:T(1,128)S(1)}, f32[1,4]{1,0:T(1,128)S(1)}, u32[]{:S(2)}, u32[]{:S(2)}) %collective-permute-start.25) | collective-permute-done | bytes 48 | tf_op jit(solution)/shard_map/ppermute | solution.py:230
  157.5 0.6 broadcast_in_dim.9
  158.1 8.2 %all-to-all-start.3 = ((f32[32,1,4]{2,1,0:T(1,128)}), f32[32,1,4]{2,1,0:T(1,128)S(1)}, u32[]{:S(2)}, u32[]{:S(2)}) async-start(f32[32,1,4]{2,1,0:T(1,128)} %broadcast_in_dim.9), calls=%async_computation.3 | async-start | bytes 32768 | tf_op jit(solution)/shard_map/all_to_all | solution.py:225
  166.3 0.6 broadcast_multiply_fusion
  166.9 9.2 %all-to-all-done.3 = f32[32,1,4]{2,1,0:T(1,128)S(1)} async-done(((f32[32,1,4]{2,1,0:T(1,128)}), f32[32,1,4]{2,1,0:T(1,128)S(1)}, u32[]{:S(2)}, u32[]{:S(2)}) %all-to-all-start.3) | async-done | bytes 544 | tf_op jit(solution)/shard_map/all_to_all | solution.py:225
  (38 shorter events, 4.1 us)
Async XLA Ops:
  0.6 0.8 copy-start.1
  1.5 6.9 %collective-permute-start = (bf16[24,1024]{1,0:T(8,128)(2,1)S(1)}, bf16[24,1024]{1,0:T(8,128)(2,1)S(1)}, u32[]{:S(2)}, u32[]{:S(2)}) collective-permute-start(bf16[24,1024]{1,0:T(8,128)(2,1)S(1)} %shard_map.49), channel_id=1, source_target_pairs={{0,0},{1,64},{2,128},{3,192},{64,1},{65,65},{66,129},{67,193},{128... | collective-permute-start | bytes 147464 | tf_op jit(solution)/shard_map/ppermute | solution.py:244
  5.0 1.5 copy-start
  55.8 60.8 %all-to-all-start.2 = ((bf16[16,256,128]{2,1,0:T(8,128)(2,1)}), bf16[16,256,128]{2,1,0:T(8,128)(2,1)S(1)}, u32[]{:S(2)}, u32[]{:S(2)}) async-start(bf16[16,256,128]{2,1,0:T(8,128)(2,1)} %get-tuple-element.43), calls=%async_computation.2 | async-start | bytes 2097152 | tf_op jit(solution)/shard_map/all_to_all | solution.py:255
  60.0 39.5 %collective-permute-start.10 = (bf16[192,1024]{1,0:T(8,128)(2,1)S(1)}, bf16[192,1024]{1,0:T(8,128)(2,1)S(1)}, u32[]{:S(2)}, u32[]{:S(2)}) collective-permute-start(bf16[192,1024]{1,0:T(8,128)(2,1)S(1)} %get-tuple-element.36.refs_3_), channel_id=1, source_target_pairs={{0,3},{1,0},{2,1},{3,2},{4,7},{5,4},{6,5},{7,6},{8,11},{9,8},{10,9... | collective-permute-start | bytes 1179656 | tf_op jit(solution)/shard_map/ppermute | solution.py:230
  66.1 33.5 %collective-permute-start.9 = (bf16[192,1024]{1,0:T(8,128)(2,1)S(1)}, bf16[192,1024]{1,0:T(8,128)(2,1)S(1)}, u32[]{:S(2)}, u32[]{:S(2)}) collective-permute-start(bf16[192,1024]{1,0:T(8,128)(2,1)S(1)} %get-tuple-element.36.refs_3_), channel_id=1, source_target_pairs={{0,1},{1,2},{2,3},{3,0},{4,5},{5,6},{6,7},{7,4},{8,9},{9,10},{10,1... | collective-permute-start | bytes 1179656 | tf_op jit(solution)/shard_map/ppermute | solution.py:230
  66.1 34.0 %collective-permute-start.8 = (bf16[192,1024]{1,0:T(8,128)(2,1)S(1)}, bf16[192,1024]{1,0:T(8,128)(2,1)}, u32[]{:S(2)}, u32[]{:S(2)}) collective-permute-start(bf16[192,1024]{1,0:T(8,128)(2,1)S(1)} %get-tuple-element.36.refs_3_), channel_id=1, source_target_pairs={{0,2},{1,3},{2,0},{3,1},{4,6},{5,7},{6,4},{7,5},{8,10},{9,11},{10,... | collective-permute-start | bytes 1179656 | tf_op jit(solution)/shard_map/ppermute | solution.py:230
  67.7 16.5 %collective-permute-start.3 = (f32[8,128]{1,0:T(8,128)S(1)}, f32[8,128]{1,0:T(8,128)S(1)}, u32[]{:S(2)}, u32[]{:S(2)}) collective-permute-start(f32[8,128]{1,0:T(8,128)S(1)} %get-tuple-element.32), channel_id=1, source_target_pairs={{0,3},{1,0},{2,1},{3,2},{4,7},{5,4},{6,5},{7,6},{8,11},{9,8},{10,9... | collective-permute-start | bytes 12296 | tf_op jit(solution)/shard_map/ppermute | solution.py:230
  69.4 18.2 %collective-permute-start.2 = (f32[8,128]{1,0:T(8,128)S(1)}, f32[8,128]{1,0:T(8,128)S(1)}, u32[]{:S(2)}, u32[]{:S(2)}) collective-permute-start(f32[8,128]{1,0:T(8,128)S(1)} %get-tuple-element.32), channel_id=1, source_target_pairs={{0,1},{1,2},{2,3},{3,0},{4,5},{5,6},{6,7},{7,4},{8,9},{9,10},{10,1... | collective-permute-start | bytes 12296 | tf_op jit(solution)/shard_map/ppermute | solution.py:230
  84.1 5.1 %collective-permute-start.1 = (f32[8,128]{1,0:T(8,128)S(1)}, f32[8,128]{1,0:T(8,128)S(1)}, u32[]{:S(2)}, u32[]{:S(2)}) collective-permute-start(f32[8,128]{1,0:T(8,128)S(1)} %get-tuple-element.32), channel_id=1, source_target_pairs={{0,2},{1,3},{2,0},{3,1},{4,6},{5,7},{6,4},{7,5},{8,10},{9,11},{10,... | collective-permute-start | bytes 12296 | tf_op jit(solution)/shard_map/ppermute | solution.py:230
  89.2 1.2 collective-permute-start.4
  90.4 3.7 %collective-permute-start.7 = (f32[16,128]{1,0:T(8,128)S(1)}, f32[16,128]{1,0:T(8,128)S(1)}, u32[]{:S(2)}, u32[]{:S(2)}) collective-permute-start(f32[16,128]{1,0:T(8,128)S(1)} %shard_map.53.mean_0), channel_id=1, source_target_pairs={{0,192},{64,0},{128,64},{192,128},{1,193},{65,1},{129,65},{193,129... | collective-permute-start | bytes 24584 | tf_op jit(solution)/shard_map/ppermute | solution.py:230
  90.9 5.9 %collective-permute-start.6 = (f32[16,128]{1,0:T(8,128)S(1)}, f32[16,128]{1,0:T(8,128)S(1)}, u32[]{:S(2)}, u32[]{:S(2)}) collective-permute-start(f32[16,128]{1,0:T(8,128)S(1)} %shard_map.53.mean_0), channel_id=1, source_target_pairs={{0,64},{64,128},{128,192},{192,0},{1,65},{65,129},{129,193},{193,1... | collective-permute-start | bytes 24584 | tf_op jit(solution)/shard_map/ppermute | solution.py:230
  94.1 5.2 %collective-permute-start.5 = (f32[16,128]{1,0:T(8,128)S(1)}, f32[16,128]{1,0:T(8,128)S(1)}, u32[]{:S(2)}, u32[]{:S(2)}) collective-permute-start(f32[16,128]{1,0:T(8,128)S(1)} %shard_map.53.mean_0), channel_id=1, source_target_pairs={{0,128},{64,192},{128,0},{192,64},{1,129},{65,193},{129,1},{193,65... | collective-permute-start | bytes 24584 | tf_op jit(solution)/shard_map/ppermute | solution.py:230
  96.8 9.9 %collective-permute-start.11 = (bf16[192,1024]{1,0:T(8,128)(2,1)S(1)}, bf16[192,1024]{1,0:T(8,128)(2,1)S(1)}, u32[]{:S(2)}, u32[]{:S(2)}) collective-permute-start(bf16[192,1024]{1,0:T(8,128)(2,1)S(1)} %get-tuple-element.36.refs_3_), channel_id=1, source_target_pairs={{0,4},{4,0},{1,5},{5,1},{2,6},{6,2},{3,7},{7,3},{8,12},{12,8},{9,1... | collective-permute-start | bytes 1179656 | tf_op jit(solution)/shard_map/ppermute | solution.py:230
  99.6 7.1 %collective-permute-start.14 = (bf16[192,1024]{1,0:T(8,128)(2,1)S(1)}, bf16[192,1024]{1,0:T(8,128)(2,1)S(1)}, u32[]{:S(2)}, u32[]{:S(2)}) collective-permute-start(bf16[192,1024]{1,0:T(8,128)(2,1)S(1)} %collective-permute-done.10.refs_6_), channel_id=1, source_target_pairs={{0,4},{4,0},{1,5},{5,1},{2,6},{6,2},{3,7},{7,3},{8,12},{12,8},{9,1... | collective-permute-start | bytes 1179656 | tf_op jit(solution)/shard_map/ppermute | solution.py:230
  99.7 7.0 %collective-permute-start.13 = (bf16[192,1024]{1,0:T(8,128)(2,1)S(1)}, bf16[192,1024]{1,0:T(8,128)(2,1)S(1)}, u32[]{:S(2)}, u32[]{:S(2)}) collective-permute-start(bf16[192,1024]{1,0:T(8,128)(2,1)S(1)} %collective-permute-done.9.refs_5_), channel_id=1, source_target_pairs={{0,4},{4,0},{1,5},{5,1},{2,6},{6,2},{3,7},{7,3},{8,12},{12,8},{9,1... | collective-permute-start | bytes 1179656 | tf_op jit(solution)/shard_map/ppermute | solution.py:230
  100.2 6.6 %collective-permute-start.12 = (bf16[192,1024]{1,0:T(8,128)(2,1)}, bf16[192,1024]{1,0:T(8,128)(2,1)S(1)}, u32[]{:S(2)}, u32[]{:S(2)}) collective-permute-start(bf16[192,1024]{1,0:T(8,128)(2,1)} %collective-permute-done.8.refs_4_), channel_id=1, source_target_pairs={{0,4},{4,0},{1,5},{5,1},{2,6},{6,2},{3,7},{7,3},{8,12},{12,8},{9,1... | collective-permute-start | bytes 1179656 | tf_op jit(solution)/shard_map/ppermute | solution.py:230
  111.7 19.6 %collective-permute-start.15 = (bf16[3,4,16,768]{3,2,1,0:T(8,128)(2,1)}, bf16[3,4,16,768]{3,2,1,0:T(8,128)(2,1)S(1)}, u32[]{:S(2)}, u32[]{:S(2)}) collective-permute-start(bf16[3,4,16,768]{3,2,1,0:T(8,128)(2,1)} %get-tuple-element.39), channel_id=1, source_target_pairs={{0,128},{64,192},{128,0},{192,64},{1,129},{65,193},{129,1},{193,65... | collective-permute-start | bytes 884744 | tf_op jit(solution)/shard_map/ppermute | solution.py:230
  114.5 16.8 %collective-permute-start.16 = (bf16[3,4,16,768]{3,2,1,0:T(8,128)(2,1)}, bf16[3,4,16,768]{3,2,1,0:T(8,128)(2,1)S(1)}, u32[]{:S(2)}, u32[]{:S(2)}) collective-permute-start(bf16[3,4,16,768]{3,2,1,0:T(8,128)(2,1)} %get-tuple-element.40), channel_id=1, source_target_pairs={{0,64},{64,128},{128,192},{192,0},{1,65},{65,129},{129,193},{193,1... | collective-permute-start | bytes 884744 | tf_op jit(solution)/shard_map/ppermute | solution.py:230
  114.5 19.3 %collective-permute-start.17 = (bf16[3,4,16,768]{3,2,1,0:T(8,128)(2,1)}, bf16[3,4,16,768]{3,2,1,0:T(8,128)(2,1)S(1)}, u32[]{:S(2)}, u32[]{:S(2)}) collective-permute-start(bf16[3,4,16,768]{3,2,1,0:T(8,128)(2,1)} %get-tuple-element.41), channel_id=1, source_target_pairs={{0,192},{64,0},{128,64},{192,128},{1,193},{65,1},{129,65},{193,129... | collective-permute-start | bytes 884744 | tf_op jit(solution)/shard_map/ppermute | solution.py:230
  128.2 9.4 %collective-permute-start.21 = (bf16[2,4,16,768]{3,2,1,0:T(8,128)(2,1)S(1)}, bf16[2,4,16,768]{3,2,1,0:T(8,128)(2,1)S(1)}, u32[]{:S(2)}, u32[]{:S(2)}) collective-permute-start(bf16[2,4,16,768]{3,2,1,0:T(8,128)(2,1)S(1)} %get-tuple-element.52), channel_id=1, source_target_pairs={{0,128},{64,192},{128,0},{192,64},{1,129},{65,193},{129,1},{193,65... | collective-permute-start | bytes 589832 | tf_op jit(solution)/shard_map/ppermute | solution.py:230
  129.1 11.3 %collective-permute-start.22 = (bf16[2,4,16,768]{3,2,1,0:T(8,128)(2,1)}, bf16[2,4,16,768]{3,2,1,0:T(8,128)(2,1)S(1)}, u32[]{:S(2)}, u32[]{:S(2)}) collective-permute-start(bf16[2,4,16,768]{3,2,1,0:T(8,128)(2,1)} %get-tuple-element.53), channel_id=1, source_target_pairs={{0,64},{64,128},{128,192},{192,0},{1,65},{65,129},{129,193},{193,1... | collective-permute-start | bytes 589832 | tf_op jit(solution)/shard_map/ppermute | solution.py:230
  131.3 12.2 %collective-permute-start.23 = (bf16[2,4,16,768]{3,2,1,0:T(8,128)(2,1)}, bf16[2,4,16,768]{3,2,1,0:T(8,128)(2,1)S(1)}, u32[]{:S(2)}, u32[]{:S(2)}) collective-permute-start(bf16[2,4,16,768]{3,2,1,0:T(8,128)(2,1)} %get-tuple-element.54), channel_id=1, source_target_pairs={{0,192},{64,0},{128,64},{192,128},{1,193},{65,1},{129,65},{193,129... | collective-permute-start | bytes 589832 | tf_op jit(solution)/shard_map/ppermute | solution.py:230
  131.3 14.8 %collective-permute-start.18 = (bf16[2,4,16,768]{3,2,1,0:T(8,128)(2,1)}, bf16[2,4,16,768]{3,2,1,0:T(8,128)(2,1)S(1)}, u32[]{:S(2)}, u32[]{:S(2)}) collective-permute-start(bf16[2,4,16,768]{3,2,1,0:T(8,128)(2,1)} %get-tuple-element.47), channel_id=1, source_target_pairs={{0,128},{64,192},{128,0},{192,64},{1,129},{65,193},{129,1},{193,65... | collective-permute-start | bytes 589832 | tf_op jit(solution)/shard_map/ppermute | solution.py:230
  133.8 13.7 %collective-permute-start.19 = (bf16[2,4,16,768]{3,2,1,0:T(8,128)(2,1)S(1)}, bf16[2,4,16,768]{3,2,1,0:T(8,128)(2,1)S(1)}, u32[]{:S(2)}, u32[]{:S(2)}) collective-permute-start(bf16[2,4,16,768]{3,2,1,0:T(8,128)(2,1)S(1)} %get-tuple-element.48), channel_id=1, source_target_pairs={{0,64},{64,128},{128,192},{192,0},{1,65},{65,129},{129,193},{193,1... | collective-permute-start | bytes 589832 | tf_op jit(solution)/shard_map/ppermute | solution.py:230
  137.6 11.1 %collective-permute-start.20 = (bf16[2,4,16,768]{3,2,1,0:T(8,128)(2,1)S(1)}, bf16[2,4,16,768]{3,2,1,0:T(8,128)(2,1)S(1)}, u32[]{:S(2)}, u32[]{:S(2)}) collective-permute-start(bf16[2,4,16,768]{3,2,1,0:T(8,128)(2,1)S(1)} %get-tuple-element.49), channel_id=1, source_target_pairs={{0,192},{64,0},{128,64},{192,128},{1,193},{65,1},{129,65},{193,129... | collective-permute-start | bytes 589832 | tf_op jit(solution)/shard_map/ppermute | solution.py:230
  149.2 1.2 collective-permute-start.24
  150.4 4.2 %collective-permute-start.27 = (f32[1,4]{1,0:T(1,128)S(1)}, f32[1,4]{1,0:T(1,128)S(1)}, u32[]{:S(2)}, u32[]{:S(2)}) collective-permute-start(f32[1,4]{1,0:T(1,128)S(1)} %add.32), channel_id=1, source_target_pairs={{0,192},{64,0},{128,64},{192,128},{1,193},{65,1},{129,65},{193,129... | collective-permute-start | bytes 56 | tf_op jit(solution)/shard_map/ppermute | solution.py:230
  151.9 3.6 %collective-permute-start.26 = (f32[1,4]{1,0:T(1,128)S(1)}, f32[1,4]{1,0:T(1,128)S(1)}, u32[]{:S(2)}, u32[]{:S(2)}) collective-permute-start(f32[1,4]{1,0:T(1,128)S(1)} %add.32), channel_id=1, source_target_pairs={{0,64},{64,128},{128,192},{192,0},{1,65},{65,129},{129,193},{193,1... | collective-permute-start | bytes 56 | tf_op jit(solution)/shard_map/ppermute | solution.py:230
  152.4 5.1 %collective-permute-start.25 = (f32[1,4]{1,0:T(1,128)S(1)}, f32[1,4]{1,0:T(1,128)S(1)}, u32[]{:S(2)}, u32[]{:S(2)}) collective-permute-start(f32[1,4]{1,0:T(1,128)S(1)} %add.32), channel_id=1, source_target_pairs={{0,128},{64,192},{128,0},{192,64},{1,129},{65,193},{129,1},{193,65... | collective-permute-start | bytes 56 | tf_op jit(solution)/shard_map/ppermute | solution.py:230
  158.1 18.0 %all-to-all-start.3 = ((f32[32,1,4]{2,1,0:T(1,128)}), f32[32,1,4]{2,1,0:T(1,128)S(1)}, u32[]{:S(2)}, u32[]{:S(2)}) async-start(f32[32,1,4]{2,1,0:T(1,128)} %broadcast_in_dim.9), calls=%async_computation.3 | async-start | bytes 32768 | tf_op jit(solution)/shard_map/all_to_all | solution.py:225

commit v10 on v8

--- a/solution.py
+++ b/solution.py
@@ -143,8 +143,9 @@
 
 def multiply(delta, tokens, out_refs, unit):
     out = lax.dot_general(
-        delta[...], tokens[...], (((1,), (1,)), ((), ())), preferred_element_type=jnp.float32
-    ).astype(jnp.bfloat16)
+        tokens[...], delta[...], (((1,), (1,)), ((), ())), preferred_element_type=jnp.float32
+    )
+    out = out.T.astype(jnp.bfloat16)
     for k in range(GRID):
         for hops in range(NX):
             at = k * UNIT + hops * ROWS

time: 183 us -> 183 us (level)
  no operation moved by 1% of the time
where the time goes in v10:
time: 183 us; the launch traced here: 181 us
  blocking collectives  53.5 us (29%)
  waiting for transfers between devices  50.9 us (28%)
  starting transfers between devices  45 us (25%)
  Pallas kernels  25.7 us (14%)
  local copies, waits for them, and re-layouts  3.65 us (2%)
    ppermute x20, waiting for transfers between devices, shifted(): lax.ppermute(value, axis, [(i, (i + hops) % size) for i in range(size)])  39.2 us
    all_to_all x1, blocking collectives, search(): received = [lax.all_to_all(merged, ZC, 0, 0, tiled=True)]  28.3 us
    ppermute x20, starting transfers between devices, shifted(): lax.ppermute(value, axis, [(i, (i + hops) % size) for i in range(size)])  25.8 us
    all_to_all x1, blocking collectives, search(): received.append(lax.all_to_all(part, ZC, 0, 0, tiled=True))  25.2 us
    all_to_all x1, starting transfers between devices, spread(): return lax.all_to_all(wide, axes, 0, 0, tiled=True)  12.2 us
    all_to_all x1, waiting for transfers between devices, spread(): return lax.all_to_all(wide, axes, 0, 0, tiled=True)  11.1 us
    pallas_call x1, Pallas kernels, search(): kernel(piece_kernel(first, units), out_shape, flops=3 * work, in_specs=[l...  9.01 us
    pallas_call x2, Pallas kernels, search(): deltas.append(step(received[send], scale, inverse))  8.32 us
  transfers between devices with their start and end apart: 23, of which 13 were waited for; matrix products, arithmetic and copies ran while one was open for 1% of the time, Pallas kernels for 14%

profile of v10, /device:TPU:2, one launch (start us, length us, event | category | flops | bytes accessed | tf_op | source)
XLA Modules:
  0.0 180.9 jit_solution(15480009241600272333)
XLA Ops:
  0.6 0.8 copy-done.1
  1.5 3.5 %collective-permute-start = (bf16[24,1024]{1,0:T(8,128)(2,1)S(1)}, bf16[24,1024]{1,0:T(8,128)(2,1)S(1)}, u32[]{:S(2)}, u32[]{:S(2)}) collective-permute-start(bf16[24,1024]{1,0:T(8,128)(2,1)S(1)} %shard_map.49), channel_id=1, source_target_pairs={{0,0},{1,64},{2,128},{3,192},{64,1},{65,65},{66,129},{67,193},{128... | collective-permute-start | bytes 147464 | tf_op jit(solution)/shard_map/ppermute | solution.py:245
  5.0 1.5 copy-done
  6.5 1.4 shard_map.50
  7.9 0.5 collective-permute-done.tokens_ref
  8.4 0.1 shard_map.51
  8.5 28.3 %all_to_all.20.parts_ref.columns_ref = bf16[16,160,128]{2,1,0:T(8,128)(2,1)S(1)} all-to-all(bf16[16,160,128]{2,1,0:T(8,128)(2,1)S(1)} %shard_map.51), channel_id=1, replica_groups=mesh['dp_0'=4,'dp_1'=8,'dp_2'=2,'tensor'=4] {'dp_1','dp_2'}, dimensions={0} | all-to-all | bytes 1310720 | tf_op jit(solution)/shard_map/all_to_all | solution.py:251
  36.8 0.2 shard_map.52
  37.0 25.2 %all_to_all.21.columns_ref = bf16[16,192,128]{2,1,0:T(8,128)(2,1)S(1)} all-to-all(bf16[16,192,128]{2,1,0:T(8,128)(2,1)S(1)} %get-tuple-element.31), channel_id=1, replica_groups=mesh['dp_0'=4,'dp_1'=8,'dp_2'=2,'tensor'=4] {'dp_1','dp_2'}, dimensions={0} | all-to-all | bytes 1572864 | tf_op jit(solution)/shard_map/all_to_all | solution.py:256
  62.2 3.6 %all-to-all-start.2 = ((bf16[16,192,128]{2,1,0:T(8,128)(2,1)}), bf16[16,192,128]{2,1,0:T(8,128)(2,1)S(1)}, u32[]{:S(2)}, u32[]{:S(2)}) async-start(bf16[16,192,128]{2,1,0:T(8,128)(2,1)} %get-tuple-element.37), calls=%async_computation.2 | async-start | bytes 1572864 | tf_op jit(solution)/shard_map/all_to_all | solution.py:256
  65.8 6.1 %collective-permute-start.10 = (bf16[192,1024]{1,0:T(8,128)(2,1)S(1)}, bf16[192,1024]{1,0:T(8,128)(2,1)S(1)}, u32[]{:S(2)}, u32[]{:S(2)}) collective-permute-start(bf16[192,1024]{1,0:T(8,128)(2,1)S(1)} %get-tuple-element.30.refs_3_), channel_id=1, source_target_pairs={{0,3},{1,0},{2,1},{3,2},{4,7},{5,4},{6,5},{7,6},{8,11},{9,8},{10,9... | collective-permute-start | bytes 1179656 | tf_op jit(solution)/shard_map/ppermute | solution.py:231
  71.9 1.6 collective-permute-start.8
  73.4 1.7 collective-permute-start.3
  75.1 0.9 collective-permute-start.2
  76.0 13.7 %collective-permute-done.3 = f32[8,128]{1,0:T(8,128)S(1)} collective-permute-done((f32[8,128]{1,0:T(8,128)S(1)}, f32[8,128]{1,0:T(8,128)S(1)}, u32[]{:S(2)}, u32[]{:S(2)}) %collective-permute-start.3) | collective-permute-done | bytes 4128 | tf_op jit(solution)/shard_map/ppermute | solution.py:231
  89.7 2.0 %collective-permute-start.1 = (f32[8,128]{1,0:T(8,128)S(1)}, f32[8,128]{1,0:T(8,128)S(1)}, u32[]{:S(2)}, u32[]{:S(2)}) collective-permute-start(f32[8,128]{1,0:T(8,128)S(1)} %get-tuple-element.26), channel_id=1, source_target_pairs={{0,2},{1,3},{2,0},{3,1},{4,6},{5,7},{6,4},{7,5},{8,10},{9,11},{10,... | collective-permute-start | bytes 12296 | tf_op jit(solution)/shard_map/ppermute | solution.py:231
  91.7 1.4 collective-permute-done.2
  93.1 1.7 collective-permute-done.1
  94.9 1.2 collective-permute-done.4.other_ref
  96.0 0.5 collective-permute-start.7
  96.5 1.6 collective-permute-start.6
  98.0 1.6 collective-permute-done.7.mean_3
  99.7 2.7 %collective-permute-start.5 = (f32[16,128]{1,0:T(8,128)S(1)}, f32[16,128]{1,0:T(8,128)S(1)}, u32[]{:S(2)}, u32[]{:S(2)}) collective-permute-start(f32[16,128]{1,0:T(8,128)S(1)} %shard_map.53.mean_0), channel_id=1, source_target_pairs={{0,128},{64,192},{128,0},{192,64},{1,129},{65,193},{129,1},{193,65... | collective-permute-start | bytes 24584 | tf_op jit(solution)/shard_map/ppermute | solution.py:231
  102.4 2.4 %collective-permute-done.5.mean_1 = f32[16,128]{1,0:T(8,128)S(1)} collective-permute-done((f32[16,128]{1,0:T(8,128)S(1)}, f32[16,128]{1,0:T(8,128)S(1)}, u32[]{:S(2)}, u32[]{:S(2)}) %collective-permute-start.5) | collective-permute-done | bytes 8224 | tf_op jit(solution)/shard_map/ppermute | solution.py:231
  104.8 0.3 shard_map.54
  105.3 0.5 collective-permute-start.13
  105.8 0.3 collective-permute-start.12
  106.0 2.1 %shard_map.55.refs_1_ = bf16[1,256,2048]{2,1,0:T(8,128)(2,1)S(1)} custom-call(bf16[16,160,128]{2,1,0:T(8,128)(2,1)S(1)} %all_to_all.20.parts_ref.columns_ref, f32[4,16,128]{2,1,0:T(8,128)S(1)} %get-tuple-element.27.scale_ref, f32[4,16,128]{2,1,0:T(8,128)S(1)} %get-tuple-element.28.inverse_ref), custom_call_target="tpu_custom_call" | custom-call | flops 3221225472 | tf_op jit(solution)/shard_map/pallas_call | solution.py:280
  108.1 6.2 %shard_map.56.refs_2_ = bf16[3,256,2048]{2,1,0:T(8,128)(2,1)S(1)} custom-call(bf16[16,192,128]{2,1,0:T(8,128)(2,1)S(1)} %all_to_all.21.columns_ref, f32[4,16,128]{2,1,0:T(8,128)S(1)} %get-tuple-element.27.scale_ref, f32[4,16,128]{2,1,0:T(8,128)S(1)} %get-tuple-element.28.inverse_ref), custom_call_target="tpu_custom_call" | custom-call | flops 3221225472 | tf_op jit(solution)/shard_map/pallas_call | solution.py:280
  114.4 5.7 %shard_map.57 = (bf16[4,4,16,768]{3,2,1,0:T(8,128)(2,1)S(1)}, bf16[4,4,16,768]{3,2,1,0:T(8,128)(2,1)}, bf16[4,4,16,768]{3,2,1,0:T(8,128)(2,1)}, bf16[4,4,16,768]{3,2,1,0:T(8,128)(2,1)}, bf16[768,2048]{1,0:T(8,128)(2,1)}) custom-call(s32[1]{0:T(128)} %bitcast.core_ref.refs_0_, bf16[1,256,2048]{2,1,0:T(8,128)(2,1)S(1)} %shard_map.55.refs_1_, ...), custom_call_target="tpu_custom_call" | custom-call | flops 1610612736 | tf_op jit(solution)/shard_map/pallas_call | solution.py:281
  120.2 2.8 %collective-permute-start.15 = (bf16[4,4,16,768]{3,2,1,0:T(8,128)(2,1)}, bf16[4,4,16,768]{3,2,1,0:T(8,128)(2,1)S(1)}, u32[]{:S(2)}, u32[]{:S(2)}) collective-permute-start(bf16[4,4,16,768]{3,2,1,0:T(8,128)(2,1)} %get-tuple-element.33), channel_id=1, source_target_pairs={{0,128},{64,192},{128,0},{192,64},{1,129},{65,193},{129,1},{193,65... | collective-permute-start | bytes 1179656 | tf_op jit(solution)/shard_map/ppermute | solution.py:231
  123.0 2.0 %collective-permute-start.17 = (bf16[4,4,16,768]{3,2,1,0:T(8,128)(2,1)}, bf16[4,4,16,768]{3,2,1,0:T(8,128)(2,1)S(1)}, u32[]{:S(2)}, u32[]{:S(2)}) collective-permute-start(bf16[4,4,16,768]{3,2,1,0:T(8,128)(2,1)} %get-tuple-element.35), channel_id=1, source_target_pairs={{0,192},{64,0},{128,64},{192,128},{1,193},{65,1},{129,65},{193,129... | collective-permute-start | bytes 1179656 | tf_op jit(solution)/shard_map/ppermute | solution.py:231
  125.0 9.0 %shard_map.58 = (bf16[3,4,16,768]{3,2,1,0:T(8,128)(2,1)S(1)}, bf16[3,4,16,768]{3,2,1,0:T(8,128)(2,1)}, bf16[3,4,16,768]{3,2,1,0:T(8,128)(2,1)}, bf16[3,4,16,768]{3,2,1,0:T(8,128)(2,1)S(1)}) custom-call(bf16[16,192,128]{2,1,0:T(8,128)(2,1)S(1)} %all-to-all-done.2.columns_ref, f32[4,16,128]{2,1,0:T(8,128)S(1)} %get-tuple-element.27.scale_ref, ...), custom_call_target="tpu_custom_call" | custom-call | flops 3623878656 | tf_op jit(solution)/shard_map/pallas_call | solution.py:288
  134.0 0.9 collective-permute-start.18
  134.9 2.2 %collective-permute-start.19 = (bf16[3,4,16,768]{3,2,1,0:T(8,128)(2,1)}, bf16[3,4,16,768]{3,2,1,0:T(8,128)(2,1)S(1)}, u32[]{:S(2)}, u32[]{:S(2)}) collective-permute-start(bf16[3,4,16,768]{3,2,1,0:T(8,128)(2,1)} %get-tuple-element.42), channel_id=1, source_target_pairs={{0,64},{64,128},{128,192},{192,0},{1,65},{65,129},{129,193},{193,1... | collective-permute-start | bytes 884744 | tf_op jit(solution)/shard_map/ppermute | solution.py:231
  137.1 4.8 %collective-permute-done.16.refs_2_ = bf16[4,4,16,768]{3,2,1,0:T(8,128)(2,1)S(1)} collective-permute-done((bf16[4,4,16,768]{3,2,1,0:T(8,128)(2,1)}, bf16[4,4,16,768]{3,2,1,0:T(8,128)(2,1)S(1)}, u32[]{:S(2)}, u32[]{:S(2)}) %collective-permute-start.16) | collective-permute-done | bytes 393248 | tf_op jit(solution)/shard_map/ppermute | solution.py:231
  141.9 0.5 collective-permute-done.17.refs_3_
  142.5 6.3 %collective-permute-done.18.refs_5_ = bf16[3,4,16,768]{3,2,1,0:T(8,128)(2,1)S(1)} collective-permute-done((bf16[3,4,16,768]{3,2,1,0:T(8,128)(2,1)}, bf16[3,4,16,768]{3,2,1,0:T(8,128)(2,1)S(1)}, u32[]{:S(2)}, u32[]{:S(2)}) %collective-permute-start.18) | collective-permute-done | bytes 294944 | tf_op jit(solution)/shard_map/ppermute | solution.py:231
  148.8 5.1 %collective-permute-done.19.refs_6_ = bf16[3,4,16,768]{3,2,1,0:T(8,128)(2,1)S(1)} collective-permute-done((bf16[3,4,16,768]{3,2,1,0:T(8,128)(2,1)}, bf16[3,4,16,768]{3,2,1,0:T(8,128)(2,1)S(1)}, u32[]{:S(2)}, u32[]{:S(2)}) %collective-permute-start.19) | collective-permute-done | bytes 294944 | tf_op jit(solution)/shard_map/ppermute | solution.py:231
  153.9 0.4 collective-permute-done.20.refs_7_
  154.3 0.6 shard_map.59
  154.9 0.7 broadcast_in_dim.9
  155.6 12.2 %all-to-all-start.3 = ((f32[256,1,4]{2,1,0:T(1,128)}), f32[256,1,4]{2,1,0:T(1,128)S(1)}, u32[]{:S(2)}, u32[]{:S(2)}) async-start(f32[256,1,4]{2,1,0:T(1,128)} %broadcast_in_dim.9), calls=%async_computation.3 | async-start | bytes 262144 | tf_op jit(solution)/shard_map/all_to_all | solution.py:226
  167.8 0.6 broadcast_multiply_fusion
  168.4 0.6 dynamic_slice.3
  169.0 11.1 %all-to-all-done.3 = f32[256,1,4]{2,1,0:T(1,128)S(1)} async-done(((f32[256,1,4]{2,1,0:T(1,128)}), f32[256,1,4]{2,1,0:T(1,128)S(1)}, u32[]{:S(2)}, u32[]{:S(2)}) %all-to-all-start.3) | async-done | bytes 4128 | tf_op jit(solution)/shard_map/all_to_all | solution.py:226
  180.1 0.3 reduce_sum.9
  180.4 0.5 broadcast_multiply_fusion.1
  (21 shorter events, 0.2 us)
Async XLA Ops:
  0.6 0.8 copy-start.1
  1.5 6.9 %collective-permute-start = (bf16[24,1024]{1,0:T(8,128)(2,1)S(1)}, bf16[24,1024]{1,0:T(8,128)(2,1)S(1)}, u32[]{:S(2)}, u32[]{:S(2)}) collective-permute-start(bf16[24,1024]{1,0:T(8,128)(2,1)S(1)} %shard_map.49), channel_id=1, source_target_pairs={{0,0},{1,64},{2,128},{3,192},{64,1},{65,65},{66,129},{67,193},{128... | collective-permute-start | bytes 147464 | tf_op jit(solution)/shard_map/ppermute | solution.py:245
  5.0 1.5 copy-start
  62.2 62.9 %all-to-all-start.2 = ((bf16[16,192,128]{2,1,0:T(8,128)(2,1)}), bf16[16,192,128]{2,1,0:T(8,128)(2,1)S(1)}, u32[]{:S(2)}, u32[]{:S(2)}) async-start(bf16[16,192,128]{2,1,0:T(8,128)(2,1)} %get-tuple-element.37), calls=%async_computation.2 | async-start | bytes 1572864 | tf_op jit(solution)/shard_map/all_to_all | solution.py:256
  65.8 39.4 %collective-permute-start.10 = (bf16[192,1024]{1,0:T(8,128)(2,1)S(1)}, bf16[192,1024]{1,0:T(8,128)(2,1)S(1)}, u32[]{:S(2)}, u32[]{:S(2)}) collective-permute-start(bf16[192,1024]{1,0:T(8,128)(2,1)S(1)} %get-tuple-element.30.refs_3_), channel_id=1, source_target_pairs={{0,3},{1,0},{2,1},{3,2},{4,7},{5,4},{6,5},{7,6},{8,11},{9,8},{10,9... | collective-permute-start | bytes 1179656 | tf_op jit(solution)/shard_map/ppermute | solution.py:231
  71.9 33.4 %collective-permute-start.9 = (bf16[192,1024]{1,0:T(8,128)(2,1)S(1)}, bf16[192,1024]{1,0:T(8,128)(2,1)S(1)}, u32[]{:S(2)}, u32[]{:S(2)}) collective-permute-start(bf16[192,1024]{1,0:T(8,128)(2,1)S(1)} %get-tuple-element.30.refs_3_), channel_id=1, source_target_pairs={{0,1},{1,2},{2,3},{3,0},{4,5},{5,6},{6,7},{7,4},{8,9},{9,10},{10,1... | collective-permute-start | bytes 1179656 | tf_op jit(solution)/shard_map/ppermute | solution.py:231
  71.9 33.9 %collective-permute-start.8 = (bf16[192,1024]{1,0:T(8,128)(2,1)S(1)}, bf16[192,1024]{1,0:T(8,128)(2,1)}, u32[]{:S(2)}, u32[]{:S(2)}) collective-permute-start(bf16[192,1024]{1,0:T(8,128)(2,1)S(1)} %get-tuple-element.30.refs_3_), channel_id=1, source_target_pairs={{0,2},{1,3},{2,0},{3,1},{4,6},{5,7},{6,4},{7,5},{8,10},{9,11},{10,... | collective-permute-start | bytes 1179656 | tf_op jit(solution)/shard_map/ppermute | solution.py:231
  73.4 16.3 %collective-permute-start.3 = (f32[8,128]{1,0:T(8,128)S(1)}, f32[8,128]{1,0:T(8,128)S(1)}, u32[]{:S(2)}, u32[]{:S(2)}) collective-permute-start(f32[8,128]{1,0:T(8,128)S(1)} %get-tuple-element.26), channel_id=1, source_target_pairs={{0,3},{1,0},{2,1},{3,2},{4,7},{5,4},{6,5},{7,6},{8,11},{9,8},{10,9... | collective-permute-start | bytes 12296 | tf_op jit(solution)/shard_map/ppermute | solution.py:231
  75.1 18.0 %collective-permute-start.2 = (f32[8,128]{1,0:T(8,128)S(1)}, f32[8,128]{1,0:T(8,128)S(1)}, u32[]{:S(2)}, u32[]{:S(2)}) collective-permute-start(f32[8,128]{1,0:T(8,128)S(1)} %get-tuple-element.26), channel_id=1, source_target_pairs={{0,1},{1,2},{2,3},{3,0},{4,5},{5,6},{6,7},{7,4},{8,9},{9,10},{10,1... | collective-permute-start | bytes 12296 | tf_op jit(solution)/shard_map/ppermute | solution.py:231
  89.7 5.1 %collective-permute-start.1 = (f32[8,128]{1,0:T(8,128)S(1)}, f32[8,128]{1,0:T(8,128)S(1)}, u32[]{:S(2)}, u32[]{:S(2)}) collective-permute-start(f32[8,128]{1,0:T(8,128)S(1)} %get-tuple-element.26), channel_id=1, source_target_pairs={{0,2},{1,3},{2,0},{3,1},{4,6},{5,7},{6,4},{7,5},{8,10},{9,11},{10,... | collective-permute-start | bytes 12296 | tf_op jit(solution)/shard_map/ppermute | solution.py:231
  94.8 1.2 collective-permute-start.4
  96.0 3.7 %collective-permute-start.7 = (f32[16,128]{1,0:T(8,128)S(1)}, f32[16,128]{1,0:T(8,128)S(1)}, u32[]{:S(2)}, u32[]{:S(2)}) collective-permute-start(f32[16,128]{1,0:T(8,128)S(1)} %shard_map.53.mean_0), channel_id=1, source_target_pairs={{0,192},{64,0},{128,64},{192,128},{1,193},{65,1},{129,65},{193,129... | collective-permute-start | bytes 24584 | tf_op jit(solution)/shard_map/ppermute | solution.py:231
  96.5 5.9 %collective-permute-start.6 = (f32[16,128]{1,0:T(8,128)S(1)}, f32[16,128]{1,0:T(8,128)S(1)}, u32[]{:S(2)}, u32[]{:S(2)}) collective-permute-start(f32[16,128]{1,0:T(8,128)S(1)} %shard_map.53.mean_0), channel_id=1, source_target_pairs={{0,64},{64,128},{128,192},{192,0},{1,65},{65,129},{129,193},{193,1... | collective-permute-start | bytes 24584 | tf_op jit(solution)/shard_map/ppermute | solution.py:231
  99.7 5.2 %collective-permute-start.5 = (f32[16,128]{1,0:T(8,128)S(1)}, f32[16,128]{1,0:T(8,128)S(1)}, u32[]{:S(2)}, u32[]{:S(2)}) collective-permute-start(f32[16,128]{1,0:T(8,128)S(1)} %shard_map.53.mean_0), channel_id=1, source_target_pairs={{0,128},{64,192},{128,0},{192,64},{1,129},{65,193},{129,1},{193,65... | collective-permute-start | bytes 24584 | tf_op jit(solution)/shard_map/ppermute | solution.py:231
  102.4 12.0 %collective-permute-start.11 = (bf16[192,1024]{1,0:T(8,128)(2,1)S(1)}, bf16[192,1024]{1,0:T(8,128)(2,1)S(1)}, u32[]{:S(2)}, u32[]{:S(2)}) collective-permute-start(bf16[192,1024]{1,0:T(8,128)(2,1)S(1)} %get-tuple-element.30.refs_3_), channel_id=1, source_target_pairs={{0,4},{4,0},{1,5},{5,1},{2,6},{6,2},{3,7},{7,3},{8,12},{12,8},{9,1... | collective-permute-start | bytes 1179656 | tf_op jit(solution)/shard_map/ppermute | solution.py:231
  105.2 9.2 %collective-permute-start.14 = (bf16[192,1024]{1,0:T(8,128)(2,1)S(1)}, bf16[192,1024]{1,0:T(8,128)(2,1)S(1)}, u32[]{:S(2)}, u32[]{:S(2)}) collective-permute-start(bf16[192,1024]{1,0:T(8,128)(2,1)S(1)} %collective-permute-done.10.refs_6_), channel_id=1, source_target_pairs={{0,4},{4,0},{1,5},{5,1},{2,6},{6,2},{3,7},{7,3},{8,12},{12,8},{9,1... | collective-permute-start | bytes 1179656 | tf_op jit(solution)/shard_map/ppermute | solution.py:231
  105.3 9.1 %collective-permute-start.13 = (bf16[192,1024]{1,0:T(8,128)(2,1)S(1)}, bf16[192,1024]{1,0:T(8,128)(2,1)S(1)}, u32[]{:S(2)}, u32[]{:S(2)}) collective-permute-start(bf16[192,1024]{1,0:T(8,128)(2,1)S(1)} %collective-permute-done.9.refs_5_), channel_id=1, source_target_pairs={{0,4},{4,0},{1,5},{5,1},{2,6},{6,2},{3,7},{7,3},{8,12},{12,8},{9,1... | collective-permute-start | bytes 1179656 | tf_op jit(solution)/shard_map/ppermute | solution.py:231
  105.8 8.6 %collective-permute-start.12 = (bf16[192,1024]{1,0:T(8,128)(2,1)}, bf16[192,1024]{1,0:T(8,128)(2,1)S(1)}, u32[]{:S(2)}, u32[]{:S(2)}) collective-permute-start(bf16[192,1024]{1,0:T(8,128)(2,1)} %collective-permute-done.8.refs_4_), channel_id=1, source_target_pairs={{0,4},{4,0},{1,5},{5,1},{2,6},{6,2},{3,7},{7,3},{8,12},{12,8},{9,1... | collective-permute-start | bytes 1179656 | tf_op jit(solution)/shard_map/ppermute | solution.py:231
  120.2 16.9 %collective-permute-start.15 = (bf16[4,4,16,768]{3,2,1,0:T(8,128)(2,1)}, bf16[4,4,16,768]{3,2,1,0:T(8,128)(2,1)S(1)}, u32[]{:S(2)}, u32[]{:S(2)}) collective-permute-start(bf16[4,4,16,768]{3,2,1,0:T(8,128)(2,1)} %get-tuple-element.33), channel_id=1, source_target_pairs={{0,128},{64,192},{128,0},{192,64},{1,129},{65,193},{129,1},{193,65... | collective-permute-start | bytes 1179656 | tf_op jit(solution)/shard_map/ppermute | solution.py:231
  123.0 18.9 %collective-permute-start.16 = (bf16[4,4,16,768]{3,2,1,0:T(8,128)(2,1)}, bf16[4,4,16,768]{3,2,1,0:T(8,128)(2,1)S(1)}, u32[]{:S(2)}, u32[]{:S(2)}) collective-permute-start(bf16[4,4,16,768]{3,2,1,0:T(8,128)(2,1)} %get-tuple-element.34), channel_id=1, source_target_pairs={{0,64},{64,128},{128,192},{192,0},{1,65},{65,129},{129,193},{193,1... | collective-permute-start | bytes 1179656 | tf_op jit(solution)/shard_map/ppermute | solution.py:231
  123.0 19.5 %collective-permute-start.17 = (bf16[4,4,16,768]{3,2,1,0:T(8,128)(2,1)}, bf16[4,4,16,768]{3,2,1,0:T(8,128)(2,1)S(1)}, u32[]{:S(2)}, u32[]{:S(2)}) collective-permute-start(bf16[4,4,16,768]{3,2,1,0:T(8,128)(2,1)} %get-tuple-element.35), channel_id=1, source_target_pairs={{0,192},{64,0},{128,64},{192,128},{1,193},{65,1},{129,65},{193,129... | collective-permute-start | bytes 1179656 | tf_op jit(solution)/shard_map/ppermute | solution.py:231
  134.0 14.7 %collective-permute-start.18 = (bf16[3,4,16,768]{3,2,1,0:T(8,128)(2,1)}, bf16[3,4,16,768]{3,2,1,0:T(8,128)(2,1)S(1)}, u32[]{:S(2)}, u32[]{:S(2)}) collective-permute-start(bf16[3,4,16,768]{3,2,1,0:T(8,128)(2,1)} %get-tuple-element.41), channel_id=1, source_target_pairs={{0,128},{64,192},{128,0},{192,64},{1,129},{65,193},{129,1},{193,65... | collective-permute-start | bytes 884744 | tf_op jit(solution)/shard_map/ppermute | solution.py:231
  134.9 19.0 %collective-permute-start.19 = (bf16[3,4,16,768]{3,2,1,0:T(8,128)(2,1)}, bf16[3,4,16,768]{3,2,1,0:T(8,128)(2,1)S(1)}, u32[]{:S(2)}, u32[]{:S(2)}) collective-permute-start(bf16[3,4,16,768]{3,2,1,0:T(8,128)(2,1)} %get-tuple-element.42), channel_id=1, source_target_pairs={{0,64},{64,128},{128,192},{192,0},{1,65},{65,129},{129,193},{193,1... | collective-permute-start | bytes 884744 | tf_op jit(solution)/shard_map/ppermute | solution.py:231
  137.1 17.2 %collective-permute-start.20 = (bf16[3,4,16,768]{3,2,1,0:T(8,128)(2,1)S(1)}, bf16[3,4,16,768]{3,2,1,0:T(8,128)(2,1)S(1)}, u32[]{:S(2)}, u32[]{:S(2)}) collective-permute-start(bf16[3,4,16,768]{3,2,1,0:T(8,128)(2,1)S(1)} %get-tuple-element.43), channel_id=1, source_target_pairs={{0,192},{64,0},{128,64},{192,128},{1,193},{65,1},{129,65},{193,129... | collective-permute-start | bytes 884744 | tf_op jit(solution)/shard_map/ppermute | solution.py:231
  155.6 24.5 %all-to-all-start.3 = ((f32[256,1,4]{2,1,0:T(1,128)}), f32[256,1,4]{2,1,0:T(1,128)S(1)}, u32[]{:S(2)}, u32[]{:S(2)}) async-start(f32[256,1,4]{2,1,0:T(1,128)} %broadcast_in_dim.9), calls=%async_computation.3 | async-start | bytes 262144 | tf_op jit(solution)/shard_map/all_to_all | solution.py:226
